TPU v7x, 32 devices: a whole 2x2x4 slice. The times are simulated.
32 devices in a mesh: year: 16 (over z, y, x), space: 2 (over core).
Axes of the slice: x: 2, y: 2, z: 4, core: 2. Of those that a mesh axis runs over, the one named last changes fastest.
Arguments:
- thermal_reading: float32 [2048, 8192], P('year', 'space'), may hold values from -24 to 24
- yearday_position: int32 [2048], P('year'), may hold values from 0 to 29, as said below
- usable_observation_tally: int32 [2048], P('year'), may hold values from 1 to 24
- location_surface_factor: float32 [8192], P('space'), may hold values from 0.2 to 5.4
Outputs:
- normalized_departure: float32 [2048, 8192], P('year', 'space')
- spread: float32 [2048], P('year')
Inputs may be any that keep to these rules, and one draw needn't show every extreme that they name: `yearday_position`: every day of 0 to 29 is the day of at least one step.
All inputs are finite; a program needn't handle non-finite values.
Results may differ from a plain program's by a relative error of at most 0.0003.
Values sent between devices are 32-bit elements; how exact they have to be, the bound alone decides.
No kernel may reach another device: no remote copies, remote signals or barrier semaphores. Data moves between devices by JAX's collectives and lax.ppermute only.
A program may use at most 64 MiB of HBM per device.

v0:
```python
import jax
import jax.numpy as jnp
from jax import lax
from jax.sharding import PartitionSpec as P

DAYS = 30


def on_device(thermal_reading, yearday_position, usable_observation_tally, location_surface_factor):
    days_row = jnp.arange(DAYS, dtype=jnp.int32)
    yearday_onehot = (yearday_position[None, :] == days_row[:, None]).astype(jnp.float32)
    observation_tally = usable_observation_tally.astype(jnp.float32)
    surface_scaled_product = jnp.dot(
        yearday_onehot * observation_tally[None, :],
        thermal_reading,
        precision=lax.Precision.HIGHEST,
    )
    hour_local = jnp.sum(yearday_onehot * observation_tally[None, :], axis=1)
    picked_elements = (yearday_position[None, :] == days_row[:, None])[:, :, None]
    yearday_ceiling = jnp.max(jnp.where(picked_elements, thermal_reading[None], -jnp.inf), axis=1)
    yearday_floor = jnp.min(jnp.where(picked_elements, thermal_reading[None], jnp.inf), axis=1)
    groups = lax.axis_size("year")
    stacked = jnp.stack([surface_scaled_product, yearday_ceiling, yearday_floor])
    received = lax.all_to_all(stacked, "year", split_axis=2, concat_axis=0, tiled=True)
    received = received.reshape(groups, 3, DAYS, received.shape[2])
    hour_total = lax.psum(hour_local, "year")
    share_sum = jnp.sum(received[:, 0], axis=0)
    share_high = jnp.max(received[:, 1], axis=0)
    share_low = jnp.min(received[:, 2], axis=0)
    shares = jnp.stack([share_sum / hour_total[:, None], 4.0 / (share_high - share_low + 1.0)])
    gathered = lax.all_gather(shares, "year", axis=2, tiled=True)
    day_mean = gathered[0]
    day_scale = gathered[1]
    interval_span = day_mean.shape[1]
    table = jnp.concatenate([day_mean, day_scale], axis=1)
    fetched_quantities = jnp.dot(yearday_onehot.T, table, precision=lax.Precision.HIGHEST)
    normalized_departure = (
        thermal_reading - fetched_quantities[:, :interval_span]
    ) * fetched_quantities[:, interval_span:]
    weighted_sq = jnp.sum(
        location_surface_factor[None, :] * normalized_departure * normalized_departure, axis=1
    )
    area_total = jnp.sum(location_surface_factor)
    weighted_sq, area_total = lax.psum((weighted_sq, area_total), "space")
    spread = weighted_sq / area_total
    return (normalized_departure, spread)


def solution(mesh):
    return jax.shard_map(
        on_device,
        mesh=mesh,
        in_specs=(P("year", "space"), P("year"), P("year"), P("space")),
        out_specs=(P("year", "space"), P("year")),
        check_vma=False,
    )
```

profile of v0, /device:TPU:0, one launch (start us, length us, event | category | flops | bytes accessed | tf_op | source)
XLA Modules:
  0.0 185.4 jit_solution(1223232323820137092)
XLA Ops:
  0.7 0.8 iota_compare_fusion
  1.5 0.7 convert_element_type.4
  2.1 14.5 %select_reduce_fusion.1 = (f32[30,4096]{1,0:T(8,128)S(1)}, f32[30,4096]{1,0:T(8,128)S(1)}) fusion(f32[128,4096]{1,0:T(8,128)} %param.4, pred[30,128]{1,0:T(8,128)(4,1)S(1)} %iota_compare_fusion), kind=kLoop, calls=%fused_computation.1 | loop fusion | flops 62668800 | bytes 3084032 | tf_op jit(solution)/shard_map/reduce_max | solution.py:20
  16.7 1.2 convolution_bitcast_fusion
  17.9 1.3 pad_maximum_fusion
  19.1 7.2 %copy.11 = f32[3,30,4096]{1,0,2:T(4,128)} copy(f32[3,30,4096]{2,1,0:T(8,128)} %pad_maximum_fusion) | data formatting | bytes 2949120 | tf_op jit(solution)/shard_map/stack | solution.py:23
  26.3 10.3 %reshape.73 = f32[16,1,23040]{2,1,0:T(1,128)} reshape(f32[4096,3,30]{2,1,0:T(4,128)} %bitcast.18) | data formatting | bytes 2949120
  36.6 8.5 %all-to-all-start = ((f32[16,1,23040]{2,1,0:T(1,128)}), f32[16,1,23040]{2,1,0:T(1,128)}, u32[]{:S(2)}, u32[]{:S(2)}) async-start(f32[16,1,23040]{2,1,0:T(1,128)} %reshape.73), calls=%async_computation | async-start | bytes 2949120 | tf_op jit(solution)/shard_map/all_to_all | solution.py:24
  45.2 0.6 reduce_sum.42
  45.7 0.1 select_reduce_fusion.2
  45.9 57.9 %psum.21 = f32[30]{0:T(128)S(1)} all-reduce(f32[30]{0:T(128)S(1)} %select_reduce_fusion.2), channel_id=1, replica_groups=mesh['year'=16,'space'=2] {'year'}, use_global_device_ids=true, to_apply=%region_4.5 | all-reduce | flops 30 | bytes 240 | tf_op jit(solution)/shard_map/psum | solution.py:26
  103.8 0.5 broadcast.56
  104.3 6.6 %reduce.3 = f32[16,23040]{1,0:T(8,128)} reduce(f32[16,1,23040]{2,1,0:T(1,128)} %all-to-all-done, f32[]{:T(128)} %broadcast.56), dimensions={1}, to_apply=%all_to_all.11.reduce_sub_computation | reduce | bytes 2949124 | tf_op jit(solution)/shard_map/all_to_all | solution.py:24
  110.9 9.3 %reshape.74 = f32[4096,3,30]{2,1,0:T(4,128)} reshape(f32[16,23040]{1,0:T(8,128)} %reduce.3) | data formatting | bytes 2949120
  120.2 11.5 %slice_reduce_fusion.2 = (f32[30,256]{0,1:T(8,128)S(1)}, f32[30,256]{0,1:T(8,128)S(1)}, f32[30,256]{0,1:T(8,128)S(1)}) fusion(f32[16,3,30,256]{2,1,3,0:T(4,128)} %bitcast.19), kind=kLoop, calls=%fused_computation.9 | loop fusion | flops 345600 | bytes 1566720 | tf_op jit(solution)/shard_map/reduce_sum | solution.py:27
  131.7 0.1 copy.13
  131.8 0.1 copy.12
  132.0 44.0 %all_gather.3 = f32[2,30,4096]{2,0,1:T(2,128)S(1)} all-gather(f32[2,30,256]{2,0,1:T(2,128)S(1)} %pad_maximum_fusion.1), channel_id=1, replica_groups=mesh['year'=16,'space'=2] {'year'}, dimensions={2}, use_global_device_ids=true | all-gather | bytes 1044480 | tf_op jit(solution)/shard_map/all_gather | solution.py:31
  176.0 1.1 fusion.12
  177.0 0.6 copy_bitcast_fusion
  177.6 1.8 fusion.1
  179.5 1.8 fusion
  181.3 3.1 %all-reduce = (f32[128]{0:T(128)S(1)}, f32[]{:T(128)}) all-reduce(f32[128]{0:T(128)S(1)} %get-tuple-element.9, f32[]{:T(128)} %reduce_sum.42), channel_id=1, replica_groups=mesh['year'=16,'space'=2] {'space'}, use_global_device_ids=true, to_apply=%region_8.9 | all-reduce | flops 129 | bytes 1032 | tf_op jit(solution)/shard_map/psum | solution.py:44
  184.3 1.1 broadcast_divide_fusion
  (10 shorter events, 0.1 us)
Async XLA Ops:
  0.6 16.0 %copy-start.2 = (s32[128]{0:T(128)S(1)}, s32[128]{0:T(128)}, u32[]{:S(2)}) copy-start(s32[128]{0:T(128)} %param.5) | copy-start | bytes 1540
  0.6 16.0 %copy-start = (f32[128,4096]{1,0:T(8,128)S(1)}, f32[128,4096]{1,0:T(8,128)}, u32[]{:S(2)}) copy-start(f32[128,4096]{1,0:T(8,128)} %param.4) | copy-start | bytes 6291460
  36.6 8.5 %copy-start.1 = (f32[4096]{0:T(1024)S(1)}, f32[4096]{0:T(1024)}, u32[]{:S(2)}) copy-start(f32[4096]{0:T(1024)} %param.7) | copy-start | bytes 49156
  36.6 67.1 %all-to-all-start = ((f32[16,1,23040]{2,1,0:T(1,128)}), f32[16,1,23040]{2,1,0:T(1,128)}, u32[]{:S(2)}, u32[]{:S(2)}) async-start(f32[16,1,23040]{2,1,0:T(1,128)} %reshape.73), calls=%async_computation | async-start | bytes 2949120 | tf_op jit(solution)/shard_map/all_to_all | solution.py:24
where the time goes:
time: 186 us; the launch traced here: 185 us
  blocking collectives  105 us (56%)
  other arithmetic  39.1 us (21%)
  local copies, waits for them, and re-layouts  29.1 us (16%)
  starting transfers between devices  8.52 us (5%)
  matrix products  3.02 us (2%)
    psum x1, blocking collectives, on_device(): hour_total = lax.psum(hour_local, 'year')  57.9 us
    all_gather x1, blocking collectives, on_device(): gathered = lax.all_gather(shares, 'year', axis=2, tiled=True)  44 us
    unnamed x9, local copies, waits for them, and re-layouts  20.2 us
    reduce_max x1, other arithmetic, on_device(): jnp.max(jnp.where(picked_elements, thermal_reading[None], -jnp.inf), axis=1)  14.5 us
    reduce_sum x1, other arithmetic, on_device(): share_sum = jnp.sum(received[:, 0], axis=0)  11.5 us
    all_to_all x1, starting transfers between devices, on_device(): lax.all_to_all(stacked, 'year', split_axis=2, concat_axis=0, tiled=True)  8.52 us
    another operation x1, local copies, waits for them, and re-layouts, on_device(): jnp.stack([surface_scaled_product, yearday_ceiling, yearday_floor])  7.19 us
    all_to_all x1, other arithmetic, on_device(): lax.all_to_all(stacked, 'year', split_axis=2, concat_axis=0, tiled=True)  6.63 us
  transfers between devices with their start and end apart: 1, of which 0 were waited for; matrix products, arithmetic and copies ran while one was open for 0% of the time, Pallas kernels for 0%

commit v1 on v0

v1 whole, which is shorter than its diff:
```python
import functools

import jax
import jax.numpy as jnp
from jax import lax
from jax.experimental import pallas as pl
from jax.experimental.pallas import tpu as pltpu
from jax.sharding import PartitionSpec as P

DAYS = 30
SUBLANES, LANES = 8, 128
GROUPS = 4
SLOTS = -(-DAYS // GROUPS)
CHUNKS = 2
HALVINGS = 3
HOURS, HIGH, LOW, TILES = SLOTS, SLOTS + 1, 2 * SLOTS + 1, 3 * SLOTS + 1
ORDERS = (((0, 1), (1, 0), (2, 2), (3, 3)), ((2, 2), (1, 0), (0, 1), (3, 3)))
AXES = ("year", "space")


def stage_bits(chunk, years):
    count = years.bit_length() - 1
    assert years == 1 << count and count > HALVINGS
    return [tuple(1 << b for b in pair) for pair in ORDERS[chunk]] + [(1 << b, 1 << b) for b in range(4, count)]


def own_bits(chunk):
    year, core = lax.axis_index("year"), lax.rem(lax.axis_index("space"), 2)
    pairs = stage_bits(chunk, lax.axis_size("year"))[:HALVINGS]
    return [jnp.where(core == 0, year // a % 2, year // b % 2) for a, b in pairs]


def place(day, bits):
    group, index = day // SLOTS, day % SLOTS
    second = 1 - (group // 2 + bits[1]) % 2
    third = 1 - (group % 2 + bits[2]) % 2
    return second, third, index


def stats_kernel(chunk, day_ref, tally_ref, x_ref, out_ref):
    bits = own_bits(chunk)
    tiles, rows = x_ref.shape[0], x_ref.shape[1] // 2
    height = rows // SUBLANES
    for half in range(2):
        for second in range(2):
            for third in range(2):
                block = out_ref.at[half, second, third]
                block[:HIGH] = jnp.zeros((HIGH, height, LANES), jnp.float32)
                block[HIGH:] = jnp.full((TILES - HIGH, height, LANES), -jnp.inf, jnp.float32)
    starts = [(1 - bits[0]) * rows, bits[0] * rows]

    def tile(t, carry):
        for k in range(SUBLANES):
            step = t * SUBLANES + k
            second, third, index = place(day_ref[step], bits)
            tally = tally_ref[step].astype(jnp.float32)
            for half in range(2):
                x = x_ref[t, pl.ds(starts[half] + k, height, stride=SUBLANES), :]
                out = out_ref.at[half, second, third]
                out[index] += tally * x
                out[HIGH + index] = jnp.maximum(out[HIGH + index], x)
                out[LOW + index] = jnp.maximum(out[LOW + index], -x)
                out[HOURS, pl.ds(index, 1), :] += jnp.full((1, LANES), tally, jnp.float32)
        return carry

    lax.fori_loop(0, tiles, tile, 0)


def stats(chunk, day, tally, x):
    tiles, rows = x.shape[0], x.shape[1] // CHUNKS
    shape = (2, 2, 2, TILES, rows // 2 // SUBLANES, LANES)
    return pl.pallas_call(
        functools.partial(stats_kernel, chunk),
        grid=(1,),
        in_specs=[
            pl.BlockSpec(memory_space=pltpu.SMEM),
            pl.BlockSpec(memory_space=pltpu.SMEM),
            pl.BlockSpec((tiles, rows, LANES), lambda i: (0, chunk, 0)),
        ],
        out_specs=pl.BlockSpec(shape, lambda i: (0,) * 6),
        out_shape=jax.ShapeDtypeStruct(shape, jnp.float32),
        name=f"stats_{chunk}",
    )(day, tally, x)


def depart_kernel(chunk, day_ref, x_ref, w_ref, recv_ref, own_ref, before_ref, *rest):
    out_ref, sums_ref, squares = rest[-3:]
    bits = own_bits(chunk)
    tiles, rows = x_ref.shape[0], x_ref.shape[1] // 2
    height = rows // SUBLANES
    starts = [(1 - bits[0]) * rows, bits[0] * rows]
    weights = [w_ref[pl.ds(pl.multiple_of((chunk * 2 + b) * height, height), height), :] for b in (1 - bits[0], bits[0])]

    def tile(t, carry):
        for k in range(SUBLANES):
            second, third, index = place(day_ref[t * SUBLANES + k], bits)
            total = None
            for half, table_ref in enumerate((recv_ref, own_ref)):
                place_x = pl.ds(starts[half] + k, height, stride=SUBLANES)
                table = table_ref.at[second, third]
                departure = (x_ref[t, place_x, :] - table[index]) * table[SLOTS + index]
                out_ref[t, place_x, :] = departure
                square = weights[half] * departure * departure
                total = square if total is None else total + square
            squares[pl.ds(pl.multiple_of((t * SUBLANES + k) * height, height), height), :] = total
        return carry

    lax.fori_loop(0, tiles, tile, 0)

    def fold(t, carry):
        start = t * SUBLANES * height
        total = squares[pl.ds(start, SUBLANES, stride=height), :]
        for j in range(1, height):
            total += squares[pl.ds(start + j, SUBLANES, stride=height), :]
        here = pl.ds(pl.multiple_of(t * SUBLANES, SUBLANES), SUBLANES)
        sums_ref[here, :] = total if before_ref is None else total + before_ref[here, :]
        return carry

    lax.fori_loop(0, tiles, fold, 0)


def depart(chunk, day, x, w, recv, own, before, out):
    tiles, rows = x.shape[0], x.shape[1] // CHUNKS
    height = rows // 2 // SUBLANES
    whole = lambda a: pl.BlockSpec(a.shape, lambda i, n=a.ndim: (0,) * n)
    column = pl.BlockSpec((tiles, rows, LANES), lambda i: (0, chunk, 0))
    steps = tiles * SUBLANES
    kernel = functools.partial(depart_kernel, chunk)
    inputs = [day, x, w, recv, own]
    in_specs = [pl.BlockSpec(memory_space=pltpu.SMEM), column, whole(w), whole(recv), whole(own)]
    aliases = {}
    if out is None:
        kernel = lambda *refs: depart_kernel(chunk, *refs[:5], None, *refs[5:])
    else:
        inputs += [before, out]
        in_specs += [whole(before), pl.BlockSpec(memory_space=pl.ANY)]
        aliases = {6: 0}
    return pl.pallas_call(
        kernel,
        grid=(1,),
        in_specs=in_specs,
        out_specs=(column, pl.BlockSpec((steps, LANES), lambda i: (0, 0))),
        out_shape=(jax.ShapeDtypeStruct(x.shape, jnp.float32), jax.ShapeDtypeStruct((steps, LANES), jnp.float32)),
        scratch_shapes=[pltpu.VMEM((steps * height, LANES), jnp.float32)],
        input_output_aliases=aliases,
        name=f"depart_{chunk}",
    )(*inputs)


def merge(a, b):
    adds = lax.broadcasted_iota(jnp.int32, (TILES, 1, 1), 0) < HIGH
    return jnp.where(adds, a + b, jnp.maximum(a, b))


def exchange(x, pair):
    years, spaces = lax.axis_size("year"), lax.axis_size("space")
    partners = [(y * spaces + s, (y ^ pair[s % 2]) * spaces + s) for y in range(years) for s in range(spaces)]
    return lax.ppermute(x, AXES, partners)


def day_tables(chunk, local):
    pairs = stage_bits(chunk, lax.axis_size("year"))
    send, keep = local[0], local[1]
    for stage, pair in enumerate(pairs):
        got = exchange(send if stage < HALVINGS else keep, pair)
        yield
        if stage < HALVINGS - 1:
            send, keep = merge(got[0], keep[0]), merge(got[1], keep[1])
        else:
            keep = merge(got, keep)
    mean = keep[:SLOTS] / keep[HOURS][:, None, :]
    scale = 4.0 / (keep[HIGH:LOW] + keep[LOW:] + 1.0)
    table = jnp.concatenate([mean, scale])
    for stage in reversed(range(HALVINGS)):
        got = exchange(table, pairs[stage])
        yield
        if stage > 0:
            table = jnp.stack([got, table])
    yield got, table


def on_device(thermal_reading, yearday_position, usable_observation_tally, location_surface_factor):
    steps, cells = thermal_reading.shape
    tiles, columns = steps // SUBLANES, cells // LANES
    x = thermal_reading.reshape(tiles, SUBLANES, columns, LANES).transpose(0, 2, 1, 3)
    x = x.reshape(tiles, columns * SUBLANES, LANES)
    w = location_surface_factor.reshape(columns, LANES)
    chunks = [day_tables(c, stats(c, yearday_position, usable_observation_tally, x)) for c in range(CHUNKS)]
    results = [None] * CHUNKS
    while not all(results):
        for c in range(CHUNKS):
            results[c] = next(chunks[c])
    out = sums = None
    for c in range(CHUNKS):
        out, sums = depart(c, yearday_position, x, w, *results[c], sums, out)
    weighted_sq, area_total = jnp.sum(sums, axis=1), jnp.sum(location_surface_factor)
    weighted_sq, area_total = lax.psum((weighted_sq, area_total), "space")
    out = out.reshape(tiles, columns, SUBLANES, LANES).transpose(0, 2, 1, 3).reshape(steps, cells)
    return out, weighted_sq / area_total


def solution(mesh):
    return jax.shard_map(
        on_device,
        mesh=mesh,
        in_specs=(P("year", "space"), P("year"), P("year"), P("space")),
        out_specs=(P("year", "space"), P("year")),
        check_vma=False,
    )
```

time: 186 us -> 81.8 us (0.44)
  blocking collectives: 105 us -> 3.17 us
  other arithmetic: 39.1 us -> 4.51 us
  waiting for transfers between devices: 0.01 us -> 27.5 us
  local copies, waits for them, and re-layouts: 29.1 us -> 3.53 us
  Pallas kernels: 0 us -> 20.5 us
  starting transfers between devices: 8.52 us -> 21.4 us
  matrix products: 3.02 us -> 0 us
    psum x1 -> x0, blocking collectives: 57.9 us -> none  [on_device(): hour_total = lax.psum(hour_local, 'year')]
    all_gather x1 -> x0, blocking collectives: 44 us -> none  [on_device(): gathered = lax.all_gather(shares, 'year', axis=2, tiled=True)]
    ppermute x0 -> x14, waiting for transfers between devices: none -> 27.5 us  [exchange(): return lax.ppermute(x, AXES, partners)]
    ppermute x0 -> x14, starting transfers between devices: none -> 21.4 us  [exchange(): return lax.ppermute(x, AXES, partners)]
    pallas_call x0 -> x4, Pallas kernels: none -> 20.5 us  [the longest x2 10.3 us: depart(): pl.pallas_call(kernel, grid=(1,), in_specs=in_specs, out_specs=(column, p...]
    unnamed x9 -> x12, local copies, waits for them, and re-layouts: 20.2 us -> 1.39 us
    reduce_max x1 -> x0, other arithmetic: 14.5 us -> none  [on_device(): jnp.max(jnp.where(picked_elements, thermal_reading[None], -jnp.inf), axis=1)]
    reduce_sum x4 -> x2, other arithmetic: 14 us -> 1.54 us  [the longest x1 0.94 us: on_device(): jnp.sum(sums, axis=1)]
  transfers between devices with their start and end apart: 1 -> 14, of which waited for: 0 -> 12; matrix products, arithmetic and copies ran while one was open for 0% -> 2% of each run, Pallas kernels for 0% -> 13%
where the time goes in v1:
time: 81.8 us; the launch traced here: 81.4 us
  waiting for transfers between devices  27.5 us (34%)
  starting transfers between devices  21.4 us (26%)
  Pallas kernels  20.5 us (25%)
  other arithmetic  4.51 us (6%)
  local copies, waits for them, and re-layouts  3.53 us (4%)
  blocking collectives  3.17 us (4%)
    ppermute x14, waiting for transfers between devices, exchange(): return lax.ppermute(x, AXES, partners)  27.5 us
    ppermute x14, starting transfers between devices, exchange(): return lax.ppermute(x, AXES, partners)  21.4 us
    pallas_call x2, Pallas kernels, depart(): pl.pallas_call(kernel, grid=(1,), in_specs=in_specs, out_specs=(column, p...  10.3 us
    pallas_call x2, Pallas kernels, stats(): pl.pallas_call(functools.partial(stats_kernel, chunk), grid=(1,), in_spec...  10.2 us
    psum x1, blocking collectives, on_device(): weighted_sq, area_total = lax.psum((weighted_sq, area_total), 'space')  3.17 us
    squeeze x2, local copies, waits for them, and re-layouts, day_tables(): send, keep = (local[0], local[1])  2.13 us
    select_n x5, other arithmetic, merge(): return jnp.where(adds, a + b, jnp.maximum(a, b))  1.68 us
  transfers between devices with their start and end apart: 14, of which 12 were waited for; matrix products, arithmetic and copies ran while one was open for 2% of the time, Pallas kernels for 13%

profile of v1, /device:TPU:0, one launch (start us, length us, event | category | flops | bytes accessed | tf_op | source)
XLA Modules:
  0.0 81.4 jit_solution(657324032178530431)
XLA Ops:
  0.6 5.1 %stats_1.1 = f32[2,2,2,25,8,128]{5,4,3,2,1,0:T(8,128)} custom-call(s32[128]{0:T(128)} %day_ref.5, s32[128]{0:T(128)} %tally_ref.3, f32[16,256,128]{2,1,0:T(8,128)} %bitcast.87), custom_call_target="tpu_custom_call" | custom-call | tf_op jit(solution)/shard_map/stats_1/pallas_call | solution.py:72
  6.8 3.1 %collective-permute-start = (f32[2,2,25,8,128]{4,3,2,1,0:T(8,128)S(1)}, f32[2,2,25,8,128]{4,3,2,1,0:T(8,128)S(1)}, u32[]{:S(2)}, u32[]{:S(2)}) collective-permute-start(f32[2,2,25,8,128]{4,3,2,1,0:T(8,128)S(1)} %slice_bitcast_fusion.1), channel_id=1, source_target_pairs={{0,8},{1,9},{2,10},{3,11},{4,12},{5,13},{6,14},{7,15},{8,0},{9,1},... | collective-permute-start | bytes 1228808 | tf_op jit(solution)/shard_map/ppermute | solution.py:158
  9.9 5.1 %stats_0.1 = f32[2,2,2,25,8,128]{5,4,3,2,1,0:T(8,128)} custom-call(s32[128]{0:T(128)} %day_ref.5, s32[128]{0:T(128)} %tally_ref.3, f32[16,256,128]{2,1,0:T(8,128)} %bitcast.88), custom_call_target="tpu_custom_call" | custom-call | tf_op jit(solution)/shard_map/stats_0/pallas_call | solution.py:72
  16.1 1.6 %collective-permute-start.7 = (f32[2,2,25,8,128]{4,3,2,1,0:T(8,128)S(1)}, f32[2,2,25,8,128]{4,3,2,1,0:T(8,128)S(1)}, u32[]{:S(2)}, u32[]{:S(2)}) collective-permute-start(f32[2,2,25,8,128]{4,3,2,1,0:T(8,128)S(1)} %slice_bitcast_fusion), channel_id=1, source_target_pairs={{0,2},{1,5},{2,0},{3,7},{4,6},{5,1},{6,4},{7,3},{8,10},{9,13},{10,... | collective-permute-start | bytes 1228808 | tf_op jit(solution)/shard_map/ppermute | solution.py:158
  17.6 1.8 %collective-permute-done = f32[2,2,25,8,128]{4,3,2,1,0:T(8,128)S(1)} collective-permute-done((f32[2,2,25,8,128]{4,3,2,1,0:T(8,128)S(1)}, f32[2,2,25,8,128]{4,3,2,1,0:T(8,128)S(1)}, u32[]{:S(2)}, u32[]{:S(2)}) %collective-permute-start) | collective-permute-done | bytes 409632 | tf_op jit(solution)/shard_map/ppermute | solution.py:158
  19.4 4.7 %collective-permute-done.7 = f32[2,2,25,8,128]{4,3,2,1,0:T(8,128)S(1)} collective-permute-done((f32[2,2,25,8,128]{4,3,2,1,0:T(8,128)S(1)}, f32[2,2,25,8,128]{4,3,2,1,0:T(8,128)S(1)}, u32[]{:S(2)}, u32[]{:S(2)}) %collective-permute-start.7) | collective-permute-done | bytes 409632 | tf_op jit(solution)/shard_map/ppermute | solution.py:158
  25.4 1.6 %collective-permute-start.8 = (f32[2,25,8,128]{3,2,1,0:T(8,128)S(1)}, f32[2,25,8,128]{3,2,1,0:T(8,128)S(1)}, u32[]{:S(2)}, u32[]{:S(2)}) collective-permute-start(f32[2,25,8,128]{3,2,1,0:T(8,128)S(1)} %get-tuple-element.12), channel_id=1, source_target_pairs={{0,4},{1,3},{2,6},{3,1},{4,0},{5,7},{6,2},{7,5},{8,12},{9,11},{10,... | collective-permute-start | bytes 614408 | tf_op jit(solution)/shard_map/ppermute | solution.py:158
  27.4 3.7 %collective-permute-done.8 = f32[2,25,8,128]{3,2,1,0:T(8,128)S(1)} collective-permute-done((f32[2,25,8,128]{3,2,1,0:T(8,128)S(1)}, f32[2,25,8,128]{3,2,1,0:T(8,128)S(1)}, u32[]{:S(2)}, u32[]{:S(2)}) %collective-permute-start.8) | collective-permute-done | bytes 204832 | tf_op jit(solution)/shard_map/ppermute | solution.py:158
  31.4 2.0 %collective-permute-done.1 = f32[2,25,8,128]{3,2,1,0:T(8,128)S(1)} collective-permute-done((f32[2,25,8,128]{3,2,1,0:T(8,128)S(1)}, f32[2,25,8,128]{3,2,1,0:T(8,128)S(1)}, u32[]{:S(2)}, u32[]{:S(2)}) %collective-permute-start.1) | collective-permute-done | bytes 204832 | tf_op jit(solution)/shard_map/ppermute | solution.py:158
  33.4 2.6 %collective-permute-done.9 = f32[25,8,128]{2,1,0:T(8,128)S(1)} collective-permute-done((f32[25,8,128]{2,1,0:T(8,128)S(1)}, f32[25,8,128]{2,1,0:T(8,128)S(1)}, u32[]{:S(2)}, u32[]{:S(2)}) %collective-permute-start.9) | collective-permute-done | bytes 102432 | tf_op jit(solution)/shard_map/ppermute | solution.py:158
  36.1 3.2 %collective-permute-start.10 = (f32[25,8,128]{2,1,0:T(8,128)S(1)}, f32[25,8,128]{2,1,0:T(8,128)S(1)}, u32[]{:S(2)}, u32[]{:S(2)}) collective-permute-start(f32[25,8,128]{2,1,0:T(8,128)S(1)} %get-tuple-element.30), channel_id=1, source_target_pairs={{0,16},{1,17},{2,18},{3,19},{4,20},{5,21},{6,22},{7,23},{8,24},{9,... | collective-permute-start | bytes 307208 | tf_op jit(solution)/shard_map/ppermute | solution.py:158
  39.3 1.3 %collective-permute-start.2 = (f32[25,8,128]{2,1,0:T(8,128)S(1)}, f32[25,8,128]{2,1,0:T(8,128)S(1)}, u32[]{:S(2)}, u32[]{:S(2)}) collective-permute-start(f32[25,8,128]{2,1,0:T(8,128)S(1)} %get-tuple-element.31), channel_id=1, source_target_pairs={{0,2},{1,5},{2,0},{3,7},{4,6},{5,1},{6,4},{7,3},{8,10},{9,13},{10,... | collective-permute-start | bytes 307208 | tf_op jit(solution)/shard_map/ppermute | solution.py:158
  40.7 2.8 %collective-permute-done.10 = f32[25,8,128]{2,1,0:T(8,128)S(1)} collective-permute-done((f32[25,8,128]{2,1,0:T(8,128)S(1)}, f32[25,8,128]{2,1,0:T(8,128)S(1)}, u32[]{:S(2)}, u32[]{:S(2)}) %collective-permute-start.10) | collective-permute-done | bytes 102432 | tf_op jit(solution)/shard_map/ppermute | solution.py:158
  44.1 2.1 %collective-permute-start.3 = (f32[25,8,128]{2,1,0:T(8,128)S(1)}, f32[25,8,128]{2,1,0:T(8,128)S(1)}, u32[]{:S(2)}, u32[]{:S(2)}) collective-permute-start(f32[25,8,128]{2,1,0:T(8,128)S(1)} %get-tuple-element.29), channel_id=1, source_target_pairs={{0,16},{1,17},{2,18},{3,19},{4,20},{5,21},{6,22},{7,23},{8,24},{9,... | collective-permute-start | bytes 307208 | tf_op jit(solution)/shard_map/ppermute | solution.py:158
  46.3 1.7 %collective-permute-start.11 = (f32[16,8,128]{2,1,0:T(8,128)S(1)}, f32[16,8,128]{2,1,0:T(8,128)S(1)}, u32[]{:S(2)}, u32[]{:S(2)}) collective-permute-start(f32[16,8,128]{2,1,0:T(8,128)S(1)} %get-tuple-element.24), channel_id=1, source_target_pairs={{0,8},{1,9},{2,10},{3,11},{4,12},{5,13},{6,14},{7,15},{8,0},{9,1},... | collective-permute-start | bytes 196616 | tf_op jit(solution)/shard_map/ppermute | solution.py:158
  48.0 3.0 %collective-permute-done.3 = f32[25,8,128]{2,1,0:T(8,128)S(1)} collective-permute-done((f32[25,8,128]{2,1,0:T(8,128)S(1)}, f32[25,8,128]{2,1,0:T(8,128)S(1)}, u32[]{:S(2)}, u32[]{:S(2)}) %collective-permute-start.3) | collective-permute-done | bytes 102432 | tf_op jit(solution)/shard_map/ppermute | solution.py:158
  51.1 1.7 %collective-permute-start.4 = (f32[16,8,128]{2,1,0:T(8,128)S(1)}, f32[16,8,128]{2,1,0:T(8,128)S(1)}, u32[]{:S(2)}, u32[]{:S(2)}) collective-permute-start(f32[16,8,128]{2,1,0:T(8,128)S(1)} %get-tuple-element.26), channel_id=1, source_target_pairs={{0,2},{1,5},{2,0},{3,7},{4,6},{5,1},{6,4},{7,3},{8,10},{9,13},{10,... | collective-permute-start | bytes 196616 | tf_op jit(solution)/shard_map/ppermute | solution.py:158
  52.9 1.6 %collective-permute-start.12 = (f32[2,16,8,128]{3,2,1,0:T(8,128)S(1)}, f32[2,16,8,128]{3,2,1,0:T(8,128)S(1)}, u32[]{:S(2)}, u32[]{:S(2)}) collective-permute-start(f32[2,16,8,128]{3,2,1,0:T(8,128)S(1)} %get-tuple-element.16), channel_id=1, source_target_pairs={{0,4},{1,3},{2,6},{3,1},{4,0},{5,7},{6,2},{7,5},{8,12},{9,11},{10,... | collective-permute-start | bytes 393224 | tf_op jit(solution)/shard_map/ppermute | solution.py:158
  55.5 1.7 %collective-permute-start.5 = (f32[2,16,8,128]{3,2,1,0:T(8,128)S(1)}, f32[2,16,8,128]{3,2,1,0:T(8,128)S(1)}, u32[]{:S(2)}, u32[]{:S(2)}) collective-permute-start(f32[2,16,8,128]{3,2,1,0:T(8,128)S(1)} %get-tuple-element.18), channel_id=1, source_target_pairs={{0,4},{1,3},{2,6},{3,1},{4,0},{5,7},{6,2},{7,5},{8,12},{9,11},{10,... | collective-permute-start | bytes 393224 | tf_op jit(solution)/shard_map/ppermute | solution.py:158
  58.9 1.6 %collective-permute-done.5 = f32[2,16,8,128]{3,2,1,0:T(8,128)S(1)} collective-permute-done((f32[2,16,8,128]{3,2,1,0:T(8,128)S(1)}, f32[2,16,8,128]{3,2,1,0:T(8,128)S(1)}, u32[]{:S(2)}, u32[]{:S(2)}) %collective-permute-start.5) | collective-permute-done | bytes 131104 | tf_op jit(solution)/shard_map/ppermute | solution.py:158
  61.3 3.1 %collective-permute-done.13.refs_3_ = f32[2,2,16,8,128]{4,3,2,1,0:T(8,128)S(1)} collective-permute-done((f32[2,2,16,8,128]{4,3,2,1,0:T(8,128)S(1)}, f32[2,2,16,8,128]{4,3,2,1,0:T(8,128)S(1)}, u32[]{:S(2)}, u32[]{:S(2)}) %collective-permute-start.13) | collective-permute-done | bytes 262176 | tf_op jit(solution)/shard_map/ppermute | solution.py:158
  65.1 5.2 %depart_0.1 = (f32[16,256,128]{2,1,0:T(8,128)}, f32[128,128]{1,0:T(8,128)}) custom-call(s32[128]{0:T(128)} %day_ref.5, f32[16,256,128]{2,1,0:T(8,128)} %bitcast.89, f32[32,128]{1,0:T(8,128)} %bitcast.92, f32[2,2,16,8,128]{4,3,2,1,0:T(8,128)} %copy-done.3, f32[2,2,16,8,128]{4,3,2,1,0:T(8,128)} %copy-done.1), custom_call_target="tpu_custom_call" | custom-call | tf_op jit(solution)/shard_map/depart_0/pallas_call | solution.py:138
  71.0 5.2 %depart_1.1 = (f32[16,256,128]{2,1,0:T(8,128)}, f32[128,128]{1,0:T(8,128)}) custom-call(s32[128]{0:T(128)} %day_ref.5, f32[16,256,128]{2,1,0:T(8,128)} %bitcast.90, f32[32,128]{1,0:T(8,128)} %bitcast.93, f32[2,2,16,8,128]{4,3,2,1,0:T(8,128)} %copy-done.4, f32[2,2,16,8,128]{4,3,2,1,0:T(8,128)} %copy-done.2, ...), custom_call_target="tpu_custom_call", output_to_operand_aliasing={{0}: (6, {})} | custom-call | tf_op jit(solution)/shard_map/depart_1/pallas_call | solution.py:138
  77.1 3.2 %all-reduce = (f32[128]{0:T(128)S(1)}, f32[]{:T(128)}) all-reduce(f32[128]{0:T(128)S(1)} %reduce_sum.18, f32[]{:T(128)} %reduce_sum.19), channel_id=1, replica_groups=mesh['year'=16,'space'=2] {'space'}, use_global_device_ids=true, to_apply=%region_1.2 | all-reduce | flops 129 | bytes 1032 | tf_op jit(solution)/shard_map/psum | solution.py:197
  (42 shorter events, 11.9 us)
Async XLA Ops:
  5.7 18.4 %copy-start = (f32[2,2,2,25,8,128]{5,4,3,2,1,0:T(8,128)S(1)}, f32[2,2,2,25,8,128]{5,4,3,2,1,0:T(8,128)}, u32[]{:S(2)}) copy-start(f32[2,2,2,25,8,128]{5,4,3,2,1,0:T(8,128)} %stats_1.1) | copy-start | bytes 2457604
  6.8 12.6 %collective-permute-start = (f32[2,2,25,8,128]{4,3,2,1,0:T(8,128)S(1)}, f32[2,2,25,8,128]{4,3,2,1,0:T(8,128)S(1)}, u32[]{:S(2)}, u32[]{:S(2)}) collective-permute-start(f32[2,2,25,8,128]{4,3,2,1,0:T(8,128)S(1)} %slice_bitcast_fusion.1), channel_id=1, source_target_pairs={{0,8},{1,9},{2,10},{3,11},{4,12},{5,13},{6,14},{7,15},{8,0},{9,1},... | collective-permute-start | bytes 1228808 | tf_op jit(solution)/shard_map/ppermute | solution.py:158
  16.1 8.0 %collective-permute-start.7 = (f32[2,2,25,8,128]{4,3,2,1,0:T(8,128)S(1)}, f32[2,2,25,8,128]{4,3,2,1,0:T(8,128)S(1)}, u32[]{:S(2)}, u32[]{:S(2)}) collective-permute-start(f32[2,2,25,8,128]{4,3,2,1,0:T(8,128)S(1)} %slice_bitcast_fusion), channel_id=1, source_target_pairs={{0,2},{1,5},{2,0},{3,7},{4,6},{5,1},{6,4},{7,3},{8,10},{9,13},{10,... | collective-permute-start | bytes 1228808 | tf_op jit(solution)/shard_map/ppermute | solution.py:158
  25.4 5.8 %collective-permute-start.8 = (f32[2,25,8,128]{3,2,1,0:T(8,128)S(1)}, f32[2,25,8,128]{3,2,1,0:T(8,128)S(1)}, u32[]{:S(2)}, u32[]{:S(2)}) collective-permute-start(f32[2,25,8,128]{3,2,1,0:T(8,128)S(1)} %get-tuple-element.12), channel_id=1, source_target_pairs={{0,4},{1,3},{2,6},{3,1},{4,0},{5,7},{6,2},{7,5},{8,12},{9,11},{10,... | collective-permute-start | bytes 614408 | tf_op jit(solution)/shard_map/ppermute | solution.py:158
  26.9 6.4 %collective-permute-start.1 = (f32[2,25,8,128]{3,2,1,0:T(8,128)S(1)}, f32[2,25,8,128]{3,2,1,0:T(8,128)S(1)}, u32[]{:S(2)}, u32[]{:S(2)}) collective-permute-start(f32[2,25,8,128]{3,2,1,0:T(8,128)S(1)} %get-tuple-element.33), channel_id=1, source_target_pairs={{0,4},{1,3},{2,6},{3,1},{4,0},{5,7},{6,2},{7,5},{8,12},{9,11},{10,... | collective-permute-start | bytes 614408 | tf_op jit(solution)/shard_map/ppermute | solution.py:158
  31.3 4.7 %collective-permute-start.9 = (f32[25,8,128]{2,1,0:T(8,128)S(1)}, f32[25,8,128]{2,1,0:T(8,128)S(1)}, u32[]{:S(2)}, u32[]{:S(2)}) collective-permute-start(f32[25,8,128]{2,1,0:T(8,128)S(1)} %bitcast_select_fusion.1), channel_id=1, source_target_pairs={{0,8},{1,9},{2,10},{3,11},{4,12},{5,13},{6,14},{7,15},{8,0},{9,1},... | collective-permute-start | bytes 307208 | tf_op jit(solution)/shard_map/ppermute | solution.py:158
  36.0 24.6 %copy-start.5 = (f32[4096]{0:T(1024)S(1)}, f32[4096]{0:T(1024)}, u32[]{:S(2)}) copy-start(f32[4096]{0:T(1024)} %param.7) | copy-start | bytes 49156
  36.1 7.4 %collective-permute-start.10 = (f32[25,8,128]{2,1,0:T(8,128)S(1)}, f32[25,8,128]{2,1,0:T(8,128)S(1)}, u32[]{:S(2)}, u32[]{:S(2)}) collective-permute-start(f32[25,8,128]{2,1,0:T(8,128)S(1)} %get-tuple-element.30), channel_id=1, source_target_pairs={{0,16},{1,17},{2,18},{3,19},{4,20},{5,21},{6,22},{7,23},{8,24},{9,... | collective-permute-start | bytes 307208 | tf_op jit(solution)/shard_map/ppermute | solution.py:158
  39.3 4.7 %collective-permute-start.2 = (f32[25,8,128]{2,1,0:T(8,128)S(1)}, f32[25,8,128]{2,1,0:T(8,128)S(1)}, u32[]{:S(2)}, u32[]{:S(2)}) collective-permute-start(f32[25,8,128]{2,1,0:T(8,128)S(1)} %get-tuple-element.31), channel_id=1, source_target_pairs={{0,2},{1,5},{2,0},{3,7},{4,6},{5,1},{6,4},{7,3},{8,10},{9,13},{10,... | collective-permute-start | bytes 307208 | tf_op jit(solution)/shard_map/ppermute | solution.py:158
  44.1 6.8 %collective-permute-start.3 = (f32[25,8,128]{2,1,0:T(8,128)S(1)}, f32[25,8,128]{2,1,0:T(8,128)S(1)}, u32[]{:S(2)}, u32[]{:S(2)}) collective-permute-start(f32[25,8,128]{2,1,0:T(8,128)S(1)} %get-tuple-element.29), channel_id=1, source_target_pairs={{0,16},{1,17},{2,18},{3,19},{4,20},{5,21},{6,22},{7,23},{8,24},{9,... | collective-permute-start | bytes 307208 | tf_op jit(solution)/shard_map/ppermute | solution.py:158
  46.3 6.6 %collective-permute-start.11 = (f32[16,8,128]{2,1,0:T(8,128)S(1)}, f32[16,8,128]{2,1,0:T(8,128)S(1)}, u32[]{:S(2)}, u32[]{:S(2)}) collective-permute-start(f32[16,8,128]{2,1,0:T(8,128)S(1)} %get-tuple-element.24), channel_id=1, source_target_pairs={{0,8},{1,9},{2,10},{3,11},{4,12},{5,13},{6,14},{7,15},{8,0},{9,1},... | collective-permute-start | bytes 196616 | tf_op jit(solution)/shard_map/ppermute | solution.py:158
  51.1 4.3 %collective-permute-start.4 = (f32[16,8,128]{2,1,0:T(8,128)S(1)}, f32[16,8,128]{2,1,0:T(8,128)S(1)}, u32[]{:S(2)}, u32[]{:S(2)}) collective-permute-start(f32[16,8,128]{2,1,0:T(8,128)S(1)} %get-tuple-element.26), channel_id=1, source_target_pairs={{0,2},{1,5},{2,0},{3,7},{4,6},{5,1},{6,4},{7,3},{8,10},{9,13},{10,... | collective-permute-start | bytes 196616 | tf_op jit(solution)/shard_map/ppermute | solution.py:158
  52.9 5.0 %collective-permute-start.12 = (f32[2,16,8,128]{3,2,1,0:T(8,128)S(1)}, f32[2,16,8,128]{3,2,1,0:T(8,128)S(1)}, u32[]{:S(2)}, u32[]{:S(2)}) collective-permute-start(f32[2,16,8,128]{3,2,1,0:T(8,128)S(1)} %get-tuple-element.16), channel_id=1, source_target_pairs={{0,4},{1,3},{2,6},{3,1},{4,0},{5,7},{6,2},{7,5},{8,12},{9,11},{10,... | collective-permute-start | bytes 393224 | tf_op jit(solution)/shard_map/ppermute | solution.py:158
  55.5 5.0 %collective-permute-start.5 = (f32[2,16,8,128]{3,2,1,0:T(8,128)S(1)}, f32[2,16,8,128]{3,2,1,0:T(8,128)S(1)}, u32[]{:S(2)}, u32[]{:S(2)}) collective-permute-start(f32[2,16,8,128]{3,2,1,0:T(8,128)S(1)} %get-tuple-element.18), channel_id=1, source_target_pairs={{0,4},{1,3},{2,6},{3,1},{4,0},{5,7},{6,2},{7,5},{8,12},{9,11},{10,... | collective-permute-start | bytes 393224 | tf_op jit(solution)/shard_map/ppermute | solution.py:158
  57.9 6.4 %copy-start.1 = (f32[2,2,16,8,128]{4,3,2,1,0:T(8,128)}, f32[2,2,16,8,128]{4,3,2,1,0:T(8,128)S(1)}, u32[]{:S(2)}) copy-start(f32[2,2,16,8,128]{4,3,2,1,0:T(8,128)S(1)} %pad_maximum_fusion.1.refs_4_) | copy-start | bytes 786436
  58.0 6.4 %collective-permute-start.13 = (f32[2,2,16,8,128]{4,3,2,1,0:T(8,128)S(1)}, f32[2,2,16,8,128]{4,3,2,1,0:T(8,128)S(1)}, u32[]{:S(2)}, u32[]{:S(2)}) collective-permute-start(f32[2,2,16,8,128]{4,3,2,1,0:T(8,128)S(1)} %pad_maximum_fusion.1.refs_4_), channel_id=1, source_target_pairs={{0,2},{1,5},{2,0},{3,7},{4,6},{5,1},{6,4},{7,3},{8,10},{9,13},{10,... | collective-permute-start | bytes 786440 | tf_op jit(solution)/shard_map/ppermute | solution.py:158
  60.6 9.7 %copy-start.2 = (f32[2,2,16,8,128]{4,3,2,1,0:T(8,128)}, f32[2,2,16,8,128]{4,3,2,1,0:T(8,128)S(1)}, u32[]{:S(2)}) copy-start(f32[2,2,16,8,128]{4,3,2,1,0:T(8,128)S(1)} %pad_maximum_fusion.own_ref) | copy-start | bytes 786436
  60.6 9.7 %collective-permute-start.6 = (f32[2,2,16,8,128]{4,3,2,1,0:T(8,128)S(1)}, f32[2,2,16,8,128]{4,3,2,1,0:T(8,128)S(1)}, u32[]{:S(2)}, u32[]{:S(2)}) collective-permute-start(f32[2,2,16,8,128]{4,3,2,1,0:T(8,128)S(1)} %pad_maximum_fusion.own_ref), channel_id=1, source_target_pairs={{0,8},{1,9},{2,10},{3,11},{4,12},{5,13},{6,14},{7,15},{8,0},{9,1},... | collective-permute-start | bytes 786440 | tf_op jit(solution)/shard_map/ppermute | solution.py:158
  64.4 0.7 copy-start.3
  70.3 0.7 copy-start.4

commit v2 on v1

v2 whole, which is shorter than its diff:
```python
import functools

import jax
import jax.numpy as jnp
from jax import lax
from jax.experimental import pallas as pl
from jax.experimental.pallas import tpu as pltpu
from jax.sharding import PartitionSpec as P

DAYS = 30
SUBLANES, LANES = 8, 128
GROUPS = 4
SLOTS = -(-DAYS // GROUPS)
CHUNKS = 2
HALVINGS = 3
HOURS, HIGH, LOW, TILES = SLOTS, SLOTS + 1, 2 * SLOTS + 1, 3 * SLOTS + 1
ORDERS = (((0, 1), (1, 0), (2, 2), (3, 3)), ((2, 2), (1, 0), (0, 1), (3, 3)))
AXES = ("year", "space")
PIECES = 4

VMEM = pl.BlockSpec(memory_space=pltpu.VMEM)
SMEM = pl.BlockSpec(memory_space=pltpu.SMEM)
HBM = pl.BlockSpec(memory_space=pltpu.HBM)


def local_call(kernel, name, out_shape, *inputs, **options):
    specs = options.pop("in_specs", [VMEM] * len(inputs))
    spaces = {id(VMEM): pltpu.VMEM, id(HBM): pltpu.HBM}
    inputs = [pltpu.with_memory_space_constraint(a, spaces[id(s)]) if id(s) in spaces else a for a, s in zip(inputs, specs)]
    limit = pltpu.CompilerParams(vmem_limit_bytes=options.pop("vmem", 1 << 20))
    return pl.pallas_call(kernel, in_specs=specs, out_shape=out_shape, name=name, compiler_params=limit, **options)(*inputs)


def vmem(*shape):
    return pltpu.VMEM(shape, jnp.float32)


def stage_bits(chunk, years):
    count = years.bit_length() - 1
    assert years == 1 << count and count > HALVINGS
    return [tuple(1 << b for b in pair) for pair in ORDERS[chunk]] + [(1 << b, 1 << b) for b in range(4, count)]


def own_bits(chunk):
    year, core = lax.axis_index("year"), lax.rem(lax.axis_index("space"), 2)
    pairs = stage_bits(chunk, lax.axis_size("year"))[:HALVINGS]
    return [jnp.where(core == 0, year // a % 2, year // b % 2) for a, b in pairs]


def day_flip(bits):
    return ((1 - bits[1]) * 2 + 1 - bits[2]) * SLOTS


def place(day, flip):
    day = lax.bitwise_xor(day, flip)
    return lax.shift_right_logical(day, SLOTS.bit_length() - 1), lax.bitwise_and(day, SLOTS - 1)


def stats_kernel(chunk, *refs):
    if chunk == 0:
        day_in, tally_in, x_in, send_ref, keep_ref, x_ref, day_ref, tally_ref, hours, arrived, listed = refs
        tiles, rows = x_in.shape[0], x_in.shape[1] // CHUNKS
        piece = tiles // PIECES
        lists = [pltpu.make_async_copy(day_in, day_ref, listed.at[0]), pltpu.make_async_copy(tally_in, tally_ref, listed.at[1])]
        copies = []
        for c in range(CHUNKS):
            for p in range(PIECES):
                at = pl.ds(p * piece, piece), pl.ds(c * rows, rows)
                copies.append(pltpu.make_async_copy(x_in.at[at], x_ref.at[at], arrived.at[c, p]))
        for copy in lists + copies:
            copy.start()
    else:
        day_ref, tally_ref, x_ref, send_ref, keep_ref, hours = refs
        tiles, rows = x_ref.shape[0], x_ref.shape[1] // CHUNKS
        piece, lists, copies = tiles // PIECES, [], []
    bits = own_bits(chunk)
    flip = day_flip(bits)
    half = rows // 2
    height = half // SUBLANES
    outs = [ref.reshape(GROUPS, *ref.shape[2:]) for ref in (send_ref, keep_ref)]
    starts = [chunk * rows + (1 - bits[0]) * half, chunk * rows + bits[0] * half]
    for out in outs:
        for slot in range(GROUPS):
            block = out.at[slot]
            block[:HIGH] = jnp.zeros((HIGH, height, LANES), jnp.float32)
            block[HIGH:LOW] = jnp.full((SLOTS, height, LANES), -jnp.inf, jnp.float32)
            block[LOW:] = jnp.full((SLOTS, height, LANES), jnp.inf, jnp.float32)
    for d in range(GROUPS * SLOTS):
        hours[d] = 0
    for copy in lists:
        copy.wait()

    def tile(t, carry):
        for k in range(SUBLANES):
            step = t * SUBLANES + k
            day, tally = day_ref[step], tally_ref[step]
            slot, index = place(day, flip)
            hours[day] += tally
            tally = tally.astype(jnp.float32)
            blocks = [out.at[slot] for out in outs]
            x = [x_ref[t, pl.ds(start + k, height, stride=SUBLANES), :] for start in starts]
            old = [[b[index], b[HIGH + index], b[LOW + index]] for b in blocks]
            new = [[o[0] + tally * v, jnp.maximum(o[1], v), jnp.minimum(o[2], v)] for o, v in zip(old, x)]
            for b, n in zip(blocks, new):
                b[index], b[HIGH + index], b[LOW + index] = n
        return carry

    for p in range(PIECES):
        if copies:
            copies[p].wait()
        lax.fori_loop(p * piece, (p + 1) * piece, tile, 0)
    for d in range(DAYS):
        slot, index = place(jnp.int32(d), flip)
        row = jnp.full((1, LANES), hours[d].astype(jnp.float32), jnp.float32)
        for out in outs:
            out[slot, HOURS, pl.ds(index, 1), :] = row
    for copy in copies[PIECES:]:
        copy.wait()


def stats(chunk, day, tally, x):
    tiles, rows = x.shape[0], x.shape[1] // CHUNKS
    half = vmem(2, GROUPS // 2, TILES, rows // 2 // SUBLANES, LANES)
    shapes, scratch = (half, half), [pltpu.SMEM((GROUPS * SLOTS,), jnp.int32)]
    if chunk == 0:
        shapes += (vmem(*x.shape),)
        lists = [pltpu.SMEM(day.shape, jnp.int32)] * 2
        scratch = lists + scratch + [pltpu.SemaphoreType.DMA((CHUNKS, PIECES)), pltpu.SemaphoreType.DMA((2,))]
    return local_call(
        functools.partial(stats_kernel, chunk),
        f"stats_{chunk}",
        shapes,
        day, tally, x,
        in_specs=[HBM] * 3 if chunk == 0 else [SMEM, SMEM, VMEM],
        out_specs=(VMEM,) * len(shapes),
        scratch_shapes=scratch,
    )


def split_kernel(got_ref, own_ref, *outs):
    lead = got_ref.shape[:-3]
    for i in range(got_ref.size // got_ref.shape[-1] // got_ref.shape[-2] // TILES):
        at, rest = [], i
        for n in reversed(lead):
            at.insert(0, rest % n)
            rest //= n
        out = outs[at[0]] if len(outs) > 1 else outs[0]
        for a, b, join in ((0, HIGH, jnp.add), (HIGH, LOW, jnp.maximum), (LOW, TILES, jnp.minimum)):
            value = join(got_ref.at[tuple(at)][a:b], own_ref.at[tuple(at)][a:b])
            (out.at[tuple(at[1:])] if len(at) > 1 else out)[a:b] = value


def table_kernel(got_ref, own_ref, table_ref):
    height = got_ref.shape[1]
    hours = got_ref[HOURS] + own_ref[HOURS]
    for i in range(SLOTS):
        total = got_ref[i] + own_ref[i]
        table_ref[i] = total / jnp.broadcast_to(hours[i : i + 1], (height, LANES))
        high = jnp.maximum(got_ref[HIGH + i], own_ref[HIGH + i])
        low = jnp.minimum(got_ref[LOW + i], own_ref[LOW + i])
        table_ref[SLOTS + i] = 4.0 / (high - low + 1.0)


def join_kernel(got_ref, own_ref, out_ref):
    out_ref[0] = got_ref[...]
    out_ref[1] = own_ref[...]


def depart_kernel(chunk, last, day_ref, x_ref, w_ref, recv_ref, own_ref, *refs):
    if chunk > 0:
        before_ref, refs = refs[0], refs[2:]
    out_ref, sums_ref, squares, ready, left = refs
    tiles, rows = x_ref.shape[0], x_ref.shape[1] // CHUNKS
    piece = tiles // PIECES
    bits = own_bits(chunk)
    flip = day_flip(bits)
    tables = [ref.reshape(GROUPS, *ref.shape[2:]) for ref in (recv_ref, own_ref)]
    half_rows = rows // 2
    height = half_rows // SUBLANES
    starts = [(1 - bits[0]) * half_rows, bits[0] * half_rows]
    weights = [w_ref[pl.ds(pl.multiple_of((chunk * 2 + b) * height, height), height), :] for b in (1 - bits[0], bits[0])]

    def tile(t, carry):
        for k in range(SUBLANES):
            slot, index = place(day_ref[t * SUBLANES + k], flip)
            total = None
            for half, table_ref in enumerate(tables):
                at = pl.ds(chunk * rows + starts[half] + k, height, stride=SUBLANES)
                table = table_ref.at[slot]
                departure = (x_ref[t, at, :] - table[index]) * table[SLOTS + index]
                ready[t, pl.ds(starts[half] + k, height, stride=SUBLANES), :] = departure
                square = weights[half] * departure * departure
                total = square if total is None else total + square
            squares[pl.ds(pl.multiple_of((t * SUBLANES + k) * height, height), height), :] = total
        return carry

    copies = []
    for p in range(PIECES):
        lax.fori_loop(p * piece, (p + 1) * piece, tile, 0)
        at = pl.ds(p * piece, piece)
        copies.append(pltpu.make_async_copy(ready.at[at], out_ref.at[at, pl.ds(chunk * rows, rows)], left.at[p]))
        copies[-1].start()
    sums = []
    for t in range(tiles):
        start = t * SUBLANES * height
        total = squares[pl.ds(start, SUBLANES, stride=height), :]
        for j in range(1, height):
            total += squares[pl.ds(start + j, SUBLANES, stride=height), :]
        at = pl.ds(t * SUBLANES, SUBLANES)
        if chunk > 0:
            total += before_ref[at, :]
        if last:
            sums.append(total)
        else:
            sums_ref[at, :] = total
    if last:
        by_step = jnp.sum(jnp.concatenate(sums).T, axis=0, keepdims=True)
        sums_ref[0:1, :] = by_step
        sums_ref[1:2, :] = jnp.full(by_step.shape, jnp.sum(w_ref[...]), jnp.float32)
        sums_ref[2:, :] = jnp.zeros((SUBLANES - 2, by_step.shape[1]), jnp.float32)
    for copy in copies:
        copy.wait()


def depart(chunk, day, x, w, recv, own, before, out):
    tiles, rows = x.shape[0], x.shape[1] // CHUNKS
    steps, last = tiles * SUBLANES, chunk == CHUNKS - 1
    inputs, specs, aliases = [day, x, w, recv, own], [SMEM] + [VMEM] * 4, {}
    if chunk > 0:
        inputs, specs, aliases = inputs + [before, out], specs + [VMEM, HBM], {6: 0}
    return local_call(
        functools.partial(depart_kernel, chunk, last),
        f"depart_{chunk}",
        (pltpu.HBM((tiles, rows * CHUNKS, LANES), jnp.float32), vmem(SUBLANES if last else steps, steps if last else LANES)),
        *inputs,
        in_specs=specs,
        out_specs=(HBM, VMEM),
        scratch_shapes=[
            pltpu.VMEM((rows // 2 * tiles, LANES), jnp.float32),
            pltpu.VMEM((tiles, rows, LANES), jnp.float32),
            pltpu.SemaphoreType.DMA((PIECES,)),
        ],
        input_output_aliases=aliases,
        vmem=4 << 20,
    )


def exchange(x, pair, name):
    years, spaces = lax.axis_size("year"), lax.axis_size("space")
    partners = [(y * spaces + s, (y ^ pair[s % 2]) * spaces + s) for y in range(years) for s in range(spaces)]
    with jax.named_scope(name):
        return lax.ppermute(pltpu.with_memory_space_constraint(x, pltpu.VMEM), AXES, partners)


def day_tables(chunk, send, keep):
    pairs = stage_bits(chunk, lax.axis_size("year"))
    for stage, pair in enumerate(pairs):
        got = exchange(send if stage < HALVINGS else keep, pair, f"send_{chunk}_{stage}")
        yield
        name = f"merge_{chunk}_{stage}"
        if stage < HALVINGS - 1:
            half = vmem(*got.shape[1:])
            send, keep = local_call(split_kernel, name, (half, half), got, keep, out_specs=(VMEM, VMEM))
        elif stage < len(pairs) - 1:
            keep = local_call(split_kernel, name, vmem(*got.shape), got, keep, out_specs=VMEM)
    table = local_call(table_kernel, name, vmem(2 * SLOTS, *got.shape[1:]), got, keep, out_specs=VMEM)
    for stage in reversed(range(HALVINGS)):
        number = len(pairs) + HALVINGS - 1 - stage
        got = exchange(table, pairs[stage], f"send_{chunk}_{number}")
        yield
        if stage > 0:
            table = local_call(join_kernel, f"merge_{chunk}_{number}", vmem(2, *got.shape), got, table, out_specs=VMEM)
    yield got, table


def on_device(thermal_reading, yearday_position, usable_observation_tally, location_surface_factor):
    steps, cells = thermal_reading.shape
    tiles, columns = steps // SUBLANES, cells // LANES
    x = thermal_reading.reshape(tiles, SUBLANES, columns, LANES).transpose(0, 2, 1, 3)
    x = x.reshape(tiles, columns * SUBLANES, LANES)
    w = location_surface_factor.reshape(columns, LANES)
    chunks = []
    for c in range(CHUNKS):
        send, keep, *copied = stats(c, yearday_position, usable_observation_tally, x)
        if copied:
            x = copied[0]
        chunks.append(day_tables(c, send, keep))
    results = [None] * CHUNKS
    while not all(results):
        for c in range(CHUNKS):
            results[c] = next(chunks[c])
    out = sums = None
    for c in range(CHUNKS):
        out, sums = depart(c, yearday_position, x, w, *results[c], sums, out)
    if lax.axis_size("space") == 2:
        sums += lax.ppermute(sums, "space", [(0, 1), (1, 0)])
    else:
        sums = lax.psum(sums, "space")
    out = out.reshape(tiles, columns, SUBLANES, LANES).transpose(0, 2, 1, 3).reshape(steps, cells)
    return out, sums[0] / sums[1]


def solution(mesh):
    return jax.shard_map(
        on_device,
        mesh=mesh,
        in_specs=(P("year", "space"), P("year"), P("year"), P("space")),
        out_specs=(P("year", "space"), P("year")),
        check_vma=False,
    )
```

time: 81.8 us -> 59.4 us (0.73)
  Pallas kernels: 20.5 us -> 7.6 us
  other arithmetic: 4.51 us -> 0.53 us
  waiting for transfers between devices: 27.5 us -> 31.3 us
  local copies, waits for them, and re-layouts: 3.53 us -> 0.01 us
  blocking collectives: 3.17 us -> 0 us
  starting transfers between devices: 21.4 us -> 19.1 us
    pallas_call x4 -> x16, Pallas kernels: 20.5 us -> 7.6 us  [local_call(): pl.pallas_call(kernel, in_specs=specs, out_shape=out_shape, name=name, co...]
    ppermute x14 -> x15, waiting for transfers between devices: 27.5 us -> 31.3 us  [the longest x14 30.1 us: exchange(): lax.ppermute(pltpu.with_memory_space_constraint(x, pltpu.VMEM), AXES, par...]
    psum x1 -> x0, blocking collectives: 3.17 us -> none  [on_device(): weighted_sq, area_total = lax.psum((weighted_sq, area_total), 'space')]
    ppermute x14 -> x15, starting transfers between devices: 21.4 us -> 19.1 us  [the longest x14 19 us: exchange(): lax.ppermute(pltpu.with_memory_space_constraint(x, pltpu.VMEM), AXES, par...]
    squeeze x2 -> x0, local copies, waits for them, and re-layouts: 2.13 us -> none  [day_tables(): send, keep = (local[0], local[1])]
    select_n x5 -> x0, other arithmetic: 1.68 us -> none  [merge(): return jnp.where(adds, a + b, jnp.maximum(a, b))]
    reduce_sum x2 -> x0, other arithmetic: 1.54 us -> none  [the longest x1 0.94 us: on_device(): jnp.sum(sums, axis=1)]
    unnamed x12 -> x6, local copies, waits for them, and re-layouts: 1.39 us -> 0.01 us
  transfers between devices with their start and end apart: 14 -> 15, of which waited for: 12 -> 13; matrix products, arithmetic and copies ran while one was open for 2% -> 0% of each run, Pallas kernels for 13% -> 6%
where the time goes in v2:
time: 59.4 us; the launch traced here: 59.3 us
  waiting for transfers between devices  31.3 us (53%)
  starting transfers between devices  19.1 us (32%)
  Pallas kernels  7.6 us (13%)
  between operations  0.75 us (1%)
    ppermute x14, waiting for transfers between devices, exchange(): lax.ppermute(pltpu.with_memory_space_constraint(x, pltpu.VMEM), AXES, par...  30.1 us
    ppermute x14, starting transfers between devices, exchange(): lax.ppermute(pltpu.with_memory_space_constraint(x, pltpu.VMEM), AXES, par...  19 us
    pallas_call x16, Pallas kernels, local_call(): pl.pallas_call(kernel, in_specs=specs, out_shape=out_shape, name=name, co...  7.6 us
  transfers between devices with their start and end apart: 15, of which 13 were waited for; matrix products, arithmetic and copies ran while one was open for 0% of the time, Pallas kernels for 6%

profile of v2, /device:TPU:0, one launch (start us, length us, event | category | flops | bytes accessed | tf_op | source)
XLA Modules:
  0.0 59.3 jit_solution(11617831541648879424)
XLA Ops:
  0.6 1.9 %stats_0.1 = (f32[2,2,25,8,128]{4,3,2,1,0:T(8,128)S(1)}, f32[2,2,25,8,128]{4,3,2,1,0:T(8,128)S(1)}, f32[16,256,128]{2,1,0:T(8,128)S(1)}) custom-call(s32[128]{0:T(128)} %day_ref.3, s32[128]{0:T(128)} %refs_1_.3, f32[16,256,128]{2,1,0:T(8,128)} %bitcast.16), custom_call_target="tpu_custom_call" | custom-call | tf_op jit(solution)/shard_map/stats_0/pallas_call | solution.py:31
  2.6 3.0 %collective-permute-start.7 = (f32[2,2,25,8,128]{4,3,2,1,0:T(8,128)S(1)}, f32[2,2,25,8,128]{4,3,2,1,0:T(8,128)S(1)}, u32[]{:S(2)}, u32[]{:S(2)}) collective-permute-start(f32[2,2,25,8,128]{4,3,2,1,0:T(8,128)S(1)} %get-tuple-element.26), channel_id=1, source_target_pairs={{0,2},{1,5},{2,0},{3,7},{4,6},{5,1},{6,4},{7,3},{8,10},{9,13},{10,... | collective-permute-start | bytes 1228808 | tf_op jit(solution)/shard_map/send_0_0/ppermute | solution.py:252
  5.6 1.4 %stats_1.1 = (f32[2,2,25,8,128]{4,3,2,1,0:T(8,128)S(1)}, f32[2,2,25,8,128]{4,3,2,1,0:T(8,128)S(1)}) custom-call(s32[128]{0:T(128)S(1)} %copy-done.1, s32[128]{0:T(128)S(1)} %copy-done.2, f32[16,256,128]{2,1,0:T(8,128)S(1)} %get-tuple-element.19.refs_2_.x_ref), custom_call_target="tpu_custom_call" | custom-call | tf_op jit(solution)/shard_map/stats_1/pallas_call | solution.py:31
  7.1 1.6 %collective-permute-start = (f32[2,2,25,8,128]{4,3,2,1,0:T(8,128)S(1)}, f32[2,2,25,8,128]{4,3,2,1,0:T(8,128)S(1)}, u32[]{:S(2)}, u32[]{:S(2)}) collective-permute-start(f32[2,2,25,8,128]{4,3,2,1,0:T(8,128)S(1)} %get-tuple-element.20), channel_id=1, source_target_pairs={{0,8},{1,9},{2,10},{3,11},{4,12},{5,13},{6,14},{7,15},{8,0},{9,1},... | collective-permute-start | bytes 1228808 | tf_op jit(solution)/shard_map/send_1_0/ppermute | solution.py:252
  8.7 2.8 %collective-permute-done.7.got_ref = f32[2,2,25,8,128]{4,3,2,1,0:T(8,128)S(1)} collective-permute-done((f32[2,2,25,8,128]{4,3,2,1,0:T(8,128)S(1)}, f32[2,2,25,8,128]{4,3,2,1,0:T(8,128)S(1)}, u32[]{:S(2)}, u32[]{:S(2)}) %collective-permute-start.7) | collective-permute-done | bytes 409632 | tf_op jit(solution)/shard_map/send_0_0/ppermute | solution.py:252
  11.6 2.1 %collective-permute-start.8 = (f32[2,25,8,128]{3,2,1,0:T(8,128)S(1)}, f32[2,25,8,128]{3,2,1,0:T(8,128)S(1)}, u32[]{:S(2)}, u32[]{:S(2)}) collective-permute-start(f32[2,25,8,128]{3,2,1,0:T(8,128)S(1)} %get-tuple-element.28), channel_id=1, source_target_pairs={{0,4},{1,3},{2,6},{3,1},{4,0},{5,7},{6,2},{7,5},{8,12},{9,11},{10,... | collective-permute-start | bytes 614408 | tf_op jit(solution)/shard_map/send_0_1/ppermute | solution.py:252
  13.7 4.4 %collective-permute-done.got_ref = f32[2,2,25,8,128]{4,3,2,1,0:T(8,128)S(1)} collective-permute-done((f32[2,2,25,8,128]{4,3,2,1,0:T(8,128)S(1)}, f32[2,2,25,8,128]{4,3,2,1,0:T(8,128)S(1)}, u32[]{:S(2)}, u32[]{:S(2)}) %collective-permute-start) | collective-permute-done | bytes 409632 | tf_op jit(solution)/shard_map/send_1_0/ppermute | solution.py:252
  18.6 1.8 %collective-permute-start.9 = (f32[25,8,128]{2,1,0:T(8,128)S(1)}, f32[25,8,128]{2,1,0:T(8,128)S(1)}, u32[]{:S(2)}, u32[]{:S(2)}) collective-permute-start(f32[25,8,128]{2,1,0:T(8,128)S(1)} %get-tuple-element.30), channel_id=1, source_target_pairs={{0,8},{1,9},{2,10},{3,11},{4,12},{5,13},{6,14},{7,15},{8,0},{9,1},... | collective-permute-start | bytes 307208 | tf_op jit(solution)/shard_map/send_0_2/ppermute | solution.py:252
  20.4 3.6 %collective-permute-done.1.got_ref = f32[2,25,8,128]{3,2,1,0:T(8,128)S(1)} collective-permute-done((f32[2,25,8,128]{3,2,1,0:T(8,128)S(1)}, f32[2,25,8,128]{3,2,1,0:T(8,128)S(1)}, u32[]{:S(2)}, u32[]{:S(2)}) %collective-permute-start.1) | collective-permute-done | bytes 204832 | tf_op jit(solution)/shard_map/send_1_1/ppermute | solution.py:252
  24.0 1.5 %collective-permute-start.2 = (f32[25,8,128]{2,1,0:T(8,128)S(1)}, f32[25,8,128]{2,1,0:T(8,128)S(1)}, u32[]{:S(2)}, u32[]{:S(2)}) collective-permute-start(f32[25,8,128]{2,1,0:T(8,128)S(1)} %get-tuple-element.24), channel_id=1, source_target_pairs={{0,2},{1,5},{2,0},{3,7},{4,6},{5,1},{6,4},{7,3},{8,10},{9,13},{10,... | collective-permute-start | bytes 307208 | tf_op jit(solution)/shard_map/send_1_2/ppermute | solution.py:252
  25.6 2.7 %collective-permute-start.10 = (f32[25,8,128]{2,1,0:T(8,128)S(1)}, f32[25,8,128]{2,1,0:T(8,128)S(1)}, u32[]{:S(2)}, u32[]{:S(2)}) collective-permute-start(f32[25,8,128]{2,1,0:T(8,128)S(1)} %merge_0_2.1.own_ref), channel_id=1, source_target_pairs={{0,16},{1,17},{2,18},{3,19},{4,20},{5,21},{6,22},{7,23},{8,24},{9,... | collective-permute-start | bytes 307208 | tf_op jit(solution)/shard_map/send_0_3/ppermute | solution.py:252
  28.8 2.7 %collective-permute-start.3 = (f32[25,8,128]{2,1,0:T(8,128)S(1)}, f32[25,8,128]{2,1,0:T(8,128)S(1)}, u32[]{:S(2)}, u32[]{:S(2)}) collective-permute-start(f32[25,8,128]{2,1,0:T(8,128)S(1)} %merge_1_2.1.own_ref), channel_id=1, source_target_pairs={{0,16},{1,17},{2,18},{3,19},{4,20},{5,21},{6,22},{7,23},{8,24},{9,... | collective-permute-start | bytes 307208 | tf_op jit(solution)/shard_map/send_1_3/ppermute | solution.py:252
  31.4 4.2 %collective-permute-done.10.got_ref = f32[25,8,128]{2,1,0:T(8,128)S(1)} collective-permute-done((f32[25,8,128]{2,1,0:T(8,128)S(1)}, f32[25,8,128]{2,1,0:T(8,128)S(1)}, u32[]{:S(2)}, u32[]{:S(2)}) %collective-permute-start.10) | collective-permute-done | bytes 102432 | tf_op jit(solution)/shard_map/send_0_3/ppermute | solution.py:252
  36.1 0.8 %collective-permute-done.3.got_ref = f32[25,8,128]{2,1,0:T(8,128)S(1)} collective-permute-done((f32[25,8,128]{2,1,0:T(8,128)S(1)}, f32[25,8,128]{2,1,0:T(8,128)S(1)}, u32[]{:S(2)}, u32[]{:S(2)}) %collective-permute-start.3) | collective-permute-done | bytes 102432 | tf_op jit(solution)/shard_map/send_1_3/ppermute | solution.py:252
  37.3 2.6 %collective-permute-done.11.got_ref = f32[16,8,128]{2,1,0:T(8,128)S(1)} collective-permute-done((f32[16,8,128]{2,1,0:T(8,128)S(1)}, f32[16,8,128]{2,1,0:T(8,128)S(1)}, u32[]{:S(2)}, u32[]{:S(2)}) %collective-permute-start.11) | collective-permute-done | bytes 65568 | tf_op jit(solution)/shard_map/send_0_4/ppermute | solution.py:252
  40.6 0.7 %collective-permute-done.4.got_ref = f32[16,8,128]{2,1,0:T(8,128)S(1)} collective-permute-done((f32[16,8,128]{2,1,0:T(8,128)S(1)}, f32[16,8,128]{2,1,0:T(8,128)S(1)}, u32[]{:S(2)}, u32[]{:S(2)}) %collective-permute-start.4) | collective-permute-done | bytes 65568 | tf_op jit(solution)/shard_map/send_1_4/ppermute | solution.py:252
  41.2 1.1 %collective-permute-start.5 = (f32[2,16,8,128]{3,2,1,0:T(8,128)S(1)}, f32[2,16,8,128]{3,2,1,0:T(8,128)S(1)}, u32[]{:S(2)}, u32[]{:S(2)}) collective-permute-start(f32[2,16,8,128]{3,2,1,0:T(8,128)S(1)} %merge_1_4.1.own_ref), channel_id=1, source_target_pairs={{0,4},{1,3},{2,6},{3,1},{4,0},{5,7},{6,2},{7,5},{8,12},{9,11},{10,... | collective-permute-start | bytes 393224 | tf_op jit(solution)/shard_map/send_1_5/ppermute | solution.py:252
  42.3 4.0 %collective-permute-done.12.got_ref = f32[2,16,8,128]{3,2,1,0:T(8,128)S(1)} collective-permute-done((f32[2,16,8,128]{3,2,1,0:T(8,128)S(1)}, f32[2,16,8,128]{3,2,1,0:T(8,128)S(1)}, u32[]{:S(2)}, u32[]{:S(2)}) %collective-permute-start.12) | collective-permute-done | bytes 131104 | tf_op jit(solution)/shard_map/send_0_5/ppermute | solution.py:252
  46.5 2.6 %collective-permute-done.5.got_ref = f32[2,16,8,128]{3,2,1,0:T(8,128)S(1)} collective-permute-done((f32[2,16,8,128]{3,2,1,0:T(8,128)S(1)}, f32[2,16,8,128]{3,2,1,0:T(8,128)S(1)}, u32[]{:S(2)}, u32[]{:S(2)}) %collective-permute-start.5) | collective-permute-done | bytes 131104 | tf_op jit(solution)/shard_map/send_1_5/ppermute | solution.py:252
  49.6 3.3 %collective-permute-done.13.recv_ref = f32[2,2,16,8,128]{4,3,2,1,0:T(8,128)S(1)} collective-permute-done((f32[2,2,16,8,128]{4,3,2,1,0:T(8,128)S(1)}, f32[2,2,16,8,128]{4,3,2,1,0:T(8,128)S(1)}, u32[]{:S(2)}, u32[]{:S(2)}) %collective-permute-start.13) | collective-permute-done | bytes 262176 | tf_op jit(solution)/shard_map/send_0_6/ppermute | solution.py:252
  52.8 1.9 %depart_0.1 = (f32[16,256,128]{2,1,0:T(8,128)}, f32[128,128]{1,0:T(8,128)S(1)}) custom-call(s32[128]{0:T(128)S(1)} %copy-done.1, f32[16,256,128]{2,1,0:T(8,128)S(1)} %get-tuple-element.19.refs_2_.x_ref, f32[32,128]{1,0:T(8,128)S(1)} %bitcast.13, f32[2,2,16,8,128]{4,3,2,1,0:T(8,128)S(1)} %collective-permute-done.13.recv_ref, ...), custom_call_target="tpu_custom_call" | custom-call | tf_op jit(solution)/shard_map/depart_0/pallas_call | solution.py:31
  54.8 0.7 %collective-permute-done.6.recv_ref = f32[2,2,16,8,128]{4,3,2,1,0:T(8,128)S(1)} collective-permute-done((f32[2,2,16,8,128]{4,3,2,1,0:T(8,128)S(1)}, f32[2,2,16,8,128]{4,3,2,1,0:T(8,128)S(1)}, u32[]{:S(2)}, u32[]{:S(2)}) %collective-permute-start.6) | collective-permute-done | bytes 262176 | tf_op jit(solution)/shard_map/send_1_6/ppermute | solution.py:252
  55.5 2.0 %depart_1.1 = (f32[16,256,128]{2,1,0:T(8,128)}, f32[8,128]{1,0:T(8,128)S(1)}) custom-call(s32[128]{0:T(128)S(1)} %copy-done.1, f32[16,256,128]{2,1,0:T(8,128)S(1)} %get-tuple-element.19.refs_2_.x_ref, f32[32,128]{1,0:T(8,128)S(1)} %bitcast.14, f32[2,2,16,8,128]{4,3,2,1,0:T(8,128)S(1)} %collective-permute-done.6.recv_ref, ...), custom_call_target="tpu_custom_call", output_to_operand_aliasing={{0}: (6, {})} | custom-call | tf_op jit(solution)/shard_map/depart_1/pallas_call | solution.py:31
  57.6 1.2 %collective-permute-done.14 = f32[8,128]{1,0:T(8,128)S(1)} collective-permute-done((f32[8,128]{1,0:T(8,128)S(1)}, f32[8,128]{1,0:T(8,128)S(1)}, u32[]{:S(2)}, u32[]{:S(2)}) %collective-permute-start.14) | collective-permute-done | bytes 4128 | tf_op jit(solution)/shard_map/ppermute | solution.py:296
  (30 shorter events, 3.8 us)
Async XLA Ops:
  0.6 5.0 %copy-start.1 = (s32[128]{0:T(128)S(1)}, s32[128]{0:T(128)}, u32[]{:S(2)}) copy-start(s32[128]{0:T(128)} %day_ref.3) | copy-start | bytes 1540
  0.6 5.0 %copy-start.2 = (s32[128]{0:T(128)S(1)}, s32[128]{0:T(128)}, u32[]{:S(2)}) copy-start(s32[128]{0:T(128)} %refs_1_.3) | copy-start | bytes 1540
  2.6 9.0 %collective-permute-start.7 = (f32[2,2,25,8,128]{4,3,2,1,0:T(8,128)S(1)}, f32[2,2,25,8,128]{4,3,2,1,0:T(8,128)S(1)}, u32[]{:S(2)}, u32[]{:S(2)}) collective-permute-start(f32[2,2,25,8,128]{4,3,2,1,0:T(8,128)S(1)} %get-tuple-element.26), channel_id=1, source_target_pairs={{0,2},{1,5},{2,0},{3,7},{4,6},{5,1},{6,4},{7,3},{8,10},{9,13},{10,... | collective-permute-start | bytes 1228808 | tf_op jit(solution)/shard_map/send_0_0/ppermute | solution.py:252
  7.1 11.0 %collective-permute-start = (f32[2,2,25,8,128]{4,3,2,1,0:T(8,128)S(1)}, f32[2,2,25,8,128]{4,3,2,1,0:T(8,128)S(1)}, u32[]{:S(2)}, u32[]{:S(2)}) collective-permute-start(f32[2,2,25,8,128]{4,3,2,1,0:T(8,128)S(1)} %get-tuple-element.20), channel_id=1, source_target_pairs={{0,8},{1,9},{2,10},{3,11},{4,12},{5,13},{6,14},{7,15},{8,0},{9,1},... | collective-permute-start | bytes 1228808 | tf_op jit(solution)/shard_map/send_1_0/ppermute | solution.py:252
  11.6 7.0 %collective-permute-start.8 = (f32[2,25,8,128]{3,2,1,0:T(8,128)S(1)}, f32[2,25,8,128]{3,2,1,0:T(8,128)S(1)}, u32[]{:S(2)}, u32[]{:S(2)}) collective-permute-start(f32[2,25,8,128]{3,2,1,0:T(8,128)S(1)} %get-tuple-element.28), channel_id=1, source_target_pairs={{0,4},{1,3},{2,6},{3,1},{4,0},{5,7},{6,2},{7,5},{8,12},{9,11},{10,... | collective-permute-start | bytes 614408 | tf_op jit(solution)/shard_map/send_0_1/ppermute | solution.py:252
  18.1 34.7 %copy-start = (f32[4096]{0:T(1024)S(1)}, f32[4096]{0:T(1024)}, u32[]{:S(2)}) copy-start(f32[4096]{0:T(1024)} %param.7) | copy-start | bytes 49156
  18.2 5.8 %collective-permute-start.1 = (f32[2,25,8,128]{3,2,1,0:T(8,128)S(1)}, f32[2,25,8,128]{3,2,1,0:T(8,128)S(1)}, u32[]{:S(2)}, u32[]{:S(2)}) collective-permute-start(f32[2,25,8,128]{3,2,1,0:T(8,128)S(1)} %get-tuple-element.22), channel_id=1, source_target_pairs={{0,4},{1,3},{2,6},{3,1},{4,0},{5,7},{6,2},{7,5},{8,12},{9,11},{10,... | collective-permute-start | bytes 614408 | tf_op jit(solution)/shard_map/send_1_1/ppermute | solution.py:252
  18.6 6.9 %collective-permute-start.9 = (f32[25,8,128]{2,1,0:T(8,128)S(1)}, f32[25,8,128]{2,1,0:T(8,128)S(1)}, u32[]{:S(2)}, u32[]{:S(2)}) collective-permute-start(f32[25,8,128]{2,1,0:T(8,128)S(1)} %get-tuple-element.30), channel_id=1, source_target_pairs={{0,8},{1,9},{2,10},{3,11},{4,12},{5,13},{6,14},{7,15},{8,0},{9,1},... | collective-permute-start | bytes 307208 | tf_op jit(solution)/shard_map/send_0_2/ppermute | solution.py:252
  24.0 4.7 %collective-permute-start.2 = (f32[25,8,128]{2,1,0:T(8,128)S(1)}, f32[25,8,128]{2,1,0:T(8,128)S(1)}, u32[]{:S(2)}, u32[]{:S(2)}) collective-permute-start(f32[25,8,128]{2,1,0:T(8,128)S(1)} %get-tuple-element.24), channel_id=1, source_target_pairs={{0,2},{1,5},{2,0},{3,7},{4,6},{5,1},{6,4},{7,3},{8,10},{9,13},{10,... | collective-permute-start | bytes 307208 | tf_op jit(solution)/shard_map/send_1_2/ppermute | solution.py:252
  25.6 10.0 %collective-permute-start.10 = (f32[25,8,128]{2,1,0:T(8,128)S(1)}, f32[25,8,128]{2,1,0:T(8,128)S(1)}, u32[]{:S(2)}, u32[]{:S(2)}) collective-permute-start(f32[25,8,128]{2,1,0:T(8,128)S(1)} %merge_0_2.1.own_ref), channel_id=1, source_target_pairs={{0,16},{1,17},{2,18},{3,19},{4,20},{5,21},{6,22},{7,23},{8,24},{9,... | collective-permute-start | bytes 307208 | tf_op jit(solution)/shard_map/send_0_3/ppermute | solution.py:252
  28.8 8.1 %collective-permute-start.3 = (f32[25,8,128]{2,1,0:T(8,128)S(1)}, f32[25,8,128]{2,1,0:T(8,128)S(1)}, u32[]{:S(2)}, u32[]{:S(2)}) collective-permute-start(f32[25,8,128]{2,1,0:T(8,128)S(1)} %merge_1_2.1.own_ref), channel_id=1, source_target_pairs={{0,16},{1,17},{2,18},{3,19},{4,20},{5,21},{6,22},{7,23},{8,24},{9,... | collective-permute-start | bytes 307208 | tf_op jit(solution)/shard_map/send_1_3/ppermute | solution.py:252
  35.6 4.3 %collective-permute-start.11 = (f32[16,8,128]{2,1,0:T(8,128)S(1)}, f32[16,8,128]{2,1,0:T(8,128)S(1)}, u32[]{:S(2)}, u32[]{:S(2)}) collective-permute-start(f32[16,8,128]{2,1,0:T(8,128)S(1)} %merge_0_3.1.own_ref), channel_id=1, source_target_pairs={{0,8},{1,9},{2,10},{3,11},{4,12},{5,13},{6,14},{7,15},{8,0},{9,1},... | collective-permute-start | bytes 196616 | tf_op jit(solution)/shard_map/send_0_4/ppermute | solution.py:252
  36.9 4.3 %collective-permute-start.4 = (f32[16,8,128]{2,1,0:T(8,128)S(1)}, f32[16,8,128]{2,1,0:T(8,128)S(1)}, u32[]{:S(2)}, u32[]{:S(2)}) collective-permute-start(f32[16,8,128]{2,1,0:T(8,128)S(1)} %merge_1_3.1.own_ref), channel_id=1, source_target_pairs={{0,2},{1,5},{2,0},{3,7},{4,6},{5,1},{6,4},{7,3},{8,10},{9,13},{10,... | collective-permute-start | bytes 196616 | tf_op jit(solution)/shard_map/send_1_4/ppermute | solution.py:252
  39.9 6.4 %collective-permute-start.12 = (f32[2,16,8,128]{3,2,1,0:T(8,128)S(1)}, f32[2,16,8,128]{3,2,1,0:T(8,128)S(1)}, u32[]{:S(2)}, u32[]{:S(2)}) collective-permute-start(f32[2,16,8,128]{3,2,1,0:T(8,128)S(1)} %merge_0_4.1.own_ref), channel_id=1, source_target_pairs={{0,4},{1,3},{2,6},{3,1},{4,0},{5,7},{6,2},{7,5},{8,12},{9,11},{10,... | collective-permute-start | bytes 393224 | tf_op jit(solution)/shard_map/send_0_5/ppermute | solution.py:252
  41.2 7.8 %collective-permute-start.5 = (f32[2,16,8,128]{3,2,1,0:T(8,128)S(1)}, f32[2,16,8,128]{3,2,1,0:T(8,128)S(1)}, u32[]{:S(2)}, u32[]{:S(2)}) collective-permute-start(f32[2,16,8,128]{3,2,1,0:T(8,128)S(1)} %merge_1_4.1.own_ref), channel_id=1, source_target_pairs={{0,4},{1,3},{2,6},{3,1},{4,0},{5,7},{6,2},{7,5},{8,12},{9,11},{10,... | collective-permute-start | bytes 393224 | tf_op jit(solution)/shard_map/send_1_5/ppermute | solution.py:252
  46.4 6.4 %collective-permute-start.13 = (f32[2,2,16,8,128]{4,3,2,1,0:T(8,128)S(1)}, f32[2,2,16,8,128]{4,3,2,1,0:T(8,128)S(1)}, u32[]{:S(2)}, u32[]{:S(2)}) collective-permute-start(f32[2,2,16,8,128]{4,3,2,1,0:T(8,128)S(1)} %merge_0_5.1.own_ref), channel_id=1, source_target_pairs={{0,2},{1,5},{2,0},{3,7},{4,6},{5,1},{6,4},{7,3},{8,10},{9,13},{10,... | collective-permute-start | bytes 786440 | tf_op jit(solution)/shard_map/send_0_6/ppermute | solution.py:252
  49.1 6.4 %collective-permute-start.6 = (f32[2,2,16,8,128]{4,3,2,1,0:T(8,128)S(1)}, f32[2,2,16,8,128]{4,3,2,1,0:T(8,128)S(1)}, u32[]{:S(2)}, u32[]{:S(2)}) collective-permute-start(f32[2,2,16,8,128]{4,3,2,1,0:T(8,128)S(1)} %merge_1_5.1.own_ref), channel_id=1, source_target_pairs={{0,8},{1,9},{2,10},{3,11},{4,12},{5,13},{6,14},{7,15},{8,0},{9,1},... | collective-permute-start | bytes 786440 | tf_op jit(solution)/shard_map/send_1_6/ppermute | solution.py:252
  57.5 1.2 %collective-permute-start.14 = (f32[8,128]{1,0:T(8,128)S(1)}, f32[8,128]{1,0:T(8,128)S(1)}, u32[]{:S(2)}, u32[]{:S(2)}) collective-permute-start(f32[8,128]{1,0:T(8,128)S(1)} %get-tuple-element.35), channel_id=1, source_target_pairs={{0,1},{1,0},{2,3},{3,2},{4,5},{5,4},{6,7},{7,6},{8,9},{9,8},{10,11... | collective-permute-start | bytes 12296 | tf_op jit(solution)/shard_map/ppermute | solution.py:296

commit v3 on v2

--- a/solution.py
+++ b/solution.py
@@ -1,4 +1,5 @@
 import functools
+import math
 
 import jax
 import jax.numpy as jnp
@@ -9,12 +10,13 @@
 
 DAYS = 30
 SUBLANES, LANES = 8, 128
-GROUPS = 4
+GROUPS = 2
 SLOTS = -(-DAYS // GROUPS)
 CHUNKS = 2
-HALVINGS = 3
+HALVINGS = 2
+REST = 2 * GROUPS >> HALVINGS
 HOURS, HIGH, LOW, TILES = SLOTS, SLOTS + 1, 2 * SLOTS + 1, 3 * SLOTS + 1
-ORDERS = (((0, 1), (1, 0), (2, 2), (3, 3)), ((2, 2), (1, 0), (0, 1), (3, 3)))
+ORDERS = (((0, 2), (1, 3), (2, 1), (3, 0)), ((1, 2), (0, 3), (3, 1), (2, 0)))
 AXES = ("year", "space")
 PIECES = 4
 
@@ -36,6 +38,7 @@
 
 
 def stage_bits(chunk, years):
+    assert HALVINGS > 1 and 2 * GROUPS >= 1 << HALVINGS and SLOTS <= 2 * SUBLANES
     count = years.bit_length() - 1
     assert years == 1 << count and count > HALVINGS
     return [tuple(1 << b for b in pair) for pair in ORDERS[chunk]] + [(1 << b, 1 << b) for b in range(4, count)]
@@ -48,12 +51,16 @@
 
 
 def day_flip(bits):
-    return ((1 - bits[1]) * 2 + 1 - bits[2]) * SLOTS
+    return sum((1 - bit) * (GROUPS >> i) for i, bit in enumerate(bits) if i > 0)
 
 
 def place(day, flip):
-    day = lax.bitwise_xor(day, flip)
-    return lax.shift_right_logical(day, SLOTS.bit_length() - 1), lax.bitwise_and(day, SLOTS - 1)
+    group = sum((day >= g * SLOTS).astype(jnp.int32) for g in range(1, GROUPS))
+    return lax.bitwise_xor(group, flip), day - group * SLOTS
+
+
+def by_group(*refs):
+    return [ref.reshape(math.prod(ref.shape[:-3]), *ref.shape[-3:]) if len(ref.shape) > 3 else ref for ref in refs]
 
 
 def stats_kernel(chunk, *refs):
@@ -77,7 +84,7 @@
     flip = day_flip(bits)
     half = rows // 2
     height = half // SUBLANES
-    outs = [ref.reshape(GROUPS, *ref.shape[2:]) for ref in (send_ref, keep_ref)]
+    outs = by_group(send_ref, keep_ref)
     starts = [chunk * rows + (1 - bits[0]) * half, chunk * rows + bits[0] * half]
     for out in outs:
         for slot in range(GROUPS):
@@ -109,18 +116,20 @@
         if copies:
             copies[p].wait()
         lax.fori_loop(p * piece, (p + 1) * piece, tile, 0)
-    for d in range(DAYS):
-        slot, index = place(jnp.int32(d), flip)
-        row = jnp.full((1, LANES), hours[d].astype(jnp.float32), jnp.float32)
-        for out in outs:
-            out[slot, HOURS, pl.ds(index, 1), :] = row
+    left = lax.broadcasted_iota(jnp.int32, (1, LANES), 1) < LANES // 2
+    for group in range(GROUPS):
+        slot = lax.bitwise_xor(group, flip)
+        for k in range(SUBLANES):
+            pair = [hours[group * SLOTS + min(i, SLOTS - 1)].astype(jnp.float32) for i in (k, k + SUBLANES)]
+            for out in outs:
+                out[slot, HOURS, k : k + 1, :] = jnp.where(left, *pair)
     for copy in copies[PIECES:]:
         copy.wait()
 
 
 def stats(chunk, day, tally, x):
     tiles, rows = x.shape[0], x.shape[1] // CHUNKS
-    half = vmem(2, GROUPS // 2, TILES, rows // 2 // SUBLANES, LANES)
+    half = vmem(*(2,) * (HALVINGS - 1), REST, TILES, rows // 2 // SUBLANES, LANES)
     shapes, scratch = (half, half), [pltpu.SMEM((GROUPS * SLOTS,), jnp.int32)]
     if chunk == 0:
         shapes += (vmem(*x.shape),)
@@ -137,28 +146,27 @@
     )
 
 
-def split_kernel(got_ref, own_ref, *outs):
-    lead = got_ref.shape[:-3]
-    for i in range(got_ref.size // got_ref.shape[-1] // got_ref.shape[-2] // TILES):
-        at, rest = [], i
-        for n in reversed(lead):
-            at.insert(0, rest % n)
-            rest //= n
-        out = outs[at[0]] if len(outs) > 1 else outs[0]
+def merge_kernel(got_ref, own_ref, *out_refs):
+    got, own, *outs = by_group(got_ref, own_ref, *out_refs)
+    each = got.shape[0] // len(outs)
+    for i in range(got.shape[0]):
         for a, b, join in ((0, HIGH, jnp.add), (HIGH, LOW, jnp.maximum), (LOW, TILES, jnp.minimum)):
-            value = join(got_ref.at[tuple(at)][a:b], own_ref.at[tuple(at)][a:b])
-            (out.at[tuple(at[1:])] if len(at) > 1 else out)[a:b] = value
+            outs[i // each][i % each, a:b] = join(got[i, a:b], own[i, a:b])
 
 
 def table_kernel(got_ref, own_ref, table_ref):
-    height = got_ref.shape[1]
-    hours = got_ref[HOURS] + own_ref[HOURS]
-    for i in range(SLOTS):
-        total = got_ref[i] + own_ref[i]
-        table_ref[i] = total / jnp.broadcast_to(hours[i : i + 1], (height, LANES))
-        high = jnp.maximum(got_ref[HIGH + i], own_ref[HIGH + i])
-        low = jnp.minimum(got_ref[LOW + i], own_ref[LOW + i])
-        table_ref[SLOTS + i] = 4.0 / (high - low + 1.0)
+    for g in range(REST):
+        got, own, table = got_ref.at[g], own_ref.at[g], table_ref.at[g]
+        hours = got[HOURS] + own[HOURS]
+        left = lax.broadcasted_iota(jnp.int32, hours.shape, 1) < LANES // 2
+        other = pltpu.roll(hours, LANES // 2, axis=1)
+        hours = jnp.concatenate([jnp.where(left, hours, other), jnp.where(left, other, hours)])
+        for i in range(SLOTS):
+            total = got[i] + own[i]
+            table[i] = total / jnp.broadcast_to(hours[i : i + 1], total.shape)
+            high = jnp.maximum(got[HIGH + i], own[HIGH + i])
+            low = jnp.minimum(got[LOW + i], own[LOW + i])
+            table[SLOTS + i] = 4.0 / (high - low + 1.0)
 
 
 def join_kernel(got_ref, own_ref, out_ref):
@@ -174,7 +182,7 @@
     piece = tiles // PIECES
     bits = own_bits(chunk)
     flip = day_flip(bits)
-    tables = [ref.reshape(GROUPS, *ref.shape[2:]) for ref in (recv_ref, own_ref)]
+    tables = by_group(recv_ref, own_ref)
     half_rows = rows // 2
     height = half_rows // SUBLANES
     starts = [(1 - bits[0]) * half_rows, bits[0] * half_rows]
@@ -260,10 +268,10 @@
         name = f"merge_{chunk}_{stage}"
         if stage < HALVINGS - 1:
             half = vmem(*got.shape[1:])
-            send, keep = local_call(split_kernel, name, (half, half), got, keep, out_specs=(VMEM, VMEM))
+            send, keep = local_call(merge_kernel, name, (half, half), got, keep, out_specs=(VMEM, VMEM))
         elif stage < len(pairs) - 1:
-            keep = local_call(split_kernel, name, vmem(*got.shape), got, keep, out_specs=VMEM)
-    table = local_call(table_kernel, name, vmem(2 * SLOTS, *got.shape[1:]), got, keep, out_specs=VMEM)
+            keep = local_call(merge_kernel, name, vmem(*got.shape), got, keep, out_specs=VMEM)
+    table = local_call(table_kernel, name, vmem(REST, 2 * SLOTS, *got.shape[-2:]), got, keep, out_specs=VMEM)
     for stage in reversed(range(HALVINGS)):
         number = len(pairs) + HALVINGS - 1 - stage
         got = exchange(table, pairs[stage], f"send_{chunk}_{number}")

time: 59.4 us -> 54.2 us (0.912)
  waiting for transfers between devices: 31.3 us -> 18.4 us
  starting transfers between devices: 19.1 us -> 26.1 us
    ppermute x14 -> x12, waiting for transfers between devices: 30.1 us -> 17.2 us  [exchange(): lax.ppermute(pltpu.with_memory_space_constraint(x, pltpu.VMEM), AXES, par...]
    ppermute x14 -> x12, starting transfers between devices: 19 us -> 26 us  [exchange(): lax.ppermute(pltpu.with_memory_space_constraint(x, pltpu.VMEM), AXES, par...]
    pallas_call x16 -> x14, Pallas kernels: 7.6 us -> 7.85 us  [local_call(): pl.pallas_call(kernel, in_specs=specs, out_shape=out_shape, name=name, co...]
  transfers between devices with their start and end apart: 15 -> 13, of which waited for: 13 -> 11; matrix products, arithmetic and copies ran while one was open for 0% -> 0% of each run, Pallas kernels for 6% -> 7%
where the time goes in v3:
time: 54.2 us; the launch traced here: 53.6 us
  starting transfers between devices  26.1 us (48%)
  waiting for transfers between devices  18.4 us (34%)
  Pallas kernels  7.85 us (14%)
  between operations  0.73 us (1%)
    ppermute x12, starting transfers between devices, exchange(): lax.ppermute(pltpu.with_memory_space_constraint(x, pltpu.VMEM), AXES, par...  26 us
    ppermute x12, waiting for transfers between devices, exchange(): lax.ppermute(pltpu.with_memory_space_constraint(x, pltpu.VMEM), AXES, par...  17.2 us
    pallas_call x14, Pallas kernels, local_call(): pl.pallas_call(kernel, in_specs=specs, out_shape=out_shape, name=name, co...  7.85 us
    ppermute x1, waiting for transfers between devices, on_device(): sums += lax.ppermute(sums, 'space', [(0, 1), (1, 0)])  1.15 us
  transfers between devices with their start and end apart: 13, of which 11 were waited for; matrix products, arithmetic and copies ran while one was open for 0% of the time, Pallas kernels for 7%

profile of v3, /device:TPU:0, one launch (start us, length us, event | category | flops | bytes accessed | tf_op | source)
XLA Modules:
  0.0 53.6 jit_solution(13194606746145959956)
XLA Ops:
  0.6 1.9 %stats_0.1 = (f32[2,1,46,8,128]{4,3,2,1,0:T(8,128)S(1)}, f32[2,1,46,8,128]{4,3,2,1,0:T(8,128)S(1)}, f32[16,256,128]{2,1,0:T(8,128)S(1)}) custom-call(s32[128]{0:T(128)} %day_ref.3, s32[128]{0:T(128)} %refs_1_.3, f32[16,256,128]{2,1,0:T(8,128)} %bitcast.16), custom_call_target="tpu_custom_call" | custom-call | tf_op jit(solution)/shard_map/stats_0/pallas_call | solution.py:33
  2.6 3.0 %collective-permute-start.6 = (f32[2,1,46,8,128]{4,3,2,1,0:T(8,128)S(1)}, f32[2,1,46,8,128]{4,3,2,1,0:T(8,128)S(1)}, u32[]{:S(2)}, u32[]{:S(2)}) collective-permute-start(f32[2,1,46,8,128]{4,3,2,1,0:T(8,128)S(1)} %get-tuple-element.20), channel_id=1, source_target_pairs={{0,2},{1,9},{2,0},{3,11},{4,6},{5,13},{6,4},{7,15},{8,10},{9,1},{1... | collective-permute-start | bytes 1130504 | tf_op jit(solution)/shard_map/send_0_0/ppermute | solution.py:260
  5.6 1.4 %stats_1.1 = (f32[2,1,46,8,128]{4,3,2,1,0:T(8,128)S(1)}, f32[2,1,46,8,128]{4,3,2,1,0:T(8,128)S(1)}) custom-call(s32[128]{0:T(128)S(1)} %copy-done.1, s32[128]{0:T(128)S(1)} %copy-done.2, f32[16,256,128]{2,1,0:T(8,128)S(1)} %get-tuple-element.15.refs_2_.x_ref), custom_call_target="tpu_custom_call" | custom-call | tf_op jit(solution)/shard_map/stats_1/pallas_call | solution.py:33
  7.1 1.6 %collective-permute-start = (f32[2,1,46,8,128]{4,3,2,1,0:T(8,128)S(1)}, f32[2,1,46,8,128]{4,3,2,1,0:T(8,128)S(1)}, u32[]{:S(2)}, u32[]{:S(2)}) collective-permute-start(f32[2,1,46,8,128]{4,3,2,1,0:T(8,128)S(1)} %get-tuple-element.16), channel_id=1, source_target_pairs={{0,4},{1,9},{2,6},{3,11},{4,0},{5,13},{6,2},{7,15},{8,12},{9,1},{1... | collective-permute-start | bytes 1130504 | tf_op jit(solution)/shard_map/send_1_0/ppermute | solution.py:260
  8.7 2.5 %collective-permute-done.6.got_ref = f32[2,1,46,8,128]{4,3,2,1,0:T(8,128)S(1)} collective-permute-done((f32[2,1,46,8,128]{4,3,2,1,0:T(8,128)S(1)}, f32[2,1,46,8,128]{4,3,2,1,0:T(8,128)S(1)}, u32[]{:S(2)}, u32[]{:S(2)}) %collective-permute-start.6) | collective-permute-done | bytes 376864 | tf_op jit(solution)/shard_map/send_0_0/ppermute | solution.py:260
  11.2 2.1 %collective-permute-start.7 = (f32[1,46,8,128]{3,2,1,0:T(8,128)S(1)}, f32[1,46,8,128]{3,2,1,0:T(8,128)S(1)}, u32[]{:S(2)}, u32[]{:S(2)}) collective-permute-start(f32[1,46,8,128]{3,2,1,0:T(8,128)S(1)} %get-tuple-element.22), channel_id=1, source_target_pairs={{0,4},{1,17},{2,6},{3,19},{4,0},{5,21},{6,2},{7,23},{8,12},{9,25},... | collective-permute-start | bytes 565256 | tf_op jit(solution)/shard_map/send_0_1/ppermute | solution.py:260
  13.4 1.4 %collective-permute-done.got_ref = f32[2,1,46,8,128]{4,3,2,1,0:T(8,128)S(1)} collective-permute-done((f32[2,1,46,8,128]{4,3,2,1,0:T(8,128)S(1)}, f32[2,1,46,8,128]{4,3,2,1,0:T(8,128)S(1)}, u32[]{:S(2)}, u32[]{:S(2)}) %collective-permute-start) | collective-permute-done | bytes 376864 | tf_op jit(solution)/shard_map/send_1_0/ppermute | solution.py:260
  15.0 2.0 %collective-permute-done.7.got_ref = f32[1,46,8,128]{3,2,1,0:T(8,128)S(1)} collective-permute-done((f32[1,46,8,128]{3,2,1,0:T(8,128)S(1)}, f32[1,46,8,128]{3,2,1,0:T(8,128)S(1)}, u32[]{:S(2)}, u32[]{:S(2)}) %collective-permute-start.7) | collective-permute-done | bytes 188448 | tf_op jit(solution)/shard_map/send_0_1/ppermute | solution.py:260
  16.9 2.1 %collective-permute-start.8 = (f32[1,46,8,128]{3,2,1,0:T(8,128)S(1)}, f32[1,46,8,128]{3,2,1,0:T(8,128)S(1)}, u32[]{:S(2)}, u32[]{:S(2)}) collective-permute-start(f32[1,46,8,128]{3,2,1,0:T(8,128)S(1)} %merge_0_1.1.own_ref), channel_id=1, source_target_pairs={{0,8},{1,5},{2,10},{3,7},{4,12},{5,1},{6,14},{7,3},{8,0},{9,13},{1... | collective-permute-start | bytes 565256 | tf_op jit(solution)/shard_map/send_0_2/ppermute | solution.py:260
  19.1 1.3 %collective-permute-done.1.got_ref = f32[1,46,8,128]{3,2,1,0:T(8,128)S(1)} collective-permute-done((f32[1,46,8,128]{3,2,1,0:T(8,128)S(1)}, f32[1,46,8,128]{3,2,1,0:T(8,128)S(1)}, u32[]{:S(2)}, u32[]{:S(2)}) %collective-permute-start.1) | collective-permute-done | bytes 188448 | tf_op jit(solution)/shard_map/send_1_1/ppermute | solution.py:260
  20.5 2.7 %collective-permute-start.2 = (f32[1,46,8,128]{3,2,1,0:T(8,128)S(1)}, f32[1,46,8,128]{3,2,1,0:T(8,128)S(1)}, u32[]{:S(2)}, u32[]{:S(2)}) collective-permute-start(f32[1,46,8,128]{3,2,1,0:T(8,128)S(1)} %merge_1_1.1.own_ref), channel_id=1, source_target_pairs={{0,16},{1,5},{2,18},{3,7},{4,20},{5,1},{6,22},{7,3},{8,24},{9,13},... | collective-permute-start | bytes 565256 | tf_op jit(solution)/shard_map/send_1_2/ppermute | solution.py:260
  23.1 1.5 %collective-permute-done.8.got_ref = f32[1,46,8,128]{3,2,1,0:T(8,128)S(1)} collective-permute-done((f32[1,46,8,128]{3,2,1,0:T(8,128)S(1)}, f32[1,46,8,128]{3,2,1,0:T(8,128)S(1)}, u32[]{:S(2)}, u32[]{:S(2)}) %collective-permute-start.8) | collective-permute-done | bytes 188448 | tf_op jit(solution)/shard_map/send_0_2/ppermute | solution.py:260
  24.7 1.5 %collective-permute-start.9 = (f32[1,46,8,128]{3,2,1,0:T(8,128)S(1)}, f32[1,46,8,128]{3,2,1,0:T(8,128)S(1)}, u32[]{:S(2)}, u32[]{:S(2)}) collective-permute-start(f32[1,46,8,128]{3,2,1,0:T(8,128)S(1)} %merge_0_2.1.own_ref), channel_id=1, source_target_pairs={{0,16},{1,3},{2,18},{3,1},{4,20},{5,7},{6,22},{7,5},{8,24},{9,11},... | collective-permute-start | bytes 565256 | tf_op jit(solution)/shard_map/send_0_3/ppermute | solution.py:260
  26.2 2.8 %collective-permute-done.2.got_ref = f32[1,46,8,128]{3,2,1,0:T(8,128)S(1)} collective-permute-done((f32[1,46,8,128]{3,2,1,0:T(8,128)S(1)}, f32[1,46,8,128]{3,2,1,0:T(8,128)S(1)}, u32[]{:S(2)}, u32[]{:S(2)}) %collective-permute-start.2) | collective-permute-done | bytes 188448 | tf_op jit(solution)/shard_map/send_1_2/ppermute | solution.py:260
  29.0 2.8 %collective-permute-start.3 = (f32[1,46,8,128]{3,2,1,0:T(8,128)S(1)}, f32[1,46,8,128]{3,2,1,0:T(8,128)S(1)}, u32[]{:S(2)}, u32[]{:S(2)}) collective-permute-start(f32[1,46,8,128]{3,2,1,0:T(8,128)S(1)} %merge_1_2.1.own_ref), channel_id=1, source_target_pairs={{0,8},{1,3},{2,10},{3,1},{4,12},{5,7},{6,14},{7,5},{8,0},{9,11},{1... | collective-permute-start | bytes 565256 | tf_op jit(solution)/shard_map/send_1_3/ppermute | solution.py:260
  31.9 1.4 %collective-permute-done.9.got_ref = f32[1,46,8,128]{3,2,1,0:T(8,128)S(1)} collective-permute-done((f32[1,46,8,128]{3,2,1,0:T(8,128)S(1)}, f32[1,46,8,128]{3,2,1,0:T(8,128)S(1)}, u32[]{:S(2)}, u32[]{:S(2)}) %collective-permute-start.9) | collective-permute-done | bytes 188448 | tf_op jit(solution)/shard_map/send_0_3/ppermute | solution.py:260
  33.4 2.6 %collective-permute-start.10 = (f32[1,30,8,128]{3,2,1,0:T(8,128)S(1)}, f32[1,30,8,128]{3,2,1,0:T(8,128)S(1)}, u32[]{:S(2)}, u32[]{:S(2)}) collective-permute-start(f32[1,30,8,128]{3,2,1,0:T(8,128)S(1)} %merge_0_3.1.own_ref), channel_id=1, source_target_pairs={{0,4},{1,17},{2,6},{3,19},{4,0},{5,21},{6,2},{7,23},{8,12},{9,25},... | collective-permute-start | bytes 368648 | tf_op jit(solution)/shard_map/send_0_4/ppermute | solution.py:260
  36.0 0.6 %collective-permute-done.3.got_ref = f32[1,46,8,128]{3,2,1,0:T(8,128)S(1)} collective-permute-done((f32[1,46,8,128]{3,2,1,0:T(8,128)S(1)}, f32[1,46,8,128]{3,2,1,0:T(8,128)S(1)}, u32[]{:S(2)}, u32[]{:S(2)}) %collective-permute-start.3) | collective-permute-done | bytes 188448 | tf_op jit(solution)/shard_map/send_1_3/ppermute | solution.py:260
  36.7 2.5 %collective-permute-start.4 = (f32[1,30,8,128]{3,2,1,0:T(8,128)S(1)}, f32[1,30,8,128]{3,2,1,0:T(8,128)S(1)}, u32[]{:S(2)}, u32[]{:S(2)}) collective-permute-start(f32[1,30,8,128]{3,2,1,0:T(8,128)S(1)} %merge_1_3.1.own_ref), channel_id=1, source_target_pairs={{0,2},{1,17},{2,0},{3,19},{4,6},{5,21},{6,4},{7,23},{8,10},{9,25},... | collective-permute-start | bytes 368648 | tf_op jit(solution)/shard_map/send_1_4/ppermute | solution.py:260
  39.2 4.3 %collective-permute-start.11 = (f32[2,1,30,8,128]{4,3,2,1,0:T(8,128)S(1)}, f32[2,1,30,8,128]{4,3,2,1,0:T(8,128)S(1)}, u32[]{:S(2)}, u32[]{:S(2)}) collective-permute-start(f32[2,1,30,8,128]{4,3,2,1,0:T(8,128)S(1)} %merge_0_4.1.own_ref), channel_id=1, source_target_pairs={{0,2},{1,9},{2,0},{3,11},{4,6},{5,13},{6,4},{7,15},{8,10},{9,1},{1... | collective-permute-start | bytes 737288 | tf_op jit(solution)/shard_map/send_0_5/ppermute | solution.py:260
  44.1 3.6 %collective-permute-done.11.recv_ref = f32[2,1,30,8,128]{4,3,2,1,0:T(8,128)S(1)} collective-permute-done((f32[2,1,30,8,128]{4,3,2,1,0:T(8,128)S(1)}, f32[2,1,30,8,128]{4,3,2,1,0:T(8,128)S(1)}, u32[]{:S(2)}, u32[]{:S(2)}) %collective-permute-start.11) | collective-permute-done | bytes 245792 | tf_op jit(solution)/shard_map/send_0_5/ppermute | solution.py:260
  47.6 2.0 %depart_0.1 = (f32[16,256,128]{2,1,0:T(8,128)}, f32[128,128]{1,0:T(8,128)S(1)}) custom-call(s32[128]{0:T(128)S(1)} %copy-done.1, f32[16,256,128]{2,1,0:T(8,128)S(1)} %get-tuple-element.15.refs_2_.x_ref, f32[32,128]{1,0:T(8,128)S(1)} %bitcast.13, f32[2,1,30,8,128]{4,3,2,1,0:T(8,128)S(1)} %collective-permute-done.11.recv_ref, ...), custom_call_target="tpu_custom_call" | custom-call | tf_op jit(solution)/shard_map/depart_0/pallas_call | solution.py:33
  49.7 2.1 %depart_1.1 = (f32[16,256,128]{2,1,0:T(8,128)}, f32[8,128]{1,0:T(8,128)S(1)}) custom-call(s32[128]{0:T(128)S(1)} %copy-done.1, f32[16,256,128]{2,1,0:T(8,128)S(1)} %get-tuple-element.15.refs_2_.x_ref, f32[32,128]{1,0:T(8,128)S(1)} %bitcast.14, f32[2,1,30,8,128]{4,3,2,1,0:T(8,128)S(1)} %collective-permute-done.5.recv_ref, ...), custom_call_target="tpu_custom_call", output_to_operand_aliasing={{0}: (6, {})} | custom-call | tf_op jit(solution)/shard_map/depart_1/pallas_call | solution.py:33
  51.9 1.2 %collective-permute-done.12 = f32[8,128]{1,0:T(8,128)S(1)} collective-permute-done((f32[8,128]{1,0:T(8,128)S(1)}, f32[8,128]{1,0:T(8,128)S(1)}, u32[]{:S(2)}, u32[]{:S(2)}) %collective-permute-start.12) | collective-permute-done | bytes 4128 | tf_op jit(solution)/shard_map/ppermute | solution.py:304
  (24 shorter events, 1.8 us)
Async XLA Ops:
  0.6 5.0 %copy-start.1 = (s32[128]{0:T(128)S(1)}, s32[128]{0:T(128)}, u32[]{:S(2)}) copy-start(s32[128]{0:T(128)} %day_ref.3) | copy-start | bytes 1540
  0.6 5.0 %copy-start.2 = (s32[128]{0:T(128)S(1)}, s32[128]{0:T(128)}, u32[]{:S(2)}) copy-start(s32[128]{0:T(128)} %refs_1_.3) | copy-start | bytes 1540
  2.6 8.6 %collective-permute-start.6 = (f32[2,1,46,8,128]{4,3,2,1,0:T(8,128)S(1)}, f32[2,1,46,8,128]{4,3,2,1,0:T(8,128)S(1)}, u32[]{:S(2)}, u32[]{:S(2)}) collective-permute-start(f32[2,1,46,8,128]{4,3,2,1,0:T(8,128)S(1)} %get-tuple-element.20), channel_id=1, source_target_pairs={{0,2},{1,9},{2,0},{3,11},{4,6},{5,13},{6,4},{7,15},{8,10},{9,1},{1... | collective-permute-start | bytes 1130504 | tf_op jit(solution)/shard_map/send_0_0/ppermute | solution.py:260
  7.1 7.7 %collective-permute-start = (f32[2,1,46,8,128]{4,3,2,1,0:T(8,128)S(1)}, f32[2,1,46,8,128]{4,3,2,1,0:T(8,128)S(1)}, u32[]{:S(2)}, u32[]{:S(2)}) collective-permute-start(f32[2,1,46,8,128]{4,3,2,1,0:T(8,128)S(1)} %get-tuple-element.16), channel_id=1, source_target_pairs={{0,4},{1,9},{2,6},{3,11},{4,0},{5,13},{6,2},{7,15},{8,12},{9,1},{1... | collective-permute-start | bytes 1130504 | tf_op jit(solution)/shard_map/send_1_0/ppermute | solution.py:260
  11.2 5.7 %collective-permute-start.7 = (f32[1,46,8,128]{3,2,1,0:T(8,128)S(1)}, f32[1,46,8,128]{3,2,1,0:T(8,128)S(1)}, u32[]{:S(2)}, u32[]{:S(2)}) collective-permute-start(f32[1,46,8,128]{3,2,1,0:T(8,128)S(1)} %get-tuple-element.22), channel_id=1, source_target_pairs={{0,4},{1,17},{2,6},{3,19},{4,0},{5,21},{6,2},{7,23},{8,12},{9,25},... | collective-permute-start | bytes 565256 | tf_op jit(solution)/shard_map/send_0_1/ppermute | solution.py:260
  14.8 5.6 %collective-permute-start.1 = (f32[1,46,8,128]{3,2,1,0:T(8,128)S(1)}, f32[1,46,8,128]{3,2,1,0:T(8,128)S(1)}, u32[]{:S(2)}, u32[]{:S(2)}) collective-permute-start(f32[1,46,8,128]{3,2,1,0:T(8,128)S(1)} %get-tuple-element.18), channel_id=1, source_target_pairs={{0,2},{1,17},{2,0},{3,19},{4,6},{5,21},{6,4},{7,23},{8,10},{9,25},... | collective-permute-start | bytes 565256 | tf_op jit(solution)/shard_map/send_1_1/ppermute | solution.py:260
  16.9 30.7 %copy-start = (f32[4096]{0:T(1024)S(1)}, f32[4096]{0:T(1024)}, u32[]{:S(2)}) copy-start(f32[4096]{0:T(1024)} %param.7) | copy-start | bytes 49156
  16.9 7.7 %collective-permute-start.8 = (f32[1,46,8,128]{3,2,1,0:T(8,128)S(1)}, f32[1,46,8,128]{3,2,1,0:T(8,128)S(1)}, u32[]{:S(2)}, u32[]{:S(2)}) collective-permute-start(f32[1,46,8,128]{3,2,1,0:T(8,128)S(1)} %merge_0_1.1.own_ref), channel_id=1, source_target_pairs={{0,8},{1,5},{2,10},{3,7},{4,12},{5,1},{6,14},{7,3},{8,0},{9,13},{1... | collective-permute-start | bytes 565256 | tf_op jit(solution)/shard_map/send_0_2/ppermute | solution.py:260
  20.5 8.6 %collective-permute-start.2 = (f32[1,46,8,128]{3,2,1,0:T(8,128)S(1)}, f32[1,46,8,128]{3,2,1,0:T(8,128)S(1)}, u32[]{:S(2)}, u32[]{:S(2)}) collective-permute-start(f32[1,46,8,128]{3,2,1,0:T(8,128)S(1)} %merge_1_1.1.own_ref), channel_id=1, source_target_pairs={{0,16},{1,5},{2,18},{3,7},{4,20},{5,1},{6,22},{7,3},{8,24},{9,13},... | collective-permute-start | bytes 565256 | tf_op jit(solution)/shard_map/send_1_2/ppermute | solution.py:260
  24.7 8.6 %collective-permute-start.9 = (f32[1,46,8,128]{3,2,1,0:T(8,128)S(1)}, f32[1,46,8,128]{3,2,1,0:T(8,128)S(1)}, u32[]{:S(2)}, u32[]{:S(2)}) collective-permute-start(f32[1,46,8,128]{3,2,1,0:T(8,128)S(1)} %merge_0_2.1.own_ref), channel_id=1, source_target_pairs={{0,16},{1,3},{2,18},{3,1},{4,20},{5,7},{6,22},{7,5},{8,24},{9,11},... | collective-permute-start | bytes 565256 | tf_op jit(solution)/shard_map/send_0_3/ppermute | solution.py:260
  29.0 7.5 %collective-permute-start.3 = (f32[1,46,8,128]{3,2,1,0:T(8,128)S(1)}, f32[1,46,8,128]{3,2,1,0:T(8,128)S(1)}, u32[]{:S(2)}, u32[]{:S(2)}) collective-permute-start(f32[1,46,8,128]{3,2,1,0:T(8,128)S(1)} %merge_1_2.1.own_ref), channel_id=1, source_target_pairs={{0,8},{1,3},{2,10},{3,1},{4,12},{5,7},{6,14},{7,5},{8,0},{9,11},{1... | collective-permute-start | bytes 565256 | tf_op jit(solution)/shard_map/send_1_3/ppermute | solution.py:260
  33.4 5.8 %collective-permute-start.10 = (f32[1,30,8,128]{3,2,1,0:T(8,128)S(1)}, f32[1,30,8,128]{3,2,1,0:T(8,128)S(1)}, u32[]{:S(2)}, u32[]{:S(2)}) collective-permute-start(f32[1,30,8,128]{3,2,1,0:T(8,128)S(1)} %merge_0_3.1.own_ref), channel_id=1, source_target_pairs={{0,4},{1,17},{2,6},{3,19},{4,0},{5,21},{6,2},{7,23},{8,12},{9,25},... | collective-permute-start | bytes 368648 | tf_op jit(solution)/shard_map/send_0_4/ppermute | solution.py:260
  36.7 6.8 %collective-permute-start.4 = (f32[1,30,8,128]{3,2,1,0:T(8,128)S(1)}, f32[1,30,8,128]{3,2,1,0:T(8,128)S(1)}, u32[]{:S(2)}, u32[]{:S(2)}) collective-permute-start(f32[1,30,8,128]{3,2,1,0:T(8,128)S(1)} %merge_1_3.1.own_ref), channel_id=1, source_target_pairs={{0,2},{1,17},{2,0},{3,19},{4,6},{5,21},{6,4},{7,23},{8,10},{9,25},... | collective-permute-start | bytes 368648 | tf_op jit(solution)/shard_map/send_1_4/ppermute | solution.py:260
  39.2 8.4 %collective-permute-start.11 = (f32[2,1,30,8,128]{4,3,2,1,0:T(8,128)S(1)}, f32[2,1,30,8,128]{4,3,2,1,0:T(8,128)S(1)}, u32[]{:S(2)}, u32[]{:S(2)}) collective-permute-start(f32[2,1,30,8,128]{4,3,2,1,0:T(8,128)S(1)} %merge_0_4.1.own_ref), channel_id=1, source_target_pairs={{0,2},{1,9},{2,0},{3,11},{4,6},{5,13},{6,4},{7,15},{8,10},{9,1},{1... | collective-permute-start | bytes 737288 | tf_op jit(solution)/shard_map/send_0_5/ppermute | solution.py:260
  43.5 6.3 %collective-permute-start.5 = (f32[2,1,30,8,128]{4,3,2,1,0:T(8,128)S(1)}, f32[2,1,30,8,128]{4,3,2,1,0:T(8,128)S(1)}, u32[]{:S(2)}, u32[]{:S(2)}) collective-permute-start(f32[2,1,30,8,128]{4,3,2,1,0:T(8,128)S(1)} %merge_1_4.1.own_ref), channel_id=1, source_target_pairs={{0,4},{1,9},{2,6},{3,11},{4,0},{5,13},{6,2},{7,15},{8,12},{9,1},{1... | collective-permute-start | bytes 737288 | tf_op jit(solution)/shard_map/send_1_5/ppermute | solution.py:260
  51.8 1.2 %collective-permute-start.12 = (f32[8,128]{1,0:T(8,128)S(1)}, f32[8,128]{1,0:T(8,128)S(1)}, u32[]{:S(2)}, u32[]{:S(2)}) collective-permute-start(f32[8,128]{1,0:T(8,128)S(1)} %get-tuple-element.27), channel_id=1, source_target_pairs={{0,1},{1,0},{2,3},{3,2},{4,5},{5,4},{6,7},{7,6},{8,9},{9,8},{10,11... | collective-permute-start | bytes 12296 | tf_op jit(solution)/shard_map/ppermute | solution.py:304

commit v4 on v3

--- a/solution.py
+++ b/solution.py
@@ -16,7 +16,7 @@
 HALVINGS = 2
 REST = 2 * GROUPS >> HALVINGS
 HOURS, HIGH, LOW, TILES = SLOTS, SLOTS + 1, 2 * SLOTS + 1, 3 * SLOTS + 1
-ORDERS = (((0, 2), (1, 3), (2, 1), (3, 0)), ((1, 2), (0, 3), (3, 1), (2, 0)))
+ORDERS = (((1, 0), (0, 1), (2, 3), (3, 2)), ((0, 2), (1, 3), (3, 1), (2, 0)))
 AXES = ("year", "space")
 PIECES = 4
 
@@ -175,11 +175,18 @@
 
 
 def depart_kernel(chunk, last, day_ref, x_ref, w_ref, recv_ref, own_ref, *refs):
-    if chunk > 0:
-        before_ref, refs = refs[0], refs[2:]
-    out_ref, sums_ref, squares, ready, left = refs
-    tiles, rows = x_ref.shape[0], x_ref.shape[1] // CHUNKS
-    piece = tiles // PIECES
+    earlier, refs = refs[: 2 * chunk], refs[2 * chunk :]
+    out_ref, sums_ref, *refs = refs
+    copies = []
+    if last:
+        whole_ref, squares, left = refs
+        rows = out_ref.shape[1]
+        for c, ref in enumerate(earlier[1::2]):
+            copies.append(pltpu.make_async_copy(ref, whole_ref.at[:, pl.ds(c * rows, rows)], left.at[c]))
+            copies[-1].start()
+    else:
+        (squares,) = refs
+    tiles, rows = out_ref.shape[0], out_ref.shape[1]
     bits = own_bits(chunk)
     flip = day_flip(bits)
     tables = by_group(recv_ref, own_ref)
@@ -193,21 +200,17 @@
             slot, index = place(day_ref[t * SUBLANES + k], flip)
             total = None
             for half, table_ref in enumerate(tables):
-                at = pl.ds(chunk * rows + starts[half] + k, height, stride=SUBLANES)
+                at = starts[half] + k
                 table = table_ref.at[slot]
-                departure = (x_ref[t, at, :] - table[index]) * table[SLOTS + index]
-                ready[t, pl.ds(starts[half] + k, height, stride=SUBLANES), :] = departure
+                x = x_ref[t, pl.ds(chunk * rows + at, height, stride=SUBLANES), :]
+                departure = (x - table[index]) * table[SLOTS + index]
+                out_ref[t, pl.ds(at, height, stride=SUBLANES), :] = departure
                 square = weights[half] * departure * departure
                 total = square if total is None else total + square
             squares[pl.ds(pl.multiple_of((t * SUBLANES + k) * height, height), height), :] = total
         return carry
 
-    copies = []
-    for p in range(PIECES):
-        lax.fori_loop(p * piece, (p + 1) * piece, tile, 0)
-        at = pl.ds(p * piece, piece)
-        copies.append(pltpu.make_async_copy(ready.at[at], out_ref.at[at, pl.ds(chunk * rows, rows)], left.at[p]))
-        copies[-1].start()
+    lax.fori_loop(0, tiles, tile, 0)
     sums = []
     for t in range(tiles):
         start = t * SUBLANES * height
@@ -215,7 +218,7 @@
         for j in range(1, height):
             total += squares[pl.ds(start + j, SUBLANES, stride=height), :]
         at = pl.ds(t * SUBLANES, SUBLANES)
-        if chunk > 0:
+        for before_ref in earlier[::2]:
             total += before_ref[at, :]
         if last:
             sums.append(total)
@@ -230,26 +233,48 @@
         copy.wait()
 
 
-def depart(chunk, day, x, w, recv, own, before, out):
+def depart(chunk, day, x, w, recv, own, earlier):
     tiles, rows = x.shape[0], x.shape[1] // CHUNKS
     steps, last = tiles * SUBLANES, chunk == CHUNKS - 1
-    inputs, specs, aliases = [day, x, w, recv, own], [SMEM] + [VMEM] * 4, {}
-    if chunk > 0:
-        inputs, specs, aliases = inputs + [before, out], specs + [VMEM, HBM], {6: 0}
+    shapes = (vmem(tiles, rows, LANES), vmem(SUBLANES if last else steps, steps if last else LANES))
+    specs, scratch = (VMEM, VMEM), [pltpu.VMEM((rows // 2 * tiles, LANES), jnp.float32)]
+    if last:
+        shapes, specs = shapes + (pltpu.HBM(x.shape, jnp.float32),), specs + (HBM,)
+        scratch.append(pltpu.SemaphoreType.DMA((chunk,)))
+    inputs = [day, x, w, recv, own, *earlier]
     return local_call(
         functools.partial(depart_kernel, chunk, last),
         f"depart_{chunk}",
-        (pltpu.HBM((tiles, rows * CHUNKS, LANES), jnp.float32), vmem(SUBLANES if last else steps, steps if last else LANES)),
+        shapes,
         *inputs,
-        in_specs=specs,
-        out_specs=(HBM, VMEM),
-        scratch_shapes=[
-            pltpu.VMEM((rows // 2 * tiles, LANES), jnp.float32),
-            pltpu.VMEM((tiles, rows, LANES), jnp.float32),
-            pltpu.SemaphoreType.DMA((PIECES,)),
-        ],
-        input_output_aliases=aliases,
-        vmem=4 << 20,
+        in_specs=[SMEM] + [VMEM] * (len(inputs) - 1),
+        out_specs=specs,
+        scratch_shapes=scratch,
+    )
+
+
+def emit_kernel(part_ref, before_ref, out_ref, left):
+    tiles, rows = part_ref.shape[0], part_ref.shape[1]
+    piece, copies = tiles // PIECES, []
+    for p in range(PIECES):
+        at = pl.ds(p * piece, piece)
+        here = out_ref.at[at, pl.ds(out_ref.shape[1] - rows, rows)]
+        copies.append(pltpu.make_async_copy(part_ref.at[at], here, left.at[p]))
+        copies[-1].start()
+    for copy in copies:
+        copy.wait()
+
+
+def emit(part, out):
+    return local_call(
+        emit_kernel,
+        "emit",
+        pltpu.HBM(out.shape, jnp.float32),
+        part, out,
+        in_specs=[VMEM, HBM],
+        out_specs=HBM,
+        scratch_shapes=[pltpu.SemaphoreType.DMA((PIECES,))],
+        input_output_aliases={1: 0},
     )
 
 
@@ -297,9 +322,11 @@
     while not all(results):
         for c in range(CHUNKS):
             results[c] = next(chunks[c])
-    out = sums = None
+    earlier = []
     for c in range(CHUNKS):
-        out, sums = depart(c, yearday_position, x, w, *results[c], sums, out)
+        part, sums, *whole = depart(c, yearday_position, x, w, *results[c], earlier)
+        earlier += [sums, part]
+    out = emit(part, *whole)
     if lax.axis_size("space") == 2:
         sums += lax.ppermute(sums, "space", [(0, 1), (1, 0)])
     else:

time: 54.2 us -> 49.9 us (0.921)
  waiting for transfers between devices: 18.4 us -> 14 us
  starting transfers between devices: 26.1 us -> 26.8 us
    ppermute x12, waiting for transfers between devices: 17.2 us -> 13.9 us  [exchange(): lax.ppermute(pltpu.with_memory_space_constraint(x, pltpu.VMEM), AXES, par...]
    ppermute x1, waiting for transfers between devices: 1.15 us -> 0.15 us  [on_device(): sums += lax.ppermute(sums, 'space', [(0, 1), (1, 0)])]
    ppermute x12, starting transfers between devices: 26 us -> 26.7 us  [exchange(): lax.ppermute(pltpu.with_memory_space_constraint(x, pltpu.VMEM), AXES, par...]
    pallas_call x14 -> x15, Pallas kernels: 7.85 us -> 7.62 us  [local_call(): pl.pallas_call(kernel, in_specs=specs, out_shape=out_shape, name=name, co...]
  transfers between devices with their start and end apart: 13 -> 13, of which waited for: 11 -> 11; matrix products, arithmetic and copies ran while one was open for 0% -> 0% of each run, Pallas kernels for 7% -> 8%
where the time goes in v4:
time: 49.9 us; the launch traced here: 49.7 us
  starting transfers between devices  26.8 us (54%)
  waiting for transfers between devices  14 us (28%)
  Pallas kernels  7.62 us (15%)
  between operations  0.74 us (1%)
  other arithmetic  0.53 us (1%)
    ppermute x12, starting transfers between devices, exchange(): lax.ppermute(pltpu.with_memory_space_constraint(x, pltpu.VMEM), AXES, par...  26.7 us
    ppermute x12, waiting for transfers between devices, exchange(): lax.ppermute(pltpu.with_memory_space_constraint(x, pltpu.VMEM), AXES, par...  13.9 us
    pallas_call x15, Pallas kernels, local_call(): pl.pallas_call(kernel, in_specs=specs, out_shape=out_shape, name=name, co...  7.62 us
  transfers between devices with their start and end apart: 13, of which 11 were waited for; matrix products, arithmetic and copies ran while one was open for 0% of the time, Pallas kernels for 8%

profile of v4, /device:TPU:0, one launch (start us, length us, event | category | flops | bytes accessed | tf_op | source)
XLA Modules:
  0.0 49.7 jit_solution(8757606043665499424)
XLA Ops:
  0.6 1.9 %stats_0.1 = (f32[2,1,46,8,128]{4,3,2,1,0:T(8,128)S(1)}, f32[2,1,46,8,128]{4,3,2,1,0:T(8,128)S(1)}, f32[16,256,128]{2,1,0:T(8,128)S(1)}) custom-call(s32[128]{0:T(128)} %day_ref.3, s32[128]{0:T(128)} %refs_1_.3, f32[16,256,128]{2,1,0:T(8,128)} %bitcast.15), custom_call_target="tpu_custom_call" | custom-call | tf_op jit(solution)/shard_map/stats_0/pallas_call | solution.py:33
  2.6 3.1 %collective-permute-start.6 = (f32[2,1,46,8,128]{4,3,2,1,0:T(8,128)S(1)}, f32[2,1,46,8,128]{4,3,2,1,0:T(8,128)S(1)}, u32[]{:S(2)}, u32[]{:S(2)}) collective-permute-start(f32[2,1,46,8,128]{4,3,2,1,0:T(8,128)S(1)} %get-tuple-element.21), channel_id=1, source_target_pairs={{0,4},{1,3},{2,6},{3,1},{4,0},{5,7},{6,2},{7,5},{8,12},{9,11},{10,... | collective-permute-start | bytes 1130504 | tf_op jit(solution)/shard_map/send_0_0/ppermute | solution.py:285
  5.7 1.4 %stats_1.1 = (f32[2,1,46,8,128]{4,3,2,1,0:T(8,128)S(1)}, f32[2,1,46,8,128]{4,3,2,1,0:T(8,128)S(1)}) custom-call(s32[128]{0:T(128)S(1)} %copy-done.1, s32[128]{0:T(128)S(1)} %copy-done.2, f32[16,256,128]{2,1,0:T(8,128)S(1)} %get-tuple-element.16.refs_2_.x_ref), custom_call_target="tpu_custom_call" | custom-call | tf_op jit(solution)/shard_map/stats_1/pallas_call | solution.py:33
  7.1 1.6 %collective-permute-start = (f32[2,1,46,8,128]{4,3,2,1,0:T(8,128)S(1)}, f32[2,1,46,8,128]{4,3,2,1,0:T(8,128)S(1)}, u32[]{:S(2)}, u32[]{:S(2)}) collective-permute-start(f32[2,1,46,8,128]{4,3,2,1,0:T(8,128)S(1)} %get-tuple-element.17), channel_id=1, source_target_pairs={{0,2},{1,9},{2,0},{3,11},{4,6},{5,13},{6,4},{7,15},{8,10},{9,1},{1... | collective-permute-start | bytes 1130504 | tf_op jit(solution)/shard_map/send_1_0/ppermute | solution.py:285
  8.7 2.6 %collective-permute-done.6.got_ref = f32[2,1,46,8,128]{4,3,2,1,0:T(8,128)S(1)} collective-permute-done((f32[2,1,46,8,128]{4,3,2,1,0:T(8,128)S(1)}, f32[2,1,46,8,128]{4,3,2,1,0:T(8,128)S(1)}, u32[]{:S(2)}, u32[]{:S(2)}) %collective-permute-start.6) | collective-permute-done | bytes 376864 | tf_op jit(solution)/shard_map/send_0_0/ppermute | solution.py:285
  11.3 2.1 %collective-permute-start.7 = (f32[1,46,8,128]{3,2,1,0:T(8,128)S(1)}, f32[1,46,8,128]{3,2,1,0:T(8,128)S(1)}, u32[]{:S(2)}, u32[]{:S(2)}) collective-permute-start(f32[1,46,8,128]{3,2,1,0:T(8,128)S(1)} %get-tuple-element.23), channel_id=1, source_target_pairs={{0,2},{1,5},{2,0},{3,7},{4,6},{5,1},{6,4},{7,3},{8,10},{9,13},{10,... | collective-permute-start | bytes 565256 | tf_op jit(solution)/shard_map/send_0_1/ppermute | solution.py:285
  13.3 1.4 %collective-permute-done.got_ref = f32[2,1,46,8,128]{4,3,2,1,0:T(8,128)S(1)} collective-permute-done((f32[2,1,46,8,128]{4,3,2,1,0:T(8,128)S(1)}, f32[2,1,46,8,128]{4,3,2,1,0:T(8,128)S(1)}, u32[]{:S(2)}, u32[]{:S(2)}) %collective-permute-start) | collective-permute-done | bytes 376864 | tf_op jit(solution)/shard_map/send_1_0/ppermute | solution.py:285
  14.8 1.5 %collective-permute-start.1 = (f32[1,46,8,128]{3,2,1,0:T(8,128)S(1)}, f32[1,46,8,128]{3,2,1,0:T(8,128)S(1)}, u32[]{:S(2)}, u32[]{:S(2)}) collective-permute-start(f32[1,46,8,128]{3,2,1,0:T(8,128)S(1)} %get-tuple-element.19), channel_id=1, source_target_pairs={{0,4},{1,17},{2,6},{3,19},{4,0},{5,21},{6,2},{7,23},{8,12},{9,25},... | collective-permute-start | bytes 565256 | tf_op jit(solution)/shard_map/send_1_1/ppermute | solution.py:285
  16.9 2.1 %collective-permute-start.8 = (f32[1,46,8,128]{3,2,1,0:T(8,128)S(1)}, f32[1,46,8,128]{3,2,1,0:T(8,128)S(1)}, u32[]{:S(2)}, u32[]{:S(2)}) collective-permute-start(f32[1,46,8,128]{3,2,1,0:T(8,128)S(1)} %merge_0_1.1.own_ref), channel_id=1, source_target_pairs={{0,8},{1,17},{2,10},{3,19},{4,12},{5,21},{6,14},{7,23},{8,0},{9,25... | collective-permute-start | bytes 565256 | tf_op jit(solution)/shard_map/send_0_2/ppermute | solution.py:285
  19.1 1.4 %collective-permute-done.1.got_ref = f32[1,46,8,128]{3,2,1,0:T(8,128)S(1)} collective-permute-done((f32[1,46,8,128]{3,2,1,0:T(8,128)S(1)}, f32[1,46,8,128]{3,2,1,0:T(8,128)S(1)}, u32[]{:S(2)}, u32[]{:S(2)}) %collective-permute-start.1) | collective-permute-done | bytes 188448 | tf_op jit(solution)/shard_map/send_1_1/ppermute | solution.py:285
  20.5 2.7 %collective-permute-start.2 = (f32[1,46,8,128]{3,2,1,0:T(8,128)S(1)}, f32[1,46,8,128]{3,2,1,0:T(8,128)S(1)}, u32[]{:S(2)}, u32[]{:S(2)}) collective-permute-start(f32[1,46,8,128]{3,2,1,0:T(8,128)S(1)} %merge_1_1.1.own_ref), channel_id=1, source_target_pairs={{0,16},{1,5},{2,18},{3,7},{4,20},{5,1},{6,22},{7,3},{8,24},{9,13},... | collective-permute-start | bytes 565256 | tf_op jit(solution)/shard_map/send_1_2/ppermute | solution.py:285
  23.2 4.8 %collective-permute-start.9 = (f32[1,46,8,128]{3,2,1,0:T(8,128)S(1)}, f32[1,46,8,128]{3,2,1,0:T(8,128)S(1)}, u32[]{:S(2)}, u32[]{:S(2)}) collective-permute-start(f32[1,46,8,128]{3,2,1,0:T(8,128)S(1)} %merge_0_2.1.own_ref), channel_id=1, source_target_pairs={{0,16},{1,9},{2,18},{3,11},{4,20},{5,13},{6,22},{7,15},{8,24},{9,1... | collective-permute-start | bytes 565256 | tf_op jit(solution)/shard_map/send_0_3/ppermute | solution.py:285
  28.0 1.3 %collective-permute-done.2.got_ref = f32[1,46,8,128]{3,2,1,0:T(8,128)S(1)} collective-permute-done((f32[1,46,8,128]{3,2,1,0:T(8,128)S(1)}, f32[1,46,8,128]{3,2,1,0:T(8,128)S(1)}, u32[]{:S(2)}, u32[]{:S(2)}) %collective-permute-start.2) | collective-permute-done | bytes 188448 | tf_op jit(solution)/shard_map/send_1_2/ppermute | solution.py:285
  29.3 1.3 %collective-permute-start.3 = (f32[1,46,8,128]{3,2,1,0:T(8,128)S(1)}, f32[1,46,8,128]{3,2,1,0:T(8,128)S(1)}, u32[]{:S(2)}, u32[]{:S(2)}) collective-permute-start(f32[1,46,8,128]{3,2,1,0:T(8,128)S(1)} %merge_1_2.1.own_ref), channel_id=1, source_target_pairs={{0,8},{1,3},{2,10},{3,1},{4,12},{5,7},{6,14},{7,5},{8,0},{9,11},{1... | collective-permute-start | bytes 565256 | tf_op jit(solution)/shard_map/send_1_3/ppermute | solution.py:285
  31.6 3.5 %collective-permute-start.10 = (f32[1,30,8,128]{3,2,1,0:T(8,128)S(1)}, f32[1,30,8,128]{3,2,1,0:T(8,128)S(1)}, u32[]{:S(2)}, u32[]{:S(2)}) collective-permute-start(f32[1,30,8,128]{3,2,1,0:T(8,128)S(1)} %merge_0_3.1.own_ref), channel_id=1, source_target_pairs={{0,2},{1,5},{2,0},{3,7},{4,6},{5,1},{6,4},{7,3},{8,10},{9,13},{10,... | collective-permute-start | bytes 368648 | tf_op jit(solution)/shard_map/send_0_4/ppermute | solution.py:285
  35.2 1.7 %collective-permute-start.4 = (f32[1,30,8,128]{3,2,1,0:T(8,128)S(1)}, f32[1,30,8,128]{3,2,1,0:T(8,128)S(1)}, u32[]{:S(2)}, u32[]{:S(2)}) collective-permute-start(f32[1,30,8,128]{3,2,1,0:T(8,128)S(1)} %merge_1_3.1.own_ref), channel_id=1, source_target_pairs={{0,4},{1,17},{2,6},{3,19},{4,0},{5,21},{6,2},{7,23},{8,12},{9,25},... | collective-permute-start | bytes 368648 | tf_op jit(solution)/shard_map/send_1_4/ppermute | solution.py:285
  36.9 1.1 %collective-permute-done.10.got_ref = f32[1,30,8,128]{3,2,1,0:T(8,128)S(1)} collective-permute-done((f32[1,30,8,128]{3,2,1,0:T(8,128)S(1)}, f32[1,30,8,128]{3,2,1,0:T(8,128)S(1)}, u32[]{:S(2)}, u32[]{:S(2)}) %collective-permute-start.10) | collective-permute-done | bytes 122912 | tf_op jit(solution)/shard_map/send_0_4/ppermute | solution.py:285
  38.0 1.1 %collective-permute-start.11 = (f32[2,1,30,8,128]{4,3,2,1,0:T(8,128)S(1)}, f32[2,1,30,8,128]{4,3,2,1,0:T(8,128)S(1)}, u32[]{:S(2)}, u32[]{:S(2)}) collective-permute-start(f32[2,1,30,8,128]{4,3,2,1,0:T(8,128)S(1)} %merge_0_4.1.own_ref), channel_id=1, source_target_pairs={{0,4},{1,3},{2,6},{3,1},{4,0},{5,7},{6,2},{7,5},{8,12},{9,11},{10,... | collective-permute-start | bytes 737288 | tf_op jit(solution)/shard_map/send_0_5/ppermute | solution.py:285
  39.1 1.0 %collective-permute-done.4.got_ref = f32[1,30,8,128]{3,2,1,0:T(8,128)S(1)} collective-permute-done((f32[1,30,8,128]{3,2,1,0:T(8,128)S(1)}, f32[1,30,8,128]{3,2,1,0:T(8,128)S(1)}, u32[]{:S(2)}, u32[]{:S(2)}) %collective-permute-start.4) | collective-permute-done | bytes 122912 | tf_op jit(solution)/shard_map/send_1_4/ppermute | solution.py:285
  40.2 1.4 %collective-permute-start.5 = (f32[2,1,30,8,128]{4,3,2,1,0:T(8,128)S(1)}, f32[2,1,30,8,128]{4,3,2,1,0:T(8,128)S(1)}, u32[]{:S(2)}, u32[]{:S(2)}) collective-permute-start(f32[2,1,30,8,128]{4,3,2,1,0:T(8,128)S(1)} %merge_1_4.1.own_ref), channel_id=1, source_target_pairs={{0,2},{1,9},{2,0},{3,11},{4,6},{5,13},{6,4},{7,15},{8,10},{9,1},{1... | collective-permute-start | bytes 737288 | tf_op jit(solution)/shard_map/send_1_5/ppermute | solution.py:285
  41.6 2.6 %collective-permute-done.11.recv_ref = f32[2,1,30,8,128]{4,3,2,1,0:T(8,128)S(1)} collective-permute-done((f32[2,1,30,8,128]{4,3,2,1,0:T(8,128)S(1)}, f32[2,1,30,8,128]{4,3,2,1,0:T(8,128)S(1)}, u32[]{:S(2)}, u32[]{:S(2)}) %collective-permute-start.11) | collective-permute-done | bytes 245792 | tf_op jit(solution)/shard_map/send_0_5/ppermute | solution.py:285
  44.3 1.4 %depart_0.1 = (f32[16,128,128]{2,1,0:T(8,128)S(1)}, f32[128,128]{1,0:T(8,128)S(1)}) custom-call(s32[128]{0:T(128)S(1)} %copy-done.1, f32[16,256,128]{2,1,0:T(8,128)S(1)} %get-tuple-element.16.refs_2_.x_ref, f32[32,128]{1,0:T(8,128)S(1)} %bitcast.13, f32[2,1,30,8,128]{4,3,2,1,0:T(8,128)S(1)} %collective-permute-done.11.recv_ref, ...), custom_call_target="tpu_custom_call" | custom-call | tf_op jit(solution)/shard_map/depart_0/pallas_call | solution.py:33
  46.5 1.5 %depart_1.1 = (f32[16,128,128]{2,1,0:T(8,128)S(1)}, f32[8,128]{1,0:T(8,128)S(1)}, f32[16,256,128]{2,1,0:T(8,128)}) custom-call(s32[128]{0:T(128)S(1)} %copy-done.1, f32[16,256,128]{2,1,0:T(8,128)S(1)} %get-tuple-element.16.refs_2_.x_ref, f32[32,128]{1,0:T(8,128)S(1)} %bitcast.14, f32[2,1,30,8,128]{4,3,2,1,0:T(8,128)S(1)} %collective-permute-done.5.recv_ref, ...), custom_call_target="tpu_custom_call" | custom-call | tf_op jit(solution)/shard_map/depart_1/pallas_call | solution.py:33
  48.1 1.0 %emit.1 = f32[16,256,128]{2,1,0:T(8,128)} custom-call(f32[16,128,128]{2,1,0:T(8,128)S(1)} %get-tuple-element.27.part_ref, f32[16,256,128]{2,1,0:T(8,128)} %get-tuple-element.28.before_ref), custom_call_target="tpu_custom_call", output_to_operand_aliasing={{}: (1, {})} | custom-call | tf_op jit(solution)/shard_map/emit/pallas_call | solution.py:33
  (25 shorter events, 3.6 us)
Async XLA Ops:
  0.6 5.0 %copy-start.1 = (s32[128]{0:T(128)S(1)}, s32[128]{0:T(128)}, u32[]{:S(2)}) copy-start(s32[128]{0:T(128)} %day_ref.3) | copy-start | bytes 1540
  0.6 5.0 %copy-start.2 = (s32[128]{0:T(128)S(1)}, s32[128]{0:T(128)}, u32[]{:S(2)}) copy-start(s32[128]{0:T(128)} %refs_1_.3) | copy-start | bytes 1540
  2.6 8.6 %collective-permute-start.6 = (f32[2,1,46,8,128]{4,3,2,1,0:T(8,128)S(1)}, f32[2,1,46,8,128]{4,3,2,1,0:T(8,128)S(1)}, u32[]{:S(2)}, u32[]{:S(2)}) collective-permute-start(f32[2,1,46,8,128]{4,3,2,1,0:T(8,128)S(1)} %get-tuple-element.21), channel_id=1, source_target_pairs={{0,4},{1,3},{2,6},{3,1},{4,0},{5,7},{6,2},{7,5},{8,12},{9,11},{10,... | collective-permute-start | bytes 1130504 | tf_op jit(solution)/shard_map/send_0_0/ppermute | solution.py:285
  7.1 7.7 %collective-permute-start = (f32[2,1,46,8,128]{4,3,2,1,0:T(8,128)S(1)}, f32[2,1,46,8,128]{4,3,2,1,0:T(8,128)S(1)}, u32[]{:S(2)}, u32[]{:S(2)}) collective-permute-start(f32[2,1,46,8,128]{4,3,2,1,0:T(8,128)S(1)} %get-tuple-element.17), channel_id=1, source_target_pairs={{0,2},{1,9},{2,0},{3,11},{4,6},{5,13},{6,4},{7,15},{8,10},{9,1},{1... | collective-permute-start | bytes 1130504 | tf_op jit(solution)/shard_map/send_1_0/ppermute | solution.py:285
  11.3 5.6 %collective-permute-start.7 = (f32[1,46,8,128]{3,2,1,0:T(8,128)S(1)}, f32[1,46,8,128]{3,2,1,0:T(8,128)S(1)}, u32[]{:S(2)}, u32[]{:S(2)}) collective-permute-start(f32[1,46,8,128]{3,2,1,0:T(8,128)S(1)} %get-tuple-element.23), channel_id=1, source_target_pairs={{0,2},{1,5},{2,0},{3,7},{4,6},{5,1},{6,4},{7,3},{8,10},{9,13},{10,... | collective-permute-start | bytes 565256 | tf_op jit(solution)/shard_map/send_0_1/ppermute | solution.py:285
  14.8 5.6 %collective-permute-start.1 = (f32[1,46,8,128]{3,2,1,0:T(8,128)S(1)}, f32[1,46,8,128]{3,2,1,0:T(8,128)S(1)}, u32[]{:S(2)}, u32[]{:S(2)}) collective-permute-start(f32[1,46,8,128]{3,2,1,0:T(8,128)S(1)} %get-tuple-element.19), channel_id=1, source_target_pairs={{0,4},{1,17},{2,6},{3,19},{4,0},{5,21},{6,2},{7,23},{8,12},{9,25},... | collective-permute-start | bytes 565256 | tf_op jit(solution)/shard_map/send_1_1/ppermute | solution.py:285
  16.9 27.4 %copy-start = (f32[4096]{0:T(1024)S(1)}, f32[4096]{0:T(1024)}, u32[]{:S(2)}) copy-start(f32[4096]{0:T(1024)} %param.7) | copy-start | bytes 49156
  16.9 6.2 %collective-permute-start.8 = (f32[1,46,8,128]{3,2,1,0:T(8,128)S(1)}, f32[1,46,8,128]{3,2,1,0:T(8,128)S(1)}, u32[]{:S(2)}, u32[]{:S(2)}) collective-permute-start(f32[1,46,8,128]{3,2,1,0:T(8,128)S(1)} %merge_0_1.1.own_ref), channel_id=1, source_target_pairs={{0,8},{1,17},{2,10},{3,19},{4,12},{5,21},{6,14},{7,23},{8,0},{9,25... | collective-permute-start | bytes 565256 | tf_op jit(solution)/shard_map/send_0_2/ppermute | solution.py:285
  20.5 8.8 %collective-permute-start.2 = (f32[1,46,8,128]{3,2,1,0:T(8,128)S(1)}, f32[1,46,8,128]{3,2,1,0:T(8,128)S(1)}, u32[]{:S(2)}, u32[]{:S(2)}) collective-permute-start(f32[1,46,8,128]{3,2,1,0:T(8,128)S(1)} %merge_1_1.1.own_ref), channel_id=1, source_target_pairs={{0,16},{1,5},{2,18},{3,7},{4,20},{5,1},{6,22},{7,3},{8,24},{9,13},... | collective-permute-start | bytes 565256 | tf_op jit(solution)/shard_map/send_1_2/ppermute | solution.py:285
  23.2 8.4 %collective-permute-start.9 = (f32[1,46,8,128]{3,2,1,0:T(8,128)S(1)}, f32[1,46,8,128]{3,2,1,0:T(8,128)S(1)}, u32[]{:S(2)}, u32[]{:S(2)}) collective-permute-start(f32[1,46,8,128]{3,2,1,0:T(8,128)S(1)} %merge_0_2.1.own_ref), channel_id=1, source_target_pairs={{0,16},{1,9},{2,18},{3,11},{4,20},{5,13},{6,22},{7,15},{8,24},{9,1... | collective-permute-start | bytes 565256 | tf_op jit(solution)/shard_map/send_0_3/ppermute | solution.py:285
  29.3 5.9 %collective-permute-start.3 = (f32[1,46,8,128]{3,2,1,0:T(8,128)S(1)}, f32[1,46,8,128]{3,2,1,0:T(8,128)S(1)}, u32[]{:S(2)}, u32[]{:S(2)}) collective-permute-start(f32[1,46,8,128]{3,2,1,0:T(8,128)S(1)} %merge_1_2.1.own_ref), channel_id=1, source_target_pairs={{0,8},{1,3},{2,10},{3,1},{4,12},{5,7},{6,14},{7,5},{8,0},{9,11},{1... | collective-permute-start | bytes 565256 | tf_op jit(solution)/shard_map/send_1_3/ppermute | solution.py:285
  31.6 6.4 %collective-permute-start.10 = (f32[1,30,8,128]{3,2,1,0:T(8,128)S(1)}, f32[1,30,8,128]{3,2,1,0:T(8,128)S(1)}, u32[]{:S(2)}, u32[]{:S(2)}) collective-permute-start(f32[1,30,8,128]{3,2,1,0:T(8,128)S(1)} %merge_0_3.1.own_ref), channel_id=1, source_target_pairs={{0,2},{1,5},{2,0},{3,7},{4,6},{5,1},{6,4},{7,3},{8,10},{9,13},{10,... | collective-permute-start | bytes 368648 | tf_op jit(solution)/shard_map/send_0_4/ppermute | solution.py:285
  35.2 4.9 %collective-permute-start.4 = (f32[1,30,8,128]{3,2,1,0:T(8,128)S(1)}, f32[1,30,8,128]{3,2,1,0:T(8,128)S(1)}, u32[]{:S(2)}, u32[]{:S(2)}) collective-permute-start(f32[1,30,8,128]{3,2,1,0:T(8,128)S(1)} %merge_1_3.1.own_ref), channel_id=1, source_target_pairs={{0,4},{1,17},{2,6},{3,19},{4,0},{5,21},{6,2},{7,23},{8,12},{9,25},... | collective-permute-start | bytes 368648 | tf_op jit(solution)/shard_map/send_1_4/ppermute | solution.py:285
  38.0 6.3 %collective-permute-start.11 = (f32[2,1,30,8,128]{4,3,2,1,0:T(8,128)S(1)}, f32[2,1,30,8,128]{4,3,2,1,0:T(8,128)S(1)}, u32[]{:S(2)}, u32[]{:S(2)}) collective-permute-start(f32[2,1,30,8,128]{4,3,2,1,0:T(8,128)S(1)} %merge_0_4.1.own_ref), channel_id=1, source_target_pairs={{0,4},{1,3},{2,6},{3,1},{4,0},{5,7},{6,2},{7,5},{8,12},{9,11},{10,... | collective-permute-start | bytes 737288 | tf_op jit(solution)/shard_map/send_0_5/ppermute | solution.py:285
  40.2 6.3 %collective-permute-start.5 = (f32[2,1,30,8,128]{4,3,2,1,0:T(8,128)S(1)}, f32[2,1,30,8,128]{4,3,2,1,0:T(8,128)S(1)}, u32[]{:S(2)}, u32[]{:S(2)}) collective-permute-start(f32[2,1,30,8,128]{4,3,2,1,0:T(8,128)S(1)} %merge_1_4.1.own_ref), channel_id=1, source_target_pairs={{0,2},{1,9},{2,0},{3,11},{4,6},{5,13},{6,4},{7,15},{8,10},{9,1},{1... | collective-permute-start | bytes 737288 | tf_op jit(solution)/shard_map/send_1_5/ppermute | solution.py:285
  48.0 1.2 %collective-permute-start.12 = (f32[8,128]{1,0:T(8,128)S(1)}, f32[8,128]{1,0:T(8,128)S(1)}, u32[]{:S(2)}, u32[]{:S(2)}) collective-permute-start(f32[8,128]{1,0:T(8,128)S(1)} %get-tuple-element.29), channel_id=1, source_target_pairs={{0,1},{1,0},{2,3},{3,2},{4,5},{5,4},{6,7},{7,6},{8,9},{9,8},{10,11... | collective-permute-start | bytes 12296 | tf_op jit(solution)/shard_map/ppermute | solution.py:331

commit v5 on v0

v5 whole, which is shorter than its diff:
```python
import functools
import math

import jax
import jax.numpy as jnp
from jax import lax
from jax.experimental import pallas as pl
from jax.experimental.pallas import tpu as pltpu
from jax.sharding import PartitionSpec as P

DAYS = 30
SUBLANES, LANES = 8, 128
CHUNKS = 3
SLOTS = -(-DAYS // CHUNKS)
BLOCKS = 4
HALVINGS = 2
HOURS, HIGH, LOW, TILES = SLOTS, SLOTS + 1, 2 * SLOTS + 1, 3 * SLOTS + 1
ORDERS = (((2, 1), (0, 3), (1, 0), (3, 2)), ((0, 1), (1, 3), (3, 2), (2, 0)), ((0, 1), (1, 3), (3, 2), (2, 0)))
AXES = ("year", "space")
PIECES = 4

VMEM = pl.BlockSpec(memory_space=pltpu.VMEM)
SMEM = pl.BlockSpec(memory_space=pltpu.SMEM)
HBM = pl.BlockSpec(memory_space=pltpu.HBM)


def local_call(kernel, name, out_shape, *inputs, **options):
    specs = options.pop("in_specs", [VMEM] * len(inputs))
    spaces = {id(VMEM): pltpu.VMEM, id(HBM): pltpu.HBM}
    inputs = [pltpu.with_memory_space_constraint(a, spaces[id(s)]) if id(s) in spaces else a for a, s in zip(inputs, specs)]
    limit = pltpu.CompilerParams(vmem_limit_bytes=options.pop("vmem", 1 << 20))
    return pl.pallas_call(kernel, in_specs=specs, out_shape=out_shape, name=name, compiler_params=limit, **options)(*inputs)


def vmem(*shape):
    return pltpu.VMEM(shape, jnp.float32)


def stage_bits(chunk, years):
    assert BLOCKS == 1 << HALVINGS and SLOTS <= 2 * SUBLANES
    count = years.bit_length() - 1
    assert years == 1 << count and count > HALVINGS
    return [tuple(1 << b for b in pair) for pair in ORDERS[chunk]] + [(1 << b, 1 << b) for b in range(4, count)]


def block_of(chunk):
    year, core = lax.axis_index("year"), lax.rem(lax.axis_index("space"), 2)
    pairs = stage_bits(chunk, lax.axis_size("year"))[:HALVINGS]
    high, low = [jnp.where(core == 0, year // a % 2, year // b % 2) for a, b in pairs]
    return [[2 * p + r for r in (1 - low, low)] for p in (1 - high, high)]


def place(day):
    chunk = sum((day >= c * SLOTS).astype(jnp.int32) for c in range(1, CHUNKS))
    return chunk, day - chunk * SLOTS


def stats_kernel(day_in, tally_in, x_in, *refs):
    outs, (x_ref, day_ref, tally_ref, hours, totals, arrived, listed) = refs[: 2 * CHUNKS], refs[2 * CHUNKS :]
    tiles, rows = x_in.shape[0], x_in.shape[1] // BLOCKS
    piece = tiles // PIECES
    height = rows // SUBLANES
    lists = [pltpu.make_async_copy(day_in, day_ref, listed.at[0]), pltpu.make_async_copy(tally_in, tally_ref, listed.at[1])]
    copies = []
    for p in range(PIECES):
        at = pl.ds(p * piece, piece)
        copies.append(pltpu.make_async_copy(x_in.at[at], x_ref.at[at], arrived.at[p]))
    for copy in lists + copies:
        copy.start()
    for i in range(CHUNKS * BLOCKS):
        at = i * TILES
        totals[at : at + HIGH] = jnp.zeros((HIGH, height, LANES), jnp.float32)
        totals[at + HIGH : at + LOW] = jnp.full((SLOTS, height, LANES), -jnp.inf, jnp.float32)
        totals[at + LOW : at + TILES] = jnp.full((SLOTS, height, LANES), jnp.inf, jnp.float32)
    for d in range(CHUNKS * SLOTS):
        hours[d] = 0
    for copy in lists:
        copy.wait()

    def tile(t, carry):
        for k in range(SUBLANES):
            step = t * SUBLANES + k
            day, tally = day_ref[step], tally_ref[step]
            chunk, index = place(day)
            base = chunk * (BLOCKS * TILES) + index
            hours[day] += tally
            tally = tally.astype(jnp.float32)
            x = [x_ref[t, pl.ds(b * rows + k, height, stride=SUBLANES), :] for b in range(BLOCKS)]
            at = [[base + b * TILES + kind for kind in (0, HIGH, LOW)] for b in range(BLOCKS)]
            old = [[totals[i] for i in a] for a in at]
            new = [[o[0] + tally * v, jnp.maximum(o[1], v), jnp.minimum(o[2], v)] for o, v in zip(old, x)]
            for a, n in zip(at, new):
                for i, v in zip(a, n):
                    totals[i] = v
        return carry

    for p in range(PIECES):
        copies[p].wait()
        lax.fori_loop(p * piece, (p + 1) * piece, tile, 0)
    left = lax.broadcasted_iota(jnp.int32, (1, LANES), 1) < LANES // 2
    for c in range(CHUNKS):
        blocks = block_of(c)
        pairs = []
        for k in range(SUBLANES):
            pairs.append([hours[c * SLOTS + min(i, SLOTS - 1)].astype(jnp.float32) for i in (k, k + SUBLANES)])
        for half in range(2):
            for slot in range(2):
                out, start = outs[2 * c + half].at[slot], (c * BLOCKS + blocks[half][slot]) * TILES
                out[...] = totals[pl.ds(start, TILES)]
                for k, pair in enumerate(pairs):
                    out[HOURS, k : k + 1, :] = jnp.where(left, *pair)


def stats(day, tally, x):
    tiles, rows = x.shape[0], x.shape[1] // BLOCKS
    height = rows // SUBLANES
    shapes = (vmem(2, TILES, height, LANES),) * (2 * CHUNKS) + (vmem(*x.shape),)
    return local_call(
        stats_kernel,
        "stats",
        shapes,
        day, tally, x,
        in_specs=[HBM] * 3,
        out_specs=(VMEM,) * len(shapes),
        scratch_shapes=[
            pltpu.SMEM(day.shape, jnp.int32),
            pltpu.SMEM(day.shape, jnp.int32),
            pltpu.SMEM((CHUNKS * SLOTS,), jnp.int32),
            vmem(CHUNKS * BLOCKS * TILES, height, LANES),
            pltpu.SemaphoreType.DMA((PIECES,)),
            pltpu.SemaphoreType.DMA((2,)),
        ],
        vmem=8 << 20,
    )


def merge_kernel(got_ref, own_ref, *outs):
    for a, b, join in ((0, HIGH, jnp.add), (HIGH, LOW, jnp.maximum), (LOW, TILES, jnp.minimum)):
        for i, out in enumerate(outs):
            got, own = (got_ref.at[i], own_ref.at[i]) if len(outs) > 1 else (got_ref, own_ref)
            out[a:b] = join(got[a:b], own[a:b])


def table_kernel(got, own, table):
    hours = got[HOURS] + own[HOURS]
    left = lax.broadcasted_iota(jnp.int32, hours.shape, 1) < LANES // 2
    other = pltpu.roll(hours, LANES // 2, axis=1)
    hours = jnp.concatenate([jnp.where(left, hours, other), jnp.where(left, other, hours)])
    for i in range(SLOTS):
        total = got[i] + own[i]
        table[i] = total / jnp.broadcast_to(hours[i : i + 1], total.shape)
        high = jnp.maximum(got[HIGH + i], own[HIGH + i])
        low = jnp.minimum(got[LOW + i], own[LOW + i])
        table[SLOTS + i] = 4.0 / (high - low + 1.0)


def join_kernel(got_ref, own_ref, out_ref):
    out_ref[0] = got_ref[...]
    out_ref[1] = own_ref[...]


def depart_kernel(day_ref, x_ref, w_ref, *refs):
    tables, (last_ref, sums_ref, whole_ref, table, ready, squares, left) = refs[: 2 * CHUNKS], refs[2 * CHUNKS :]
    tiles, rows = x_ref.shape[0], x_ref.shape[1] // BLOCKS
    piece = tiles // PIECES
    height = rows // SUBLANES
    for c in range(CHUNKS):
        blocks = block_of(c)
        for half in range(2):
            for slot in range(2):
                start = (c * BLOCKS + blocks[half][slot]) * 2 * SLOTS
                table[pl.ds(start, 2 * SLOTS)] = tables[2 * c + half][slot]
    weights = [w_ref[b * height : (b + 1) * height, :] for b in range(BLOCKS)]

    def tile(first, out_ref, t, carry):
        for k in range(SUBLANES):
            chunk, index = place(day_ref[t * SUBLANES + k])
            base = chunk * (BLOCKS * 2 * SLOTS) + index
            total = None
            for b in range(BLOCKS):
                at = pl.ds(b * rows + k, height, stride=SUBLANES)
                mean, scale = table[base + b * 2 * SLOTS], table[base + (b * 2 + 1) * SLOTS]
                departure = (x_ref[t, at, :] - mean) * scale
                out_ref[t - first, at, :] = departure
                square = weights[b] * departure * departure
                total = square if total is None else total + square
            squares[pl.ds(pl.multiple_of((t * SUBLANES + k) * height, height), height), :] = total
        return carry

    copies = []
    for p in range(PIECES):
        first, final = p * piece, p == PIECES - 1
        out = last_ref if final else ready
        lax.fori_loop(first, first + piece, functools.partial(tile, first if final else 0, out), 0)
        if not final:
            at = pl.ds(first, piece)
            copies.append(pltpu.make_async_copy(ready.at[at], whole_ref.at[at], left.at[p]))
            copies[-1].start()
    sums = []
    for t in range(tiles):
        start = t * SUBLANES * height
        total = squares[pl.ds(start, SUBLANES, stride=height), :]
        for j in range(1, height):
            total += squares[pl.ds(start + j, SUBLANES, stride=height), :]
        sums.append(total)
    by_step = jnp.sum(jnp.concatenate(sums).T, axis=0, keepdims=True)
    sums_ref[0:1, :] = by_step
    sums_ref[1:2, :] = jnp.full(by_step.shape, jnp.sum(w_ref[...]), jnp.float32)
    sums_ref[2:, :] = jnp.zeros((SUBLANES - 2, by_step.shape[1]), jnp.float32)
    for copy in copies:
        copy.wait()


def depart(day, x, w, tables):
    tiles, rows = x.shape[0], x.shape[1] // BLOCKS
    height, piece, steps = rows // SUBLANES, tiles // PIECES, tiles * SUBLANES
    inputs = [day, x, w, *tables]
    return local_call(
        depart_kernel,
        "depart",
        (vmem(piece, *x.shape[1:]), vmem(SUBLANES, steps), pltpu.HBM(x.shape, jnp.float32)),
        *inputs,
        in_specs=[SMEM] + [VMEM] * (len(inputs) - 1),
        out_specs=(VMEM, VMEM, HBM),
        scratch_shapes=[
            vmem(CHUNKS * BLOCKS * 2 * SLOTS, height, LANES),
            vmem(tiles - piece, *x.shape[1:]),
            vmem(steps * height, LANES),
            pltpu.SemaphoreType.DMA((PIECES - 1,)),
        ],
        vmem=8 << 20,
    )


def emit_kernel(part_ref, before_ref, out_ref, left):
    piece, tiles = part_ref.shape[0], out_ref.shape[0]
    copies = []
    for i in range(piece):
        copies.append(pltpu.make_async_copy(part_ref.at[i], out_ref.at[tiles - piece + i], left.at[i]))
        copies[-1].start()
    for copy in copies:
        copy.wait()


def emit(part, out):
    return local_call(
        emit_kernel,
        "emit",
        pltpu.HBM(out.shape, jnp.float32),
        part, out,
        in_specs=[VMEM, HBM],
        out_specs=HBM,
        scratch_shapes=[pltpu.SemaphoreType.DMA((part.shape[0],))],
        input_output_aliases={1: 0},
    )


def exchange(x, pair, name):
    years, spaces = lax.axis_size("year"), lax.axis_size("space")
    partners = [(y * spaces + s, (y ^ pair[s % 2]) * spaces + s) for y in range(years) for s in range(spaces)]
    with jax.named_scope(name):
        return lax.ppermute(pltpu.with_memory_space_constraint(x, pltpu.VMEM), AXES, partners)


def day_tables(chunk, send, keep):
    pairs = stage_bits(chunk, lax.axis_size("year"))
    for stage, pair in enumerate(pairs):
        got = exchange(send if stage < HALVINGS else keep, pair, f"send_{chunk}_{stage}")
        yield
        name = f"merge_{chunk}_{stage}"
        if stage < HALVINGS - 1:
            half = vmem(*got.shape[1:])
            send, keep = local_call(merge_kernel, name, (half, half), got, keep, out_specs=(VMEM, VMEM))
        elif stage < len(pairs) - 1:
            keep = local_call(merge_kernel, name, vmem(*got.shape), got, keep, out_specs=VMEM)
    table = local_call(table_kernel, name, vmem(2 * SLOTS, *got.shape[1:]), got, keep, out_specs=VMEM)
    for stage in reversed(range(HALVINGS)):
        number = len(pairs) + HALVINGS - 1 - stage
        got = exchange(table, pairs[stage], f"send_{chunk}_{number}")
        yield
        if stage > 0:
            table = local_call(join_kernel, f"merge_{chunk}_{number}", vmem(2, *got.shape), got, table, out_specs=VMEM)
    yield got, table


def on_device(thermal_reading, yearday_position, usable_observation_tally, location_surface_factor):
    steps, cells = thermal_reading.shape
    tiles, columns = steps // SUBLANES, cells // LANES
    x = thermal_reading.reshape(tiles, SUBLANES, columns, LANES).transpose(0, 2, 1, 3)
    x = x.reshape(tiles, columns * SUBLANES, LANES)
    w = location_surface_factor.reshape(columns, LANES)
    *halves, x = stats(yearday_position, usable_observation_tally, x)
    chunks = [day_tables(c, *halves[2 * c : 2 * c + 2]) for c in range(CHUNKS)]
    results = [None] * CHUNKS
    while not all(results):
        for c in range(CHUNKS):
            results[c] = next(chunks[c])
    part, sums, out = depart(yearday_position, x, w, [table for pair in results for table in pair])
    out = emit(part, out)
    if lax.axis_size("space") == 2:
        sums += lax.ppermute(sums, "space", [(0, 1), (1, 0)])
    else:
        sums = lax.psum(sums, "space")
    out = out.reshape(tiles, columns, SUBLANES, LANES).transpose(0, 2, 1, 3).reshape(steps, cells)
    return out, sums[0] / sums[1]


def solution(mesh):
    return jax.shard_map(
        on_device,
        mesh=mesh,
        in_specs=(P("year", "space"), P("year"), P("year"), P("space")),
        out_specs=(P("year", "space"), P("year")),
        check_vma=False,
    )
```

time: 186 us -> 48.4 us (0.26)
  blocking collectives: 105 us -> 0 us
  other arithmetic: 39.1 us -> 0.53 us
  local copies, waits for them, and re-layouts: 29.1 us -> 0.01 us
  starting transfers between devices: 8.52 us -> 27 us
  waiting for transfers between devices: 0.01 us -> 14 us
  Pallas kernels: 0 us -> 5.97 us
  matrix products: 3.02 us -> 0 us
    psum x2 -> x0, blocking collectives: 61 us -> none  [the longest x1 57.9 us: on_device(): hour_total = lax.psum(hour_local, 'year')]
    all_gather x1 -> x0, blocking collectives: 44 us -> none  [on_device(): gathered = lax.all_gather(shares, 'year', axis=2, tiled=True)]
    ppermute x0 -> x19, starting transfers between devices: none -> 27 us  [the longest x18 26.9 us: exchange(): lax.ppermute(pltpu.with_memory_space_constraint(x, pltpu.VMEM), AXES, par...]
    unnamed x9 -> x4, local copies, waits for them, and re-layouts: 20.2 us -> 0.01 us
    reduce_max x1 -> x0, other arithmetic: 14.5 us -> none  [on_device(): jnp.max(jnp.where(picked_elements, thermal_reading[None], -jnp.inf), axis=1)]
    ppermute x0 -> x19, waiting for transfers between devices: none -> 14 us  [the longest x18 13.7 us: exchange(): lax.ppermute(pltpu.with_memory_space_constraint(x, pltpu.VMEM), AXES, par...]
    reduce_sum x4 -> x0, other arithmetic: 14 us -> none  [the longest x1 11.5 us: on_device(): share_sum = jnp.sum(received[:, 0], axis=0)]
    all_to_all x1 -> x0, starting transfers between devices: 8.52 us -> none  [on_device(): lax.all_to_all(stacked, 'year', split_axis=2, concat_axis=0, tiled=True)]
  transfers between devices with their start and end apart: 1 -> 19, of which waited for: 0 -> 12; matrix products, arithmetic and copies ran while one was open for 0% -> 0% of each run, Pallas kernels for 0% -> 3%
where the time goes in v5:
time: 48.4 us; the launch traced here: 48.2 us
  starting transfers between devices  27 us (56%)
  waiting for transfers between devices  14 us (29%)
  Pallas kernels  5.97 us (12%)
  between operations  0.72 us (1%)
  other arithmetic  0.53 us (1%)
    ppermute x18, starting transfers between devices, exchange(): lax.ppermute(pltpu.with_memory_space_constraint(x, pltpu.VMEM), AXES, par...  26.9 us
    ppermute x18, waiting for transfers between devices, exchange(): lax.ppermute(pltpu.with_memory_space_constraint(x, pltpu.VMEM), AXES, par...  13.7 us
    pallas_call x18, Pallas kernels, local_call(): pl.pallas_call(kernel, in_specs=specs, out_shape=out_shape, name=name, co...  5.97 us
  transfers between devices with their start and end apart: 19, of which 12 were waited for; matrix products, arithmetic and copies ran while one was open for 0% of the time, Pallas kernels for 3%

profile of v5, /device:TPU:0, one launch (start us, length us, event | category | flops | bytes accessed | tf_op | source)
XLA Modules:
  0.0 48.2 jit_solution(17383481457238721840)
XLA Ops:
  0.6 2.4 %stats.1 = (f32[2,31,8,128]{3,2,1,0:T(8,128)S(1)}, f32[2,31,8,128]{3,2,1,0:T(8,128)S(1)}, f32[2,31,8,128]{3,2,1,0:T(8,128)S(1)}, f32[2,31,8,128]{3,2,1,0:T(8,128...) custom-call(s32[128]{0:T(128)} %day_ref.1, s32[128]{0:T(128)} %tally_in.1, ...), custom_call_target="tpu_custom_call" | custom-call | tf_op jit(solution)/shard_map/stats/pallas_call | solution.py:32
  3.0 3.1 %collective-permute-start = (f32[2,31,8,128]{3,2,1,0:T(8,128)S(1)}, f32[2,31,8,128]{3,2,1,0:T(8,128)S(1)}, u32[]{:S(2)}, u32[]{:S(2)}) collective-permute-start(f32[2,31,8,128]{3,2,1,0:T(8,128)S(1)} %get-tuple-element.19), channel_id=1, source_target_pairs={{0,8},{1,5},{2,10},{3,7},{4,12},{5,1},{6,14},{7,3},{8,0},{9,13},{1... | collective-permute-start | bytes 761864 | tf_op jit(solution)/shard_map/send_0_0/ppermute | solution.py:262
  6.1 1.5 %collective-permute-start.6 = (f32[2,31,8,128]{3,2,1,0:T(8,128)S(1)}, f32[2,31,8,128]{3,2,1,0:T(8,128)S(1)}, u32[]{:S(2)}, u32[]{:S(2)}) collective-permute-start(f32[2,31,8,128]{3,2,1,0:T(8,128)S(1)} %get-tuple-element.23), channel_id=1, source_target_pairs={{0,2},{1,5},{2,0},{3,7},{4,6},{5,1},{6,4},{7,3},{8,10},{9,13},{10,... | collective-permute-start | bytes 761864 | tf_op jit(solution)/shard_map/send_1_0/ppermute | solution.py:262
  8.1 2.2 %collective-permute-done.got_ref = f32[2,31,8,128]{3,2,1,0:T(8,128)S(1)} collective-permute-done((f32[2,31,8,128]{3,2,1,0:T(8,128)S(1)}, f32[2,31,8,128]{3,2,1,0:T(8,128)S(1)}, u32[]{:S(2)}, u32[]{:S(2)}) %collective-permute-start) | collective-permute-done | bytes 253984 | tf_op jit(solution)/shard_map/send_0_0/ppermute | solution.py:262
  10.4 2.0 %collective-permute-start.1 = (f32[31,8,128]{2,1,0:T(8,128)S(1)}, f32[31,8,128]{2,1,0:T(8,128)S(1)}, u32[]{:S(2)}, u32[]{:S(2)}) collective-permute-start(f32[31,8,128]{2,1,0:T(8,128)S(1)} %get-tuple-element.21), channel_id=1, source_target_pairs={{0,2},{1,17},{2,0},{3,19},{4,6},{5,21},{6,4},{7,23},{8,10},{9,25},... | collective-permute-start | bytes 380936 | tf_op jit(solution)/shard_map/send_0_1/ppermute | solution.py:262
  12.5 1.6 %collective-permute-start.7 = (f32[31,8,128]{2,1,0:T(8,128)S(1)}, f32[31,8,128]{2,1,0:T(8,128)S(1)}, u32[]{:S(2)}, u32[]{:S(2)}) collective-permute-start(f32[31,8,128]{2,1,0:T(8,128)S(1)} %get-tuple-element.25), channel_id=1, source_target_pairs={{0,4},{1,17},{2,6},{3,19},{4,0},{5,21},{6,2},{7,23},{8,12},{9,25},... | collective-permute-start | bytes 380936 | tf_op jit(solution)/shard_map/send_1_1/ppermute | solution.py:262
  14.0 1.1 %collective-permute-done.12.got_ref = f32[2,31,8,128]{3,2,1,0:T(8,128)S(1)} collective-permute-done((f32[2,31,8,128]{3,2,1,0:T(8,128)S(1)}, f32[2,31,8,128]{3,2,1,0:T(8,128)S(1)}, u32[]{:S(2)}, u32[]{:S(2)}) %collective-permute-start.12) | collective-permute-done | bytes 253984 | tf_op jit(solution)/shard_map/send_2_0/ppermute | solution.py:262
  15.2 1.6 %collective-permute-start.13 = (f32[31,8,128]{2,1,0:T(8,128)S(1)}, f32[31,8,128]{2,1,0:T(8,128)S(1)}, u32[]{:S(2)}, u32[]{:S(2)}) collective-permute-start(f32[31,8,128]{2,1,0:T(8,128)S(1)} %get-tuple-element.29), channel_id=1, source_target_pairs={{0,4},{1,17},{2,6},{3,19},{4,0},{5,21},{6,2},{7,23},{8,12},{9,25},... | collective-permute-start | bytes 380936 | tf_op jit(solution)/shard_map/send_2_1/ppermute | solution.py:262
  16.8 1.3 %collective-permute-start.2 = (f32[31,8,128]{2,1,0:T(8,128)S(1)}, f32[31,8,128]{2,1,0:T(8,128)S(1)}, u32[]{:S(2)}, u32[]{:S(2)}) collective-permute-start(f32[31,8,128]{2,1,0:T(8,128)S(1)} %merge_0_1.1.own_ref), channel_id=1, source_target_pairs={{0,4},{1,3},{2,6},{3,1},{4,0},{5,7},{6,2},{7,5},{8,12},{9,11},{10,... | collective-permute-start | bytes 380936 | tf_op jit(solution)/shard_map/send_0_2/ppermute | solution.py:262
  18.1 2.7 %collective-permute-start.8 = (f32[31,8,128]{2,1,0:T(8,128)S(1)}, f32[31,8,128]{2,1,0:T(8,128)S(1)}, u32[]{:S(2)}, u32[]{:S(2)}) collective-permute-start(f32[31,8,128]{2,1,0:T(8,128)S(1)} %merge_1_1.1.own_ref), channel_id=1, source_target_pairs={{0,16},{1,9},{2,18},{3,11},{4,20},{5,13},{6,22},{7,15},{8,24},{9,1... | collective-permute-start | bytes 380936 | tf_op jit(solution)/shard_map/send_1_2/ppermute | solution.py:262
  20.8 2.0 %collective-permute-start.14 = (f32[31,8,128]{2,1,0:T(8,128)S(1)}, f32[31,8,128]{2,1,0:T(8,128)S(1)}, u32[]{:S(2)}, u32[]{:S(2)}) collective-permute-start(f32[31,8,128]{2,1,0:T(8,128)S(1)} %merge_2_1.1.own_ref), channel_id=1, source_target_pairs={{0,16},{1,9},{2,18},{3,11},{4,20},{5,13},{6,22},{7,15},{8,24},{9,1... | collective-permute-start | bytes 380936 | tf_op jit(solution)/shard_map/send_2_2/ppermute | solution.py:262
  22.8 1.6 %collective-permute-start.3 = (f32[31,8,128]{2,1,0:T(8,128)S(1)}, f32[31,8,128]{2,1,0:T(8,128)S(1)}, u32[]{:S(2)}, u32[]{:S(2)}) collective-permute-start(f32[31,8,128]{2,1,0:T(8,128)S(1)} %merge_0_2.1.own), channel_id=1, source_target_pairs={{0,16},{1,9},{2,18},{3,11},{4,20},{5,13},{6,22},{7,15},{8,24},{9,1... | collective-permute-start | bytes 380936 | tf_op jit(solution)/shard_map/send_0_3/ppermute | solution.py:262
  25.1 1.3 %collective-permute-start.9 = (f32[31,8,128]{2,1,0:T(8,128)S(1)}, f32[31,8,128]{2,1,0:T(8,128)S(1)}, u32[]{:S(2)}, u32[]{:S(2)}) collective-permute-start(f32[31,8,128]{2,1,0:T(8,128)S(1)} %merge_1_2.1.own), channel_id=1, source_target_pairs={{0,8},{1,3},{2,10},{3,1},{4,12},{5,7},{6,14},{7,5},{8,0},{9,11},{1... | collective-permute-start | bytes 380936 | tf_op jit(solution)/shard_map/send_1_3/ppermute | solution.py:262
  26.3 1.7 %collective-permute-done.14.got_ref = f32[31,8,128]{2,1,0:T(8,128)S(1)} collective-permute-done((f32[31,8,128]{2,1,0:T(8,128)S(1)}, f32[31,8,128]{2,1,0:T(8,128)S(1)}, u32[]{:S(2)}, u32[]{:S(2)}) %collective-permute-start.14) | collective-permute-done | bytes 127008 | tf_op jit(solution)/shard_map/send_2_2/ppermute | solution.py:262
  28.1 1.0 %collective-permute-start.15 = (f32[31,8,128]{2,1,0:T(8,128)S(1)}, f32[31,8,128]{2,1,0:T(8,128)S(1)}, u32[]{:S(2)}, u32[]{:S(2)}) collective-permute-start(f32[31,8,128]{2,1,0:T(8,128)S(1)} %merge_2_2.1.own), channel_id=1, source_target_pairs={{0,8},{1,3},{2,10},{3,1},{4,12},{5,7},{6,14},{7,5},{8,0},{9,11},{1... | collective-permute-start | bytes 380936 | tf_op jit(solution)/shard_map/send_2_3/ppermute | solution.py:262
  29.0 1.7 %collective-permute-done.3.got = f32[31,8,128]{2,1,0:T(8,128)S(1)} collective-permute-done((f32[31,8,128]{2,1,0:T(8,128)S(1)}, f32[31,8,128]{2,1,0:T(8,128)S(1)}, u32[]{:S(2)}, u32[]{:S(2)}) %collective-permute-start.3) | collective-permute-done | bytes 127008 | tf_op jit(solution)/shard_map/send_0_3/ppermute | solution.py:262
  30.9 1.6 %collective-permute-start.4 = (f32[20,8,128]{2,1,0:T(8,128)S(1)}, f32[20,8,128]{2,1,0:T(8,128)S(1)}, u32[]{:S(2)}, u32[]{:S(2)}) collective-permute-start(f32[20,8,128]{2,1,0:T(8,128)S(1)} %merge_0_3.1.own_ref), channel_id=1, source_target_pairs={{0,2},{1,17},{2,0},{3,19},{4,6},{5,21},{6,4},{7,23},{8,10},{9,25},... | collective-permute-start | bytes 245768 | tf_op jit(solution)/shard_map/send_0_4/ppermute | solution.py:262
  32.5 1.0 %collective-permute-start.10 = (f32[20,8,128]{2,1,0:T(8,128)S(1)}, f32[20,8,128]{2,1,0:T(8,128)S(1)}, u32[]{:S(2)}, u32[]{:S(2)}) collective-permute-start(f32[20,8,128]{2,1,0:T(8,128)S(1)} %merge_1_3.1.own_ref), channel_id=1, source_target_pairs={{0,4},{1,17},{2,6},{3,19},{4,0},{5,21},{6,2},{7,23},{8,12},{9,25},... | collective-permute-start | bytes 245768 | tf_op jit(solution)/shard_map/send_1_4/ppermute | solution.py:262
  33.6 1.2 %collective-permute-start.16 = (f32[20,8,128]{2,1,0:T(8,128)S(1)}, f32[20,8,128]{2,1,0:T(8,128)S(1)}, u32[]{:S(2)}, u32[]{:S(2)}) collective-permute-start(f32[20,8,128]{2,1,0:T(8,128)S(1)} %merge_2_3.1.own_ref), channel_id=1, source_target_pairs={{0,4},{1,17},{2,6},{3,19},{4,0},{5,21},{6,2},{7,23},{8,12},{9,25},... | collective-permute-start | bytes 245768 | tf_op jit(solution)/shard_map/send_2_4/ppermute | solution.py:262
  38.1 1.2 %collective-permute-start.17 = (f32[2,20,8,128]{3,2,1,0:T(8,128)S(1)}, f32[2,20,8,128]{3,2,1,0:T(8,128)S(1)}, u32[]{:S(2)}, u32[]{:S(2)}) collective-permute-start(f32[2,20,8,128]{3,2,1,0:T(8,128)S(1)} %merge_2_4.1.refs_5_), channel_id=1, source_target_pairs={{0,2},{1,5},{2,0},{3,7},{4,6},{5,1},{6,4},{7,3},{8,10},{9,13},{10,... | collective-permute-start | bytes 491528 | tf_op jit(solution)/shard_map/send_2_5/ppermute | solution.py:262
  39.3 1.4 %collective-permute-done.5.refs_0_ = f32[2,20,8,128]{3,2,1,0:T(8,128)S(1)} collective-permute-done((f32[2,20,8,128]{3,2,1,0:T(8,128)S(1)}, f32[2,20,8,128]{3,2,1,0:T(8,128)S(1)}, u32[]{:S(2)}, u32[]{:S(2)}) %collective-permute-start.5) | collective-permute-done | bytes 163872 | tf_op jit(solution)/shard_map/send_0_5/ppermute | solution.py:262
  40.8 1.6 %collective-permute-done.11.refs_2_ = f32[2,20,8,128]{3,2,1,0:T(8,128)S(1)} collective-permute-done((f32[2,20,8,128]{3,2,1,0:T(8,128)S(1)}, f32[2,20,8,128]{3,2,1,0:T(8,128)S(1)}, u32[]{:S(2)}, u32[]{:S(2)}) %collective-permute-start.11) | collective-permute-done | bytes 163872 | tf_op jit(solution)/shard_map/send_1_5/ppermute | solution.py:262
  42.4 1.8 %collective-permute-done.17.refs_4_ = f32[2,20,8,128]{3,2,1,0:T(8,128)S(1)} collective-permute-done((f32[2,20,8,128]{3,2,1,0:T(8,128)S(1)}, f32[2,20,8,128]{3,2,1,0:T(8,128)S(1)}, u32[]{:S(2)}, u32[]{:S(2)}) %collective-permute-start.17) | collective-permute-done | bytes 163872 | tf_op jit(solution)/shard_map/send_2_5/ppermute | solution.py:262
  44.2 2.3 %depart.1 = (f32[4,256,128]{2,1,0:T(8,128)S(1)}, f32[8,128]{1,0:T(8,128)S(1)}, f32[16,256,128]{2,1,0:T(8,128)}) custom-call(s32[128]{0:T(128)S(1)} %copy-done.1, f32[16,256,128]{2,1,0:T(8,128)S(1)} %get-tuple-element.18.x_ref, f32[32,128]{1,0:T(8,128)S(1)} %bitcast.13, f32[2,20,8,128]{3,2,1,0:T(8,128)S(1)} %collective-permute-done.5.refs_0_, ...), custom_call_target="tpu_custom_call" | custom-call | tf_op jit(solution)/shard_map/depart/pallas_call | solution.py:32
  (38 shorter events, 6.7 us)
Async XLA Ops:
  3.0 7.4 %collective-permute-start = (f32[2,31,8,128]{3,2,1,0:T(8,128)S(1)}, f32[2,31,8,128]{3,2,1,0:T(8,128)S(1)}, u32[]{:S(2)}, u32[]{:S(2)}) collective-permute-start(f32[2,31,8,128]{3,2,1,0:T(8,128)S(1)} %get-tuple-element.19), channel_id=1, source_target_pairs={{0,8},{1,5},{2,10},{3,7},{4,12},{5,1},{6,14},{7,3},{8,0},{9,13},{1... | collective-permute-start | bytes 761864 | tf_op jit(solution)/shard_map/send_0_0/ppermute | solution.py:262
  6.1 6.3 %collective-permute-start.6 = (f32[2,31,8,128]{3,2,1,0:T(8,128)S(1)}, f32[2,31,8,128]{3,2,1,0:T(8,128)S(1)}, u32[]{:S(2)}, u32[]{:S(2)}) collective-permute-start(f32[2,31,8,128]{3,2,1,0:T(8,128)S(1)} %get-tuple-element.23), channel_id=1, source_target_pairs={{0,2},{1,5},{2,0},{3,7},{4,6},{5,1},{6,4},{7,3},{8,10},{9,13},{10,... | collective-permute-start | bytes 761864 | tf_op jit(solution)/shard_map/send_1_0/ppermute | solution.py:262
  7.6 7.5 %collective-permute-start.12 = (f32[2,31,8,128]{3,2,1,0:T(8,128)S(1)}, f32[2,31,8,128]{3,2,1,0:T(8,128)S(1)}, u32[]{:S(2)}, u32[]{:S(2)}) collective-permute-start(f32[2,31,8,128]{3,2,1,0:T(8,128)S(1)} %get-tuple-element.27), channel_id=1, source_target_pairs={{0,2},{1,5},{2,0},{3,7},{4,6},{5,1},{6,4},{7,3},{8,10},{9,13},{10,... | collective-permute-start | bytes 761864 | tf_op jit(solution)/shard_map/send_2_0/ppermute | solution.py:262
  10.4 6.3 %collective-permute-start.1 = (f32[31,8,128]{2,1,0:T(8,128)S(1)}, f32[31,8,128]{2,1,0:T(8,128)S(1)}, u32[]{:S(2)}, u32[]{:S(2)}) collective-permute-start(f32[31,8,128]{2,1,0:T(8,128)S(1)} %get-tuple-element.21), channel_id=1, source_target_pairs={{0,2},{1,17},{2,0},{3,19},{4,6},{5,21},{6,4},{7,23},{8,10},{9,25},... | collective-permute-start | bytes 380936 | tf_op jit(solution)/shard_map/send_0_1/ppermute | solution.py:262
  12.5 5.6 %collective-permute-start.7 = (f32[31,8,128]{2,1,0:T(8,128)S(1)}, f32[31,8,128]{2,1,0:T(8,128)S(1)}, u32[]{:S(2)}, u32[]{:S(2)}) collective-permute-start(f32[31,8,128]{2,1,0:T(8,128)S(1)} %get-tuple-element.25), channel_id=1, source_target_pairs={{0,4},{1,17},{2,6},{3,19},{4,0},{5,21},{6,2},{7,23},{8,12},{9,25},... | collective-permute-start | bytes 380936 | tf_op jit(solution)/shard_map/send_1_1/ppermute | solution.py:262
  15.2 5.6 %collective-permute-start.13 = (f32[31,8,128]{2,1,0:T(8,128)S(1)}, f32[31,8,128]{2,1,0:T(8,128)S(1)}, u32[]{:S(2)}, u32[]{:S(2)}) collective-permute-start(f32[31,8,128]{2,1,0:T(8,128)S(1)} %get-tuple-element.29), channel_id=1, source_target_pairs={{0,4},{1,17},{2,6},{3,19},{4,0},{5,21},{6,2},{7,23},{8,12},{9,25},... | collective-permute-start | bytes 380936 | tf_op jit(solution)/shard_map/send_2_1/ppermute | solution.py:262
  16.7 27.4 %copy-start = (f32[4096]{0:T(1024)S(1)}, f32[4096]{0:T(1024)}, u32[]{:S(2)}) copy-start(f32[4096]{0:T(1024)} %param.7) | copy-start | bytes 49156
  16.8 27.4 %copy-start.1 = (s32[128]{0:T(128)S(1)}, s32[128]{0:T(128)}, u32[]{:S(2)}) copy-start(s32[128]{0:T(128)} %day_ref.1) | copy-start | bytes 1540
  16.8 6.1 %collective-permute-start.2 = (f32[31,8,128]{2,1,0:T(8,128)S(1)}, f32[31,8,128]{2,1,0:T(8,128)S(1)}, u32[]{:S(2)}, u32[]{:S(2)}) collective-permute-start(f32[31,8,128]{2,1,0:T(8,128)S(1)} %merge_0_1.1.own_ref), channel_id=1, source_target_pairs={{0,4},{1,3},{2,6},{3,1},{4,0},{5,7},{6,2},{7,5},{8,12},{9,11},{10,... | collective-permute-start | bytes 380936 | tf_op jit(solution)/shard_map/send_0_2/ppermute | solution.py:262
  18.1 6.9 %collective-permute-start.8 = (f32[31,8,128]{2,1,0:T(8,128)S(1)}, f32[31,8,128]{2,1,0:T(8,128)S(1)}, u32[]{:S(2)}, u32[]{:S(2)}) collective-permute-start(f32[31,8,128]{2,1,0:T(8,128)S(1)} %merge_1_1.1.own_ref), channel_id=1, source_target_pairs={{0,16},{1,9},{2,18},{3,11},{4,20},{5,13},{6,22},{7,15},{8,24},{9,1... | collective-permute-start | bytes 380936 | tf_op jit(solution)/shard_map/send_1_2/ppermute | solution.py:262
  20.8 7.3 %collective-permute-start.14 = (f32[31,8,128]{2,1,0:T(8,128)S(1)}, f32[31,8,128]{2,1,0:T(8,128)S(1)}, u32[]{:S(2)}, u32[]{:S(2)}) collective-permute-start(f32[31,8,128]{2,1,0:T(8,128)S(1)} %merge_2_1.1.own_ref), channel_id=1, source_target_pairs={{0,16},{1,9},{2,18},{3,11},{4,20},{5,13},{6,22},{7,15},{8,24},{9,1... | collective-permute-start | bytes 380936 | tf_op jit(solution)/shard_map/send_2_2/ppermute | solution.py:262
  22.8 7.9 %collective-permute-start.3 = (f32[31,8,128]{2,1,0:T(8,128)S(1)}, f32[31,8,128]{2,1,0:T(8,128)S(1)}, u32[]{:S(2)}, u32[]{:S(2)}) collective-permute-start(f32[31,8,128]{2,1,0:T(8,128)S(1)} %merge_0_2.1.own), channel_id=1, source_target_pairs={{0,16},{1,9},{2,18},{3,11},{4,20},{5,13},{6,22},{7,15},{8,24},{9,1... | collective-permute-start | bytes 380936 | tf_op jit(solution)/shard_map/send_0_3/ppermute | solution.py:262
  25.1 7.4 %collective-permute-start.9 = (f32[31,8,128]{2,1,0:T(8,128)S(1)}, f32[31,8,128]{2,1,0:T(8,128)S(1)}, u32[]{:S(2)}, u32[]{:S(2)}) collective-permute-start(f32[31,8,128]{2,1,0:T(8,128)S(1)} %merge_1_2.1.own), channel_id=1, source_target_pairs={{0,8},{1,3},{2,10},{3,1},{4,12},{5,7},{6,14},{7,5},{8,0},{9,11},{1... | collective-permute-start | bytes 380936 | tf_op jit(solution)/shard_map/send_1_3/ppermute | solution.py:262
  28.1 5.4 %collective-permute-start.15 = (f32[31,8,128]{2,1,0:T(8,128)S(1)}, f32[31,8,128]{2,1,0:T(8,128)S(1)}, u32[]{:S(2)}, u32[]{:S(2)}) collective-permute-start(f32[31,8,128]{2,1,0:T(8,128)S(1)} %merge_2_2.1.own), channel_id=1, source_target_pairs={{0,8},{1,3},{2,10},{3,1},{4,12},{5,7},{6,14},{7,5},{8,0},{9,11},{1... | collective-permute-start | bytes 380936 | tf_op jit(solution)/shard_map/send_2_3/ppermute | solution.py:262
  30.9 4.5 %collective-permute-start.4 = (f32[20,8,128]{2,1,0:T(8,128)S(1)}, f32[20,8,128]{2,1,0:T(8,128)S(1)}, u32[]{:S(2)}, u32[]{:S(2)}) collective-permute-start(f32[20,8,128]{2,1,0:T(8,128)S(1)} %merge_0_3.1.own_ref), channel_id=1, source_target_pairs={{0,2},{1,17},{2,0},{3,19},{4,6},{5,21},{6,4},{7,23},{8,10},{9,25},... | collective-permute-start | bytes 245768 | tf_op jit(solution)/shard_map/send_0_4/ppermute | solution.py:262
  32.5 4.5 %collective-permute-start.10 = (f32[20,8,128]{2,1,0:T(8,128)S(1)}, f32[20,8,128]{2,1,0:T(8,128)S(1)}, u32[]{:S(2)}, u32[]{:S(2)}) collective-permute-start(f32[20,8,128]{2,1,0:T(8,128)S(1)} %merge_1_3.1.own_ref), channel_id=1, source_target_pairs={{0,4},{1,17},{2,6},{3,19},{4,0},{5,21},{6,2},{7,23},{8,12},{9,25},... | collective-permute-start | bytes 245768 | tf_op jit(solution)/shard_map/send_1_4/ppermute | solution.py:262
  33.6 4.5 %collective-permute-start.16 = (f32[20,8,128]{2,1,0:T(8,128)S(1)}, f32[20,8,128]{2,1,0:T(8,128)S(1)}, u32[]{:S(2)}, u32[]{:S(2)}) collective-permute-start(f32[20,8,128]{2,1,0:T(8,128)S(1)} %merge_2_3.1.own_ref), channel_id=1, source_target_pairs={{0,4},{1,17},{2,6},{3,19},{4,0},{5,21},{6,2},{7,23},{8,12},{9,25},... | collective-permute-start | bytes 245768 | tf_op jit(solution)/shard_map/send_2_4/ppermute | solution.py:262
  35.4 5.4 %collective-permute-start.5 = (f32[2,20,8,128]{3,2,1,0:T(8,128)S(1)}, f32[2,20,8,128]{3,2,1,0:T(8,128)S(1)}, u32[]{:S(2)}, u32[]{:S(2)}) collective-permute-start(f32[2,20,8,128]{3,2,1,0:T(8,128)S(1)} %merge_0_4.1.refs_1_), channel_id=1, source_target_pairs={{0,8},{1,5},{2,10},{3,7},{4,12},{5,1},{6,14},{7,3},{8,0},{9,13},{1... | collective-permute-start | bytes 491528 | tf_op jit(solution)/shard_map/send_0_5/ppermute | solution.py:262
  37.0 5.4 %collective-permute-start.11 = (f32[2,20,8,128]{3,2,1,0:T(8,128)S(1)}, f32[2,20,8,128]{3,2,1,0:T(8,128)S(1)}, u32[]{:S(2)}, u32[]{:S(2)}) collective-permute-start(f32[2,20,8,128]{3,2,1,0:T(8,128)S(1)} %merge_1_4.1.refs_3_), channel_id=1, source_target_pairs={{0,2},{1,5},{2,0},{3,7},{4,6},{5,1},{6,4},{7,3},{8,10},{9,13},{10,... | collective-permute-start | bytes 491528 | tf_op jit(solution)/shard_map/send_1_5/ppermute | solution.py:262
  38.1 6.1 %collective-permute-start.17 = (f32[2,20,8,128]{3,2,1,0:T(8,128)S(1)}, f32[2,20,8,128]{3,2,1,0:T(8,128)S(1)}, u32[]{:S(2)}, u32[]{:S(2)}) collective-permute-start(f32[2,20,8,128]{3,2,1,0:T(8,128)S(1)} %merge_2_4.1.refs_5_), channel_id=1, source_target_pairs={{0,2},{1,5},{2,0},{3,7},{4,6},{5,1},{6,4},{7,3},{8,10},{9,13},{10,... | collective-permute-start | bytes 491528 | tf_op jit(solution)/shard_map/send_2_5/ppermute | solution.py:262
  46.5 1.2 %collective-permute-start.18 = (f32[8,128]{1,0:T(8,128)S(1)}, f32[8,128]{1,0:T(8,128)S(1)}, u32[]{:S(2)}, u32[]{:S(2)}) collective-permute-start(f32[8,128]{1,0:T(8,128)S(1)} %get-tuple-element.33), channel_id=1, source_target_pairs={{0,1},{1,0},{2,3},{3,2},{4,5},{5,4},{6,7},{7,6},{8,9},{9,8},{10,11... | collective-permute-start | bytes 12296 | tf_op jit(solution)/shard_map/ppermute | solution.py:301

commit v6 on v5

--- a/solution.py
+++ b/solution.py
@@ -15,9 +15,12 @@
 BLOCKS = 4
 HALVINGS = 2
 HOURS, HIGH, LOW, TILES = SLOTS, SLOTS + 1, 2 * SLOTS + 1, 3 * SLOTS + 1
+KINDS = (0, HIGH, jnp.add), (HIGH, LOW, jnp.maximum), (LOW, TILES, jnp.minimum)
 ORDERS = (((2, 1), (0, 3), (1, 0), (3, 2)), ((0, 1), (1, 3), (3, 2), (2, 0)), ((0, 1), (1, 3), (3, 2), (2, 0)))
 AXES = ("year", "space")
 PIECES = 4
+LATE = 2
+TOGETHER = 4
 
 VMEM = pl.BlockSpec(memory_space=pltpu.VMEM)
 SMEM = pl.BlockSpec(memory_space=pltpu.SMEM)
@@ -56,7 +59,7 @@
 
 
 def stats_kernel(day_in, tally_in, x_in, *refs):
-    outs, (x_ref, day_ref, tally_ref, hours, totals, arrived, listed) = refs[: 2 * CHUNKS], refs[2 * CHUNKS :]
+    outs, (x_ref, day_ref, tally_ref, hours, even, odd, arrived, listed) = refs[: 2 * CHUNKS], refs[2 * CHUNKS :]
     tiles, rows = x_in.shape[0], x_in.shape[1] // BLOCKS
     piece = tiles // PIECES
     height = rows // SUBLANES
@@ -69,9 +72,10 @@
         copy.start()
     for i in range(CHUNKS * BLOCKS):
         at = i * TILES
-        totals[at : at + HIGH] = jnp.zeros((HIGH, height, LANES), jnp.float32)
-        totals[at + HIGH : at + LOW] = jnp.full((SLOTS, height, LANES), -jnp.inf, jnp.float32)
-        totals[at + LOW : at + TILES] = jnp.full((SLOTS, height, LANES), jnp.inf, jnp.float32)
+        for totals in (even, odd):
+            totals[at : at + HIGH] = jnp.zeros((HIGH, height, LANES), jnp.float32)
+            totals[at + HIGH : at + LOW] = jnp.full((SLOTS, height, LANES), -jnp.inf, jnp.float32)
+            totals[at + LOW : at + TILES] = jnp.full((SLOTS, height, LANES), jnp.inf, jnp.float32)
     for d in range(CHUNKS * SLOTS):
         hours[d] = 0
     for copy in lists:
@@ -79,7 +83,7 @@
 
     def tile(t, carry):
         for k in range(SUBLANES):
-            step = t * SUBLANES + k
+            step, totals = t * SUBLANES + k, odd if k % 2 else even
             day, tally = day_ref[step], tally_ref[step]
             chunk, index = place(day)
             base = chunk * (BLOCKS * TILES) + index
@@ -106,7 +110,9 @@
         for half in range(2):
             for slot in range(2):
                 out, start = outs[2 * c + half].at[slot], (c * BLOCKS + blocks[half][slot]) * TILES
-                out[...] = totals[pl.ds(start, TILES)]
+                for a, b, join in KINDS:
+                    at = pl.ds(start + a, b - a)
+                    out[a:b] = join(even[at], odd[at])
                 for k, pair in enumerate(pairs):
                     out[HOURS, k : k + 1, :] = jnp.where(left, *pair)
 
@@ -127,6 +133,7 @@
             pltpu.SMEM(day.shape, jnp.int32),
             pltpu.SMEM((CHUNKS * SLOTS,), jnp.int32),
             vmem(CHUNKS * BLOCKS * TILES, height, LANES),
+            vmem(CHUNKS * BLOCKS * TILES, height, LANES),
             pltpu.SemaphoreType.DMA((PIECES,)),
             pltpu.SemaphoreType.DMA((2,)),
         ],
@@ -135,7 +142,7 @@
 
 
 def merge_kernel(got_ref, own_ref, *outs):
-    for a, b, join in ((0, HIGH, jnp.add), (HIGH, LOW, jnp.maximum), (LOW, TILES, jnp.minimum)):
+    for a, b, join in KINDS:
         for i, out in enumerate(outs):
             got, own = (got_ref.at[i], own_ref.at[i]) if len(outs) > 1 else (got_ref, own_ref)
             out[a:b] = join(got[a:b], own[a:b])
@@ -159,8 +166,11 @@
     out_ref[1] = own_ref[...]
 
 
-def depart_kernel(day_ref, x_ref, w_ref, *refs):
-    tables, (last_ref, sums_ref, whole_ref, table, ready, squares, left) = refs[: 2 * CHUNKS], refs[2 * CHUNKS :]
+def depart_kernel(day_in, x_ref, w_ref, *refs):
+    tables, refs = refs[: 2 * CHUNKS], refs[2 * CHUNKS :]
+    last_ref, sums_ref, whole_ref, table, ready, squares, left, day_ref, listed = refs
+    days = pltpu.make_async_copy(day_in, day_ref, listed)
+    days.start()
     tiles, rows = x_ref.shape[0], x_ref.shape[1] // BLOCKS
     piece = tiles // PIECES
     height = rows // SUBLANES
@@ -170,29 +180,35 @@
             for slot in range(2):
                 start = (c * BLOCKS + blocks[half][slot]) * 2 * SLOTS
                 table[pl.ds(start, 2 * SLOTS)] = tables[2 * c + half][slot]
+    days.wait()
     weights = [w_ref[b * height : (b + 1) * height, :] for b in range(BLOCKS)]
 
     def tile(first, out_ref, t, carry):
-        for k in range(SUBLANES):
-            chunk, index = place(day_ref[t * SUBLANES + k])
-            base = chunk * (BLOCKS * 2 * SLOTS) + index
-            total = None
-            for b in range(BLOCKS):
-                at = pl.ds(b * rows + k, height, stride=SUBLANES)
-                mean, scale = table[base + b * 2 * SLOTS], table[base + (b * 2 + 1) * SLOTS]
-                departure = (x_ref[t, at, :] - mean) * scale
-                out_ref[t - first, at, :] = departure
-                square = weights[b] * departure * departure
-                total = square if total is None else total + square
-            squares[pl.ds(pl.multiple_of((t * SUBLANES + k) * height, height), height), :] = total
+        for k in range(0, SUBLANES, TOGETHER):
+            loaded = []
+            for j in range(k, k + TOGETHER):
+                chunk, index = place(day_ref[t * SUBLANES + j])
+                base = chunk * (BLOCKS * 2 * SLOTS) + index
+                for b in range(BLOCKS):
+                    x = x_ref[t, pl.ds(b * rows + j, height, stride=SUBLANES), :]
+                    loaded.append((x, table[base + b * 2 * SLOTS], table[base + (b * 2 + 1) * SLOTS]))
+            for j in range(k, k + TOGETHER):
+                total = None
+                for b in range(BLOCKS):
+                    x, mean, scale = loaded[(j - k) * BLOCKS + b]
+                    departure = (x - mean) * scale
+                    out_ref[t - first, pl.ds(b * rows + j, height, stride=SUBLANES), :] = departure
+                    square = weights[b] * departure * departure
+                    total = square if total is None else total + square
+                squares[pl.ds(pl.multiple_of((t * SUBLANES + j) * height, height), height), :] = total
         return carry
 
     copies = []
     for p in range(PIECES):
-        first, final = p * piece, p == PIECES - 1
-        out = last_ref if final else ready
-        lax.fori_loop(first, first + piece, functools.partial(tile, first if final else 0, out), 0)
-        if not final:
+        first, late = p * piece, p >= PIECES - LATE
+        before = (PIECES - LATE) * piece if late else 0
+        lax.fori_loop(first, first + piece, functools.partial(tile, before, last_ref if late else ready), 0)
+        if not late:
             at = pl.ds(first, piece)
             copies.append(pltpu.make_async_copy(ready.at[at], whole_ref.at[at], left.at[p]))
             copies[-1].start()
@@ -213,20 +229,22 @@
 
 def depart(day, x, w, tables):
     tiles, rows = x.shape[0], x.shape[1] // BLOCKS
-    height, piece, steps = rows // SUBLANES, tiles // PIECES, tiles * SUBLANES
+    height, late, steps = rows // SUBLANES, tiles // PIECES * LATE, tiles * SUBLANES
     inputs = [day, x, w, *tables]
     return local_call(
         depart_kernel,
         "depart",
-        (vmem(piece, *x.shape[1:]), vmem(SUBLANES, steps), pltpu.HBM(x.shape, jnp.float32)),
+        (vmem(late, *x.shape[1:]), vmem(SUBLANES, steps), pltpu.HBM(x.shape, jnp.float32)),
         *inputs,
-        in_specs=[SMEM] + [VMEM] * (len(inputs) - 1),
+        in_specs=[VMEM] * len(inputs),
         out_specs=(VMEM, VMEM, HBM),
         scratch_shapes=[
             vmem(CHUNKS * BLOCKS * 2 * SLOTS, height, LANES),
-            vmem(tiles - piece, *x.shape[1:]),
+            vmem(tiles - late, *x.shape[1:]),
             vmem(steps * height, LANES),
-            pltpu.SemaphoreType.DMA((PIECES - 1,)),
+            pltpu.SemaphoreType.DMA((PIECES - LATE,)),
+            pltpu.SMEM(day.shape, jnp.int32),
+            pltpu.SemaphoreType.DMA,
         ],
         vmem=8 << 20,
     )

time: 48.4 us -> 47.8 us (0.988)
  no operation moved by 1% of the time
where the time goes in v6:
time: 47.8 us; the launch traced here: 47.7 us
  starting transfers between devices  27 us (56%)
  waiting for transfers between devices  13.8 us (29%)
  Pallas kernels  5.61 us (12%)
  between operations  0.72 us (2%)
  other arithmetic  0.53 us (1%)
    ppermute x18, starting transfers between devices, exchange(): lax.ppermute(pltpu.with_memory_space_constraint(x, pltpu.VMEM), AXES, par...  26.9 us
    ppermute x18, waiting for transfers between devices, exchange(): lax.ppermute(pltpu.with_memory_space_constraint(x, pltpu.VMEM), AXES, par...  13.7 us
    pallas_call x18, Pallas kernels, local_call(): pl.pallas_call(kernel, in_specs=specs, out_shape=out_shape, name=name, co...  5.61 us
  transfers between devices with their start and end apart: 19, of which 12 were waited for; matrix products, arithmetic and copies ran while one was open for 0% of the time, Pallas kernels for 3%

profile of v6, /device:TPU:0, one launch (start us, length us, event | category | flops | bytes accessed | tf_op | source)
XLA Modules:
  0.0 47.7 jit_solution(14634831002702092380)
XLA Ops:
  0.6 2.2 %stats.1 = (f32[2,31,8,128]{3,2,1,0:T(8,128)S(1)}, f32[2,31,8,128]{3,2,1,0:T(8,128)S(1)}, f32[2,31,8,128]{3,2,1,0:T(8,128)S(1)}, f32[2,31,8,128]{3,2,1,0:T(8,128...) custom-call(s32[128]{0:T(128)} %day_in.3, s32[128]{0:T(128)} %tally_in.1, ...), custom_call_target="tpu_custom_call" | custom-call | tf_op jit(solution)/shard_map/stats/pallas_call | solution.py:35
  2.8 3.1 %collective-permute-start = (f32[2,31,8,128]{3,2,1,0:T(8,128)S(1)}, f32[2,31,8,128]{3,2,1,0:T(8,128)S(1)}, u32[]{:S(2)}, u32[]{:S(2)}) collective-permute-start(f32[2,31,8,128]{3,2,1,0:T(8,128)S(1)} %get-tuple-element.19), channel_id=1, source_target_pairs={{0,8},{1,5},{2,10},{3,7},{4,12},{5,1},{6,14},{7,3},{8,0},{9,13},{1... | collective-permute-start | bytes 761864 | tf_op jit(solution)/shard_map/send_0_0/ppermute | solution.py:280
  5.9 1.5 %collective-permute-start.6 = (f32[2,31,8,128]{3,2,1,0:T(8,128)S(1)}, f32[2,31,8,128]{3,2,1,0:T(8,128)S(1)}, u32[]{:S(2)}, u32[]{:S(2)}) collective-permute-start(f32[2,31,8,128]{3,2,1,0:T(8,128)S(1)} %get-tuple-element.23), channel_id=1, source_target_pairs={{0,2},{1,5},{2,0},{3,7},{4,6},{5,1},{6,4},{7,3},{8,10},{9,13},{10,... | collective-permute-start | bytes 761864 | tf_op jit(solution)/shard_map/send_1_0/ppermute | solution.py:280
  8.0 2.2 %collective-permute-done.got_ref = f32[2,31,8,128]{3,2,1,0:T(8,128)S(1)} collective-permute-done((f32[2,31,8,128]{3,2,1,0:T(8,128)S(1)}, f32[2,31,8,128]{3,2,1,0:T(8,128)S(1)}, u32[]{:S(2)}, u32[]{:S(2)}) %collective-permute-start) | collective-permute-done | bytes 253984 | tf_op jit(solution)/shard_map/send_0_0/ppermute | solution.py:280
  10.2 2.0 %collective-permute-start.1 = (f32[31,8,128]{2,1,0:T(8,128)S(1)}, f32[31,8,128]{2,1,0:T(8,128)S(1)}, u32[]{:S(2)}, u32[]{:S(2)}) collective-permute-start(f32[31,8,128]{2,1,0:T(8,128)S(1)} %get-tuple-element.21), channel_id=1, source_target_pairs={{0,2},{1,17},{2,0},{3,19},{4,6},{5,21},{6,4},{7,23},{8,10},{9,25},... | collective-permute-start | bytes 380936 | tf_op jit(solution)/shard_map/send_0_1/ppermute | solution.py:280
  12.3 1.6 %collective-permute-start.7 = (f32[31,8,128]{2,1,0:T(8,128)S(1)}, f32[31,8,128]{2,1,0:T(8,128)S(1)}, u32[]{:S(2)}, u32[]{:S(2)}) collective-permute-start(f32[31,8,128]{2,1,0:T(8,128)S(1)} %get-tuple-element.25), channel_id=1, source_target_pairs={{0,4},{1,17},{2,6},{3,19},{4,0},{5,21},{6,2},{7,23},{8,12},{9,25},... | collective-permute-start | bytes 380936 | tf_op jit(solution)/shard_map/send_1_1/ppermute | solution.py:280
  13.9 1.1 %collective-permute-done.12.got_ref = f32[2,31,8,128]{3,2,1,0:T(8,128)S(1)} collective-permute-done((f32[2,31,8,128]{3,2,1,0:T(8,128)S(1)}, f32[2,31,8,128]{3,2,1,0:T(8,128)S(1)}, u32[]{:S(2)}, u32[]{:S(2)}) %collective-permute-start.12) | collective-permute-done | bytes 253984 | tf_op jit(solution)/shard_map/send_2_0/ppermute | solution.py:280
  15.0 1.6 %collective-permute-start.13 = (f32[31,8,128]{2,1,0:T(8,128)S(1)}, f32[31,8,128]{2,1,0:T(8,128)S(1)}, u32[]{:S(2)}, u32[]{:S(2)}) collective-permute-start(f32[31,8,128]{2,1,0:T(8,128)S(1)} %get-tuple-element.29), channel_id=1, source_target_pairs={{0,4},{1,17},{2,6},{3,19},{4,0},{5,21},{6,2},{7,23},{8,12},{9,25},... | collective-permute-start | bytes 380936 | tf_op jit(solution)/shard_map/send_2_1/ppermute | solution.py:280
  16.6 1.3 %collective-permute-start.2 = (f32[31,8,128]{2,1,0:T(8,128)S(1)}, f32[31,8,128]{2,1,0:T(8,128)S(1)}, u32[]{:S(2)}, u32[]{:S(2)}) collective-permute-start(f32[31,8,128]{2,1,0:T(8,128)S(1)} %merge_0_1.1.own_ref), channel_id=1, source_target_pairs={{0,4},{1,3},{2,6},{3,1},{4,0},{5,7},{6,2},{7,5},{8,12},{9,11},{10,... | collective-permute-start | bytes 380936 | tf_op jit(solution)/shard_map/send_0_2/ppermute | solution.py:280
  17.9 2.7 %collective-permute-start.8 = (f32[31,8,128]{2,1,0:T(8,128)S(1)}, f32[31,8,128]{2,1,0:T(8,128)S(1)}, u32[]{:S(2)}, u32[]{:S(2)}) collective-permute-start(f32[31,8,128]{2,1,0:T(8,128)S(1)} %merge_1_1.1.own_ref), channel_id=1, source_target_pairs={{0,16},{1,9},{2,18},{3,11},{4,20},{5,13},{6,22},{7,15},{8,24},{9,1... | collective-permute-start | bytes 380936 | tf_op jit(solution)/shard_map/send_1_2/ppermute | solution.py:280
  20.6 2.0 %collective-permute-start.14 = (f32[31,8,128]{2,1,0:T(8,128)S(1)}, f32[31,8,128]{2,1,0:T(8,128)S(1)}, u32[]{:S(2)}, u32[]{:S(2)}) collective-permute-start(f32[31,8,128]{2,1,0:T(8,128)S(1)} %merge_2_1.1.own_ref), channel_id=1, source_target_pairs={{0,16},{1,9},{2,18},{3,11},{4,20},{5,13},{6,22},{7,15},{8,24},{9,1... | collective-permute-start | bytes 380936 | tf_op jit(solution)/shard_map/send_2_2/ppermute | solution.py:280
  22.7 1.6 %collective-permute-start.3 = (f32[31,8,128]{2,1,0:T(8,128)S(1)}, f32[31,8,128]{2,1,0:T(8,128)S(1)}, u32[]{:S(2)}, u32[]{:S(2)}) collective-permute-start(f32[31,8,128]{2,1,0:T(8,128)S(1)} %merge_0_2.1.own), channel_id=1, source_target_pairs={{0,16},{1,9},{2,18},{3,11},{4,20},{5,13},{6,22},{7,15},{8,24},{9,1... | collective-permute-start | bytes 380936 | tf_op jit(solution)/shard_map/send_0_3/ppermute | solution.py:280
  24.9 1.3 %collective-permute-start.9 = (f32[31,8,128]{2,1,0:T(8,128)S(1)}, f32[31,8,128]{2,1,0:T(8,128)S(1)}, u32[]{:S(2)}, u32[]{:S(2)}) collective-permute-start(f32[31,8,128]{2,1,0:T(8,128)S(1)} %merge_1_2.1.own), channel_id=1, source_target_pairs={{0,8},{1,3},{2,10},{3,1},{4,12},{5,7},{6,14},{7,5},{8,0},{9,11},{1... | collective-permute-start | bytes 380936 | tf_op jit(solution)/shard_map/send_1_3/ppermute | solution.py:280
  26.2 1.7 %collective-permute-done.14.got_ref = f32[31,8,128]{2,1,0:T(8,128)S(1)} collective-permute-done((f32[31,8,128]{2,1,0:T(8,128)S(1)}, f32[31,8,128]{2,1,0:T(8,128)S(1)}, u32[]{:S(2)}, u32[]{:S(2)}) %collective-permute-start.14) | collective-permute-done | bytes 127008 | tf_op jit(solution)/shard_map/send_2_2/ppermute | solution.py:280
  28.9 1.7 %collective-permute-done.3.got = f32[31,8,128]{2,1,0:T(8,128)S(1)} collective-permute-done((f32[31,8,128]{2,1,0:T(8,128)S(1)}, f32[31,8,128]{2,1,0:T(8,128)S(1)}, u32[]{:S(2)}, u32[]{:S(2)}) %collective-permute-start.3) | collective-permute-done | bytes 127008 | tf_op jit(solution)/shard_map/send_0_3/ppermute | solution.py:280
  30.7 1.6 %collective-permute-start.4 = (f32[20,8,128]{2,1,0:T(8,128)S(1)}, f32[20,8,128]{2,1,0:T(8,128)S(1)}, u32[]{:S(2)}, u32[]{:S(2)}) collective-permute-start(f32[20,8,128]{2,1,0:T(8,128)S(1)} %merge_0_3.1.own_ref), channel_id=1, source_target_pairs={{0,2},{1,17},{2,0},{3,19},{4,6},{5,21},{6,4},{7,23},{8,10},{9,25},... | collective-permute-start | bytes 245768 | tf_op jit(solution)/shard_map/send_0_4/ppermute | solution.py:280
  32.3 1.0 %collective-permute-start.10 = (f32[20,8,128]{2,1,0:T(8,128)S(1)}, f32[20,8,128]{2,1,0:T(8,128)S(1)}, u32[]{:S(2)}, u32[]{:S(2)}) collective-permute-start(f32[20,8,128]{2,1,0:T(8,128)S(1)} %merge_1_3.1.own_ref), channel_id=1, source_target_pairs={{0,4},{1,17},{2,6},{3,19},{4,0},{5,21},{6,2},{7,23},{8,12},{9,25},... | collective-permute-start | bytes 245768 | tf_op jit(solution)/shard_map/send_1_4/ppermute | solution.py:280
  33.4 1.2 %collective-permute-start.16 = (f32[20,8,128]{2,1,0:T(8,128)S(1)}, f32[20,8,128]{2,1,0:T(8,128)S(1)}, u32[]{:S(2)}, u32[]{:S(2)}) collective-permute-start(f32[20,8,128]{2,1,0:T(8,128)S(1)} %merge_2_3.1.own_ref), channel_id=1, source_target_pairs={{0,4},{1,17},{2,6},{3,19},{4,0},{5,21},{6,2},{7,23},{8,12},{9,25},... | collective-permute-start | bytes 245768 | tf_op jit(solution)/shard_map/send_2_4/ppermute | solution.py:280
  37.9 1.2 %collective-permute-start.17 = (f32[2,20,8,128]{3,2,1,0:T(8,128)S(1)}, f32[2,20,8,128]{3,2,1,0:T(8,128)S(1)}, u32[]{:S(2)}, u32[]{:S(2)}) collective-permute-start(f32[2,20,8,128]{3,2,1,0:T(8,128)S(1)} %merge_2_4.1.refs_5_), channel_id=1, source_target_pairs={{0,2},{1,5},{2,0},{3,7},{4,6},{5,1},{6,4},{7,3},{8,10},{9,13},{10,... | collective-permute-start | bytes 491528 | tf_op jit(solution)/shard_map/send_2_5/ppermute | solution.py:280
  39.2 1.4 %collective-permute-done.5.refs_0_ = f32[2,20,8,128]{3,2,1,0:T(8,128)S(1)} collective-permute-done((f32[2,20,8,128]{3,2,1,0:T(8,128)S(1)}, f32[2,20,8,128]{3,2,1,0:T(8,128)S(1)}, u32[]{:S(2)}, u32[]{:S(2)}) %collective-permute-start.5) | collective-permute-done | bytes 163872 | tf_op jit(solution)/shard_map/send_0_5/ppermute | solution.py:280
  40.6 1.6 %collective-permute-done.11.refs_2_ = f32[2,20,8,128]{3,2,1,0:T(8,128)S(1)} collective-permute-done((f32[2,20,8,128]{3,2,1,0:T(8,128)S(1)}, f32[2,20,8,128]{3,2,1,0:T(8,128)S(1)}, u32[]{:S(2)}, u32[]{:S(2)}) %collective-permute-start.11) | collective-permute-done | bytes 163872 | tf_op jit(solution)/shard_map/send_1_5/ppermute | solution.py:280
  42.2 1.8 %collective-permute-done.17.refs_4_ = f32[2,20,8,128]{3,2,1,0:T(8,128)S(1)} collective-permute-done((f32[2,20,8,128]{3,2,1,0:T(8,128)S(1)}, f32[2,20,8,128]{3,2,1,0:T(8,128)S(1)}, u32[]{:S(2)}, u32[]{:S(2)}) %collective-permute-start.17) | collective-permute-done | bytes 163872 | tf_op jit(solution)/shard_map/send_2_5/ppermute | solution.py:280
  44.0 1.9 %depart.1 = (f32[8,256,128]{2,1,0:T(8,128)S(1)}, f32[8,128]{1,0:T(8,128)S(1)}, f32[16,256,128]{2,1,0:T(8,128)}) custom-call(s32[128]{0:T(128)S(1)} %copy-done.1, f32[16,256,128]{2,1,0:T(8,128)S(1)} %get-tuple-element.18.x_ref, f32[32,128]{1,0:T(8,128)S(1)} %bitcast.13, f32[2,20,8,128]{3,2,1,0:T(8,128)S(1)} %collective-permute-done.5.refs_0_, ...), custom_call_target="tpu_custom_call" | custom-call | tf_op jit(solution)/shard_map/depart/pallas_call | solution.py:35
  46.0 1.0 %emit.1 = f32[16,256,128]{2,1,0:T(8,128)} custom-call(f32[8,256,128]{2,1,0:T(8,128)S(1)} %get-tuple-element.31.part_ref, f32[16,256,128]{2,1,0:T(8,128)} %get-tuple-element.32.before_ref), custom_call_target="tpu_custom_call", output_to_operand_aliasing={{}: (1, {})} | custom-call | tf_op jit(solution)/shard_map/emit/pallas_call | solution.py:35
  (38 shorter events, 6.6 us)
Async XLA Ops:
  2.8 7.4 %collective-permute-start = (f32[2,31,8,128]{3,2,1,0:T(8,128)S(1)}, f32[2,31,8,128]{3,2,1,0:T(8,128)S(1)}, u32[]{:S(2)}, u32[]{:S(2)}) collective-permute-start(f32[2,31,8,128]{3,2,1,0:T(8,128)S(1)} %get-tuple-element.19), channel_id=1, source_target_pairs={{0,8},{1,5},{2,10},{3,7},{4,12},{5,1},{6,14},{7,3},{8,0},{9,13},{1... | collective-permute-start | bytes 761864 | tf_op jit(solution)/shard_map/send_0_0/ppermute | solution.py:280
  5.9 6.3 %collective-permute-start.6 = (f32[2,31,8,128]{3,2,1,0:T(8,128)S(1)}, f32[2,31,8,128]{3,2,1,0:T(8,128)S(1)}, u32[]{:S(2)}, u32[]{:S(2)}) collective-permute-start(f32[2,31,8,128]{3,2,1,0:T(8,128)S(1)} %get-tuple-element.23), channel_id=1, source_target_pairs={{0,2},{1,5},{2,0},{3,7},{4,6},{5,1},{6,4},{7,3},{8,10},{9,13},{10,... | collective-permute-start | bytes 761864 | tf_op jit(solution)/shard_map/send_1_0/ppermute | solution.py:280
  7.4 7.5 %collective-permute-start.12 = (f32[2,31,8,128]{3,2,1,0:T(8,128)S(1)}, f32[2,31,8,128]{3,2,1,0:T(8,128)S(1)}, u32[]{:S(2)}, u32[]{:S(2)}) collective-permute-start(f32[2,31,8,128]{3,2,1,0:T(8,128)S(1)} %get-tuple-element.27), channel_id=1, source_target_pairs={{0,2},{1,5},{2,0},{3,7},{4,6},{5,1},{6,4},{7,3},{8,10},{9,13},{10,... | collective-permute-start | bytes 761864 | tf_op jit(solution)/shard_map/send_2_0/ppermute | solution.py:280
  10.2 6.3 %collective-permute-start.1 = (f32[31,8,128]{2,1,0:T(8,128)S(1)}, f32[31,8,128]{2,1,0:T(8,128)S(1)}, u32[]{:S(2)}, u32[]{:S(2)}) collective-permute-start(f32[31,8,128]{2,1,0:T(8,128)S(1)} %get-tuple-element.21), channel_id=1, source_target_pairs={{0,2},{1,17},{2,0},{3,19},{4,6},{5,21},{6,4},{7,23},{8,10},{9,25},... | collective-permute-start | bytes 380936 | tf_op jit(solution)/shard_map/send_0_1/ppermute | solution.py:280
  12.3 5.6 %collective-permute-start.7 = (f32[31,8,128]{2,1,0:T(8,128)S(1)}, f32[31,8,128]{2,1,0:T(8,128)S(1)}, u32[]{:S(2)}, u32[]{:S(2)}) collective-permute-start(f32[31,8,128]{2,1,0:T(8,128)S(1)} %get-tuple-element.25), channel_id=1, source_target_pairs={{0,4},{1,17},{2,6},{3,19},{4,0},{5,21},{6,2},{7,23},{8,12},{9,25},... | collective-permute-start | bytes 380936 | tf_op jit(solution)/shard_map/send_1_1/ppermute | solution.py:280
  15.0 5.6 %collective-permute-start.13 = (f32[31,8,128]{2,1,0:T(8,128)S(1)}, f32[31,8,128]{2,1,0:T(8,128)S(1)}, u32[]{:S(2)}, u32[]{:S(2)}) collective-permute-start(f32[31,8,128]{2,1,0:T(8,128)S(1)} %get-tuple-element.29), channel_id=1, source_target_pairs={{0,4},{1,17},{2,6},{3,19},{4,0},{5,21},{6,2},{7,23},{8,12},{9,25},... | collective-permute-start | bytes 380936 | tf_op jit(solution)/shard_map/send_2_1/ppermute | solution.py:280
  16.6 27.4 %copy-start = (f32[4096]{0:T(1024)S(1)}, f32[4096]{0:T(1024)}, u32[]{:S(2)}) copy-start(f32[4096]{0:T(1024)} %param.7) | copy-start | bytes 49156
  16.6 27.4 %copy-start.1 = (s32[128]{0:T(128)S(1)}, s32[128]{0:T(128)}, u32[]{:S(2)}) copy-start(s32[128]{0:T(128)} %day_in.3) | copy-start | bytes 1540
  16.6 6.1 %collective-permute-start.2 = (f32[31,8,128]{2,1,0:T(8,128)S(1)}, f32[31,8,128]{2,1,0:T(8,128)S(1)}, u32[]{:S(2)}, u32[]{:S(2)}) collective-permute-start(f32[31,8,128]{2,1,0:T(8,128)S(1)} %merge_0_1.1.own_ref), channel_id=1, source_target_pairs={{0,4},{1,3},{2,6},{3,1},{4,0},{5,7},{6,2},{7,5},{8,12},{9,11},{10,... | collective-permute-start | bytes 380936 | tf_op jit(solution)/shard_map/send_0_2/ppermute | solution.py:280
  17.9 6.9 %collective-permute-start.8 = (f32[31,8,128]{2,1,0:T(8,128)S(1)}, f32[31,8,128]{2,1,0:T(8,128)S(1)}, u32[]{:S(2)}, u32[]{:S(2)}) collective-permute-start(f32[31,8,128]{2,1,0:T(8,128)S(1)} %merge_1_1.1.own_ref), channel_id=1, source_target_pairs={{0,16},{1,9},{2,18},{3,11},{4,20},{5,13},{6,22},{7,15},{8,24},{9,1... | collective-permute-start | bytes 380936 | tf_op jit(solution)/shard_map/send_1_2/ppermute | solution.py:280
  20.6 7.3 %collective-permute-start.14 = (f32[31,8,128]{2,1,0:T(8,128)S(1)}, f32[31,8,128]{2,1,0:T(8,128)S(1)}, u32[]{:S(2)}, u32[]{:S(2)}) collective-permute-start(f32[31,8,128]{2,1,0:T(8,128)S(1)} %merge_2_1.1.own_ref), channel_id=1, source_target_pairs={{0,16},{1,9},{2,18},{3,11},{4,20},{5,13},{6,22},{7,15},{8,24},{9,1... | collective-permute-start | bytes 380936 | tf_op jit(solution)/shard_map/send_2_2/ppermute | solution.py:280
  22.7 7.9 %collective-permute-start.3 = (f32[31,8,128]{2,1,0:T(8,128)S(1)}, f32[31,8,128]{2,1,0:T(8,128)S(1)}, u32[]{:S(2)}, u32[]{:S(2)}) collective-permute-start(f32[31,8,128]{2,1,0:T(8,128)S(1)} %merge_0_2.1.own), channel_id=1, source_target_pairs={{0,16},{1,9},{2,18},{3,11},{4,20},{5,13},{6,22},{7,15},{8,24},{9,1... | collective-permute-start | bytes 380936 | tf_op jit(solution)/shard_map/send_0_3/ppermute | solution.py:280
  24.9 7.4 %collective-permute-start.9 = (f32[31,8,128]{2,1,0:T(8,128)S(1)}, f32[31,8,128]{2,1,0:T(8,128)S(1)}, u32[]{:S(2)}, u32[]{:S(2)}) collective-permute-start(f32[31,8,128]{2,1,0:T(8,128)S(1)} %merge_1_2.1.own), channel_id=1, source_target_pairs={{0,8},{1,3},{2,10},{3,1},{4,12},{5,7},{6,14},{7,5},{8,0},{9,11},{1... | collective-permute-start | bytes 380936 | tf_op jit(solution)/shard_map/send_1_3/ppermute | solution.py:280
  27.9 5.4 %collective-permute-start.15 = (f32[31,8,128]{2,1,0:T(8,128)S(1)}, f32[31,8,128]{2,1,0:T(8,128)S(1)}, u32[]{:S(2)}, u32[]{:S(2)}) collective-permute-start(f32[31,8,128]{2,1,0:T(8,128)S(1)} %merge_2_2.1.own), channel_id=1, source_target_pairs={{0,8},{1,3},{2,10},{3,1},{4,12},{5,7},{6,14},{7,5},{8,0},{9,11},{1... | collective-permute-start | bytes 380936 | tf_op jit(solution)/shard_map/send_2_3/ppermute | solution.py:280
  30.7 4.5 %collective-permute-start.4 = (f32[20,8,128]{2,1,0:T(8,128)S(1)}, f32[20,8,128]{2,1,0:T(8,128)S(1)}, u32[]{:S(2)}, u32[]{:S(2)}) collective-permute-start(f32[20,8,128]{2,1,0:T(8,128)S(1)} %merge_0_3.1.own_ref), channel_id=1, source_target_pairs={{0,2},{1,17},{2,0},{3,19},{4,6},{5,21},{6,4},{7,23},{8,10},{9,25},... | collective-permute-start | bytes 245768 | tf_op jit(solution)/shard_map/send_0_4/ppermute | solution.py:280
  32.3 4.5 %collective-permute-start.10 = (f32[20,8,128]{2,1,0:T(8,128)S(1)}, f32[20,8,128]{2,1,0:T(8,128)S(1)}, u32[]{:S(2)}, u32[]{:S(2)}) collective-permute-start(f32[20,8,128]{2,1,0:T(8,128)S(1)} %merge_1_3.1.own_ref), channel_id=1, source_target_pairs={{0,4},{1,17},{2,6},{3,19},{4,0},{5,21},{6,2},{7,23},{8,12},{9,25},... | collective-permute-start | bytes 245768 | tf_op jit(solution)/shard_map/send_1_4/ppermute | solution.py:280
  33.4 4.5 %collective-permute-start.16 = (f32[20,8,128]{2,1,0:T(8,128)S(1)}, f32[20,8,128]{2,1,0:T(8,128)S(1)}, u32[]{:S(2)}, u32[]{:S(2)}) collective-permute-start(f32[20,8,128]{2,1,0:T(8,128)S(1)} %merge_2_3.1.own_ref), channel_id=1, source_target_pairs={{0,4},{1,17},{2,6},{3,19},{4,0},{5,21},{6,2},{7,23},{8,12},{9,25},... | collective-permute-start | bytes 245768 | tf_op jit(solution)/shard_map/send_2_4/ppermute | solution.py:280
  35.2 5.4 %collective-permute-start.5 = (f32[2,20,8,128]{3,2,1,0:T(8,128)S(1)}, f32[2,20,8,128]{3,2,1,0:T(8,128)S(1)}, u32[]{:S(2)}, u32[]{:S(2)}) collective-permute-start(f32[2,20,8,128]{3,2,1,0:T(8,128)S(1)} %merge_0_4.1.refs_1_), channel_id=1, source_target_pairs={{0,8},{1,5},{2,10},{3,7},{4,12},{5,1},{6,14},{7,3},{8,0},{9,13},{1... | collective-permute-start | bytes 491528 | tf_op jit(solution)/shard_map/send_0_5/ppermute | solution.py:280
  36.9 5.4 %collective-permute-start.11 = (f32[2,20,8,128]{3,2,1,0:T(8,128)S(1)}, f32[2,20,8,128]{3,2,1,0:T(8,128)S(1)}, u32[]{:S(2)}, u32[]{:S(2)}) collective-permute-start(f32[2,20,8,128]{3,2,1,0:T(8,128)S(1)} %merge_1_4.1.refs_3_), channel_id=1, source_target_pairs={{0,2},{1,5},{2,0},{3,7},{4,6},{5,1},{6,4},{7,3},{8,10},{9,13},{10,... | collective-permute-start | bytes 491528 | tf_op jit(solution)/shard_map/send_1_5/ppermute | solution.py:280
  37.9 6.1 %collective-permute-start.17 = (f32[2,20,8,128]{3,2,1,0:T(8,128)S(1)}, f32[2,20,8,128]{3,2,1,0:T(8,128)S(1)}, u32[]{:S(2)}, u32[]{:S(2)}) collective-permute-start(f32[2,20,8,128]{3,2,1,0:T(8,128)S(1)} %merge_2_4.1.refs_5_), channel_id=1, source_target_pairs={{0,2},{1,5},{2,0},{3,7},{4,6},{5,1},{6,4},{7,3},{8,10},{9,13},{10,... | collective-permute-start | bytes 491528 | tf_op jit(solution)/shard_map/send_2_5/ppermute | solution.py:280
  45.9 1.2 %collective-permute-start.18 = (f32[8,128]{1,0:T(8,128)S(1)}, f32[8,128]{1,0:T(8,128)S(1)}, u32[]{:S(2)}, u32[]{:S(2)}) collective-permute-start(f32[8,128]{1,0:T(8,128)S(1)} %get-tuple-element.33), channel_id=1, source_target_pairs={{0,1},{1,0},{2,3},{3,2},{4,5},{5,4},{6,7},{7,6},{8,9},{9,8},{10,11... | collective-permute-start | bytes 12296 | tf_op jit(solution)/shard_map/ppermute | solution.py:319

commit v7 on v6

--- a/solution.py
+++ b/solution.py
@@ -16,10 +16,10 @@
 HALVINGS = 2
 HOURS, HIGH, LOW, TILES = SLOTS, SLOTS + 1, 2 * SLOTS + 1, 3 * SLOTS + 1
 KINDS = (0, HIGH, jnp.add), (HIGH, LOW, jnp.maximum), (LOW, TILES, jnp.minimum)
-ORDERS = (((2, 1), (0, 3), (1, 0), (3, 2)), ((0, 1), (1, 3), (3, 2), (2, 0)), ((0, 1), (1, 3), (3, 2), (2, 0)))
+ORDERS = (((2, 1), (0, 3), (1, 2), (3, 0)), ((0, 1), (1, 3), (3, 0), (2, 2)), ((2, 1), (0, 3), (3, 2), (1, 0)))
 AXES = ("year", "space")
-PIECES = 4
-LATE = 2
+PIECES = 8
+LATE = 4
 TOGETHER = 4
 
 VMEM = pl.BlockSpec(memory_space=pltpu.VMEM)

time: 47.8 us -> 47.5 us (level)
  starting transfers between devices: 27 us -> 26 us
  waiting for transfers between devices: 13.8 us -> 14.6 us
    ppermute x18, starting transfers between devices: 26.9 us -> 25.9 us  [exchange(): lax.ppermute(pltpu.with_memory_space_constraint(x, pltpu.VMEM), AXES, par...]
    ppermute x18, waiting for transfers between devices: 13.7 us -> 14.4 us  [exchange(): lax.ppermute(pltpu.with_memory_space_constraint(x, pltpu.VMEM), AXES, par...]
  transfers between devices with their start and end apart: 19 -> 19, of which waited for: 12 -> 11; matrix products, arithmetic and copies ran while one was open for 0% -> 0% of each run, Pallas kernels for 3% -> 3%
where the time goes in v7:
time: 47.5 us; the launch traced here: 47.3 us
  starting transfers between devices  26 us (55%)
  waiting for transfers between devices  14.6 us (31%)
  Pallas kernels  5.49 us (12%)
  between operations  0.73 us (2%)
  other arithmetic  0.53 us (1%)
    ppermute x18, starting transfers between devices, exchange(): lax.ppermute(pltpu.with_memory_space_constraint(x, pltpu.VMEM), AXES, par...  25.9 us
    ppermute x18, waiting for transfers between devices, exchange(): lax.ppermute(pltpu.with_memory_space_constraint(x, pltpu.VMEM), AXES, par...  14.4 us
    pallas_call x18, Pallas kernels, local_call(): pl.pallas_call(kernel, in_specs=specs, out_shape=out_shape, name=name, co...  5.49 us
  transfers between devices with their start and end apart: 19, of which 11 were waited for; matrix products, arithmetic and copies ran while one was open for 0% of the time, Pallas kernels for 3%

profile of v7, /device:TPU:0, one launch (start us, length us, event | category | flops | bytes accessed | tf_op | source)
XLA Modules:
  0.0 47.3 jit_solution(17585172485054128423)
XLA Ops:
  0.6 2.1 %stats.1 = (f32[2,31,8,128]{3,2,1,0:T(8,128)S(1)}, f32[2,31,8,128]{3,2,1,0:T(8,128)S(1)}, f32[2,31,8,128]{3,2,1,0:T(8,128)S(1)}, f32[2,31,8,128]{3,2,1,0:T(8,128...) custom-call(s32[128]{0:T(128)} %day_in.3, s32[128]{0:T(128)} %tally_in.1, ...), custom_call_target="tpu_custom_call" | custom-call | tf_op jit(solution)/shard_map/stats/pallas_call | solution.py:35
  2.8 3.1 %collective-permute-start = (f32[2,31,8,128]{3,2,1,0:T(8,128)S(1)}, f32[2,31,8,128]{3,2,1,0:T(8,128)S(1)}, u32[]{:S(2)}, u32[]{:S(2)}) collective-permute-start(f32[2,31,8,128]{3,2,1,0:T(8,128)S(1)} %get-tuple-element.19), channel_id=1, source_target_pairs={{0,8},{1,5},{2,10},{3,7},{4,12},{5,1},{6,14},{7,3},{8,0},{9,13},{1... | collective-permute-start | bytes 761864 | tf_op jit(solution)/shard_map/send_0_0/ppermute | solution.py:280
  5.9 1.5 %collective-permute-start.6 = (f32[2,31,8,128]{3,2,1,0:T(8,128)S(1)}, f32[2,31,8,128]{3,2,1,0:T(8,128)S(1)}, u32[]{:S(2)}, u32[]{:S(2)}) collective-permute-start(f32[2,31,8,128]{3,2,1,0:T(8,128)S(1)} %get-tuple-element.23), channel_id=1, source_target_pairs={{0,2},{1,5},{2,0},{3,7},{4,6},{5,1},{6,4},{7,3},{8,10},{9,13},{10,... | collective-permute-start | bytes 761864 | tf_op jit(solution)/shard_map/send_1_0/ppermute | solution.py:280
  7.8 2.3 %collective-permute-done.got_ref = f32[2,31,8,128]{3,2,1,0:T(8,128)S(1)} collective-permute-done((f32[2,31,8,128]{3,2,1,0:T(8,128)S(1)}, f32[2,31,8,128]{3,2,1,0:T(8,128)S(1)}, u32[]{:S(2)}, u32[]{:S(2)}) %collective-permute-start) | collective-permute-done | bytes 253984 | tf_op jit(solution)/shard_map/send_0_0/ppermute | solution.py:280
  10.2 2.0 %collective-permute-start.1 = (f32[31,8,128]{2,1,0:T(8,128)S(1)}, f32[31,8,128]{2,1,0:T(8,128)S(1)}, u32[]{:S(2)}, u32[]{:S(2)}) collective-permute-start(f32[31,8,128]{2,1,0:T(8,128)S(1)} %get-tuple-element.21), channel_id=1, source_target_pairs={{0,2},{1,17},{2,0},{3,19},{4,6},{5,21},{6,4},{7,23},{8,10},{9,25},... | collective-permute-start | bytes 380936 | tf_op jit(solution)/shard_map/send_0_1/ppermute | solution.py:280
  12.2 1.6 %collective-permute-start.7 = (f32[31,8,128]{2,1,0:T(8,128)S(1)}, f32[31,8,128]{2,1,0:T(8,128)S(1)}, u32[]{:S(2)}, u32[]{:S(2)}) collective-permute-start(f32[31,8,128]{2,1,0:T(8,128)S(1)} %get-tuple-element.25), channel_id=1, source_target_pairs={{0,4},{1,17},{2,6},{3,19},{4,0},{5,21},{6,2},{7,23},{8,12},{9,25},... | collective-permute-start | bytes 380936 | tf_op jit(solution)/shard_map/send_1_1/ppermute | solution.py:280
  13.8 1.2 %collective-permute-done.12.got_ref = f32[2,31,8,128]{3,2,1,0:T(8,128)S(1)} collective-permute-done((f32[2,31,8,128]{3,2,1,0:T(8,128)S(1)}, f32[2,31,8,128]{3,2,1,0:T(8,128)S(1)}, u32[]{:S(2)}, u32[]{:S(2)}) %collective-permute-start.12) | collective-permute-done | bytes 253984 | tf_op jit(solution)/shard_map/send_2_0/ppermute | solution.py:280
  15.1 0.9 %collective-permute-start.13 = (f32[31,8,128]{2,1,0:T(8,128)S(1)}, f32[31,8,128]{2,1,0:T(8,128)S(1)}, u32[]{:S(2)}, u32[]{:S(2)}) collective-permute-start(f32[31,8,128]{2,1,0:T(8,128)S(1)} %get-tuple-element.29), channel_id=1, source_target_pairs={{0,2},{1,17},{2,0},{3,19},{4,6},{5,21},{6,4},{7,23},{8,10},{9,25},... | collective-permute-start | bytes 380936 | tf_op jit(solution)/shard_map/send_2_1/ppermute | solution.py:280
  16.0 1.6 %collective-permute-start.2 = (f32[31,8,128]{2,1,0:T(8,128)S(1)}, f32[31,8,128]{2,1,0:T(8,128)S(1)}, u32[]{:S(2)}, u32[]{:S(2)}) collective-permute-start(f32[31,8,128]{2,1,0:T(8,128)S(1)} %merge_0_1.1.own_ref), channel_id=1, source_target_pairs={{0,4},{1,9},{2,6},{3,11},{4,0},{5,13},{6,2},{7,15},{8,12},{9,1},{1... | collective-permute-start | bytes 380936 | tf_op jit(solution)/shard_map/send_0_2/ppermute | solution.py:280
  17.6 2.7 %collective-permute-start.8 = (f32[31,8,128]{2,1,0:T(8,128)S(1)}, f32[31,8,128]{2,1,0:T(8,128)S(1)}, u32[]{:S(2)}, u32[]{:S(2)}) collective-permute-start(f32[31,8,128]{2,1,0:T(8,128)S(1)} %merge_1_1.1.own_ref), channel_id=1, source_target_pairs={{0,16},{1,3},{2,18},{3,1},{4,20},{5,7},{6,22},{7,5},{8,24},{9,11},... | collective-permute-start | bytes 380936 | tf_op jit(solution)/shard_map/send_1_2/ppermute | solution.py:280
  20.4 2.8 %collective-permute-start.14 = (f32[31,8,128]{2,1,0:T(8,128)S(1)}, f32[31,8,128]{2,1,0:T(8,128)S(1)}, u32[]{:S(2)}, u32[]{:S(2)}) collective-permute-start(f32[31,8,128]{2,1,0:T(8,128)S(1)} %merge_2_1.1.own_ref), channel_id=1, source_target_pairs={{0,16},{1,9},{2,18},{3,11},{4,20},{5,13},{6,22},{7,15},{8,24},{9,1... | collective-permute-start | bytes 380936 | tf_op jit(solution)/shard_map/send_2_2/ppermute | solution.py:280
  23.8 1.1 %collective-permute-done.8.got_ref = f32[31,8,128]{2,1,0:T(8,128)S(1)} collective-permute-done((f32[31,8,128]{2,1,0:T(8,128)S(1)}, f32[31,8,128]{2,1,0:T(8,128)S(1)}, u32[]{:S(2)}, u32[]{:S(2)}) %collective-permute-start.8) | collective-permute-done | bytes 127008 | tf_op jit(solution)/shard_map/send_1_2/ppermute | solution.py:280
  25.4 1.8 %collective-permute-done.14.got_ref = f32[31,8,128]{2,1,0:T(8,128)S(1)} collective-permute-done((f32[31,8,128]{2,1,0:T(8,128)S(1)}, f32[31,8,128]{2,1,0:T(8,128)S(1)}, u32[]{:S(2)}, u32[]{:S(2)}) %collective-permute-start.14) | collective-permute-done | bytes 127008 | tf_op jit(solution)/shard_map/send_2_2/ppermute | solution.py:280
  27.2 1.3 %collective-permute-start.15 = (f32[31,8,128]{2,1,0:T(8,128)S(1)}, f32[31,8,128]{2,1,0:T(8,128)S(1)}, u32[]{:S(2)}, u32[]{:S(2)}) collective-permute-start(f32[31,8,128]{2,1,0:T(8,128)S(1)} %merge_2_2.1.own), channel_id=1, source_target_pairs={{0,4},{1,3},{2,6},{3,1},{4,0},{5,7},{6,2},{7,5},{8,12},{9,11},{10,... | collective-permute-start | bytes 380936 | tf_op jit(solution)/shard_map/send_2_3/ppermute | solution.py:280
  28.5 2.1 %collective-permute-done.3.got = f32[31,8,128]{2,1,0:T(8,128)S(1)} collective-permute-done((f32[31,8,128]{2,1,0:T(8,128)S(1)}, f32[31,8,128]{2,1,0:T(8,128)S(1)}, u32[]{:S(2)}, u32[]{:S(2)}) %collective-permute-start.3) | collective-permute-done | bytes 127008 | tf_op jit(solution)/shard_map/send_0_3/ppermute | solution.py:280
  30.7 0.5 %collective-permute-start.4 = (f32[20,8,128]{2,1,0:T(8,128)S(1)}, f32[20,8,128]{2,1,0:T(8,128)S(1)}, u32[]{:S(2)}, u32[]{:S(2)}) collective-permute-start(f32[20,8,128]{2,1,0:T(8,128)S(1)} %merge_0_3.1.own_ref), channel_id=1, source_target_pairs={{0,2},{1,17},{2,0},{3,19},{4,6},{5,21},{6,4},{7,23},{8,10},{9,25},... | collective-permute-start | bytes 245768 | tf_op jit(solution)/shard_map/send_0_4/ppermute | solution.py:280
  31.7 1.6 %collective-permute-start.10 = (f32[20,8,128]{2,1,0:T(8,128)S(1)}, f32[20,8,128]{2,1,0:T(8,128)S(1)}, u32[]{:S(2)}, u32[]{:S(2)}) collective-permute-start(f32[20,8,128]{2,1,0:T(8,128)S(1)} %merge_1_3.1.own_ref), channel_id=1, source_target_pairs={{0,4},{1,17},{2,6},{3,19},{4,0},{5,21},{6,2},{7,23},{8,12},{9,25},... | collective-permute-start | bytes 245768 | tf_op jit(solution)/shard_map/send_1_4/ppermute | solution.py:280
  33.4 2.4 %collective-permute-start.16 = (f32[20,8,128]{2,1,0:T(8,128)S(1)}, f32[20,8,128]{2,1,0:T(8,128)S(1)}, u32[]{:S(2)}, u32[]{:S(2)}) collective-permute-start(f32[20,8,128]{2,1,0:T(8,128)S(1)} %merge_2_3.1.own_ref), channel_id=1, source_target_pairs={{0,2},{1,17},{2,0},{3,19},{4,6},{5,21},{6,4},{7,23},{8,10},{9,25},... | collective-permute-start | bytes 245768 | tf_op jit(solution)/shard_map/send_2_4/ppermute | solution.py:280
  36.3 2.0 %collective-permute-start.11 = (f32[2,20,8,128]{3,2,1,0:T(8,128)S(1)}, f32[2,20,8,128]{3,2,1,0:T(8,128)S(1)}, u32[]{:S(2)}, u32[]{:S(2)}) collective-permute-start(f32[2,20,8,128]{3,2,1,0:T(8,128)S(1)} %merge_1_4.1.refs_3_), channel_id=1, source_target_pairs={{0,2},{1,5},{2,0},{3,7},{4,6},{5,1},{6,4},{7,3},{8,10},{9,13},{10,... | collective-permute-start | bytes 491528 | tf_op jit(solution)/shard_map/send_1_5/ppermute | solution.py:280
  38.6 2.6 %collective-permute-done.5.refs_0_ = f32[2,20,8,128]{3,2,1,0:T(8,128)S(1)} collective-permute-done((f32[2,20,8,128]{3,2,1,0:T(8,128)S(1)}, f32[2,20,8,128]{3,2,1,0:T(8,128)S(1)}, u32[]{:S(2)}, u32[]{:S(2)}) %collective-permute-start.5) | collective-permute-done | bytes 163872 | tf_op jit(solution)/shard_map/send_0_5/ppermute | solution.py:280
  41.7 2.0 %collective-permute-done.17.refs_4_ = f32[2,20,8,128]{3,2,1,0:T(8,128)S(1)} collective-permute-done((f32[2,20,8,128]{3,2,1,0:T(8,128)S(1)}, f32[2,20,8,128]{3,2,1,0:T(8,128)S(1)}, u32[]{:S(2)}, u32[]{:S(2)}) %collective-permute-start.17) | collective-permute-done | bytes 163872 | tf_op jit(solution)/shard_map/send_2_5/ppermute | solution.py:280
  43.7 1.8 %depart.1 = (f32[8,256,128]{2,1,0:T(8,128)S(1)}, f32[8,128]{1,0:T(8,128)S(1)}, f32[16,256,128]{2,1,0:T(8,128)}) custom-call(s32[128]{0:T(128)S(1)} %copy-done.1, f32[16,256,128]{2,1,0:T(8,128)S(1)} %get-tuple-element.18.x_ref, f32[32,128]{1,0:T(8,128)S(1)} %bitcast.13, f32[2,20,8,128]{3,2,1,0:T(8,128)S(1)} %collective-permute-done.5.refs_0_, ...), custom_call_target="tpu_custom_call" | custom-call | tf_op jit(solution)/shard_map/depart/pallas_call | solution.py:35
  45.6 1.0 %emit.1 = f32[16,256,128]{2,1,0:T(8,128)} custom-call(f32[8,256,128]{2,1,0:T(8,128)S(1)} %get-tuple-element.31.part_ref, f32[16,256,128]{2,1,0:T(8,128)} %get-tuple-element.32.before_ref), custom_call_target="tpu_custom_call", output_to_operand_aliasing={{}: (1, {})} | custom-call | tf_op jit(solution)/shard_map/emit/pallas_call | solution.py:35
  46.8 0.5 %fusion = f32[128]{0:T(128)} fusion(f32[8,128]{1,0:T(8,128)S(1)} %add.3), kind=kLoop, calls=%fused_computation.1 | loop fusion | flops 128 | bytes 1536 | tf_op jit(solution)/shard_map/div | solution.py:323
  (38 shorter events, 3.8 us)
Async XLA Ops:
  2.8 7.4 %collective-permute-start = (f32[2,31,8,128]{3,2,1,0:T(8,128)S(1)}, f32[2,31,8,128]{3,2,1,0:T(8,128)S(1)}, u32[]{:S(2)}, u32[]{:S(2)}) collective-permute-start(f32[2,31,8,128]{3,2,1,0:T(8,128)S(1)} %get-tuple-element.19), channel_id=1, source_target_pairs={{0,8},{1,5},{2,10},{3,7},{4,12},{5,1},{6,14},{7,3},{8,0},{9,13},{1... | collective-permute-start | bytes 761864 | tf_op jit(solution)/shard_map/send_0_0/ppermute | solution.py:280
  5.9 6.3 %collective-permute-start.6 = (f32[2,31,8,128]{3,2,1,0:T(8,128)S(1)}, f32[2,31,8,128]{3,2,1,0:T(8,128)S(1)}, u32[]{:S(2)}, u32[]{:S(2)}) collective-permute-start(f32[2,31,8,128]{3,2,1,0:T(8,128)S(1)} %get-tuple-element.23), channel_id=1, source_target_pairs={{0,2},{1,5},{2,0},{3,7},{4,6},{5,1},{6,4},{7,3},{8,10},{9,13},{10,... | collective-permute-start | bytes 761864 | tf_op jit(solution)/shard_map/send_1_0/ppermute | solution.py:280
  7.4 7.6 %collective-permute-start.12 = (f32[2,31,8,128]{3,2,1,0:T(8,128)S(1)}, f32[2,31,8,128]{3,2,1,0:T(8,128)S(1)}, u32[]{:S(2)}, u32[]{:S(2)}) collective-permute-start(f32[2,31,8,128]{3,2,1,0:T(8,128)S(1)} %get-tuple-element.27), channel_id=1, source_target_pairs={{0,8},{1,5},{2,10},{3,7},{4,12},{5,1},{6,14},{7,3},{8,0},{9,13},{1... | collective-permute-start | bytes 761864 | tf_op jit(solution)/shard_map/send_2_0/ppermute | solution.py:280
  10.2 5.8 %collective-permute-start.1 = (f32[31,8,128]{2,1,0:T(8,128)S(1)}, f32[31,8,128]{2,1,0:T(8,128)S(1)}, u32[]{:S(2)}, u32[]{:S(2)}) collective-permute-start(f32[31,8,128]{2,1,0:T(8,128)S(1)} %get-tuple-element.21), channel_id=1, source_target_pairs={{0,2},{1,17},{2,0},{3,19},{4,6},{5,21},{6,4},{7,23},{8,10},{9,25},... | collective-permute-start | bytes 380936 | tf_op jit(solution)/shard_map/send_0_1/ppermute | solution.py:280
  12.2 5.4 %collective-permute-start.7 = (f32[31,8,128]{2,1,0:T(8,128)S(1)}, f32[31,8,128]{2,1,0:T(8,128)S(1)}, u32[]{:S(2)}, u32[]{:S(2)}) collective-permute-start(f32[31,8,128]{2,1,0:T(8,128)S(1)} %get-tuple-element.25), channel_id=1, source_target_pairs={{0,4},{1,17},{2,6},{3,19},{4,0},{5,21},{6,2},{7,23},{8,12},{9,25},... | collective-permute-start | bytes 380936 | tf_op jit(solution)/shard_map/send_1_1/ppermute | solution.py:280
  15.1 5.3 %collective-permute-start.13 = (f32[31,8,128]{2,1,0:T(8,128)S(1)}, f32[31,8,128]{2,1,0:T(8,128)S(1)}, u32[]{:S(2)}, u32[]{:S(2)}) collective-permute-start(f32[31,8,128]{2,1,0:T(8,128)S(1)} %get-tuple-element.29), channel_id=1, source_target_pairs={{0,2},{1,17},{2,0},{3,19},{4,6},{5,21},{6,4},{7,23},{8,10},{9,25},... | collective-permute-start | bytes 380936 | tf_op jit(solution)/shard_map/send_2_1/ppermute | solution.py:280
  16.0 27.7 %copy-start = (f32[4096]{0:T(1024)S(1)}, f32[4096]{0:T(1024)}, u32[]{:S(2)}) copy-start(f32[4096]{0:T(1024)} %param.7) | copy-start | bytes 49156
  16.0 27.7 %copy-start.1 = (s32[128]{0:T(128)S(1)}, s32[128]{0:T(128)}, u32[]{:S(2)}) copy-start(s32[128]{0:T(128)} %day_in.3) | copy-start | bytes 1540
  16.0 7.2 %collective-permute-start.2 = (f32[31,8,128]{2,1,0:T(8,128)S(1)}, f32[31,8,128]{2,1,0:T(8,128)S(1)}, u32[]{:S(2)}, u32[]{:S(2)}) collective-permute-start(f32[31,8,128]{2,1,0:T(8,128)S(1)} %merge_0_1.1.own_ref), channel_id=1, source_target_pairs={{0,4},{1,9},{2,6},{3,11},{4,0},{5,13},{6,2},{7,15},{8,12},{9,1},{1... | collective-permute-start | bytes 380936 | tf_op jit(solution)/shard_map/send_0_2/ppermute | solution.py:280
  17.6 7.3 %collective-permute-start.8 = (f32[31,8,128]{2,1,0:T(8,128)S(1)}, f32[31,8,128]{2,1,0:T(8,128)S(1)}, u32[]{:S(2)}, u32[]{:S(2)}) collective-permute-start(f32[31,8,128]{2,1,0:T(8,128)S(1)} %merge_1_1.1.own_ref), channel_id=1, source_target_pairs={{0,16},{1,3},{2,18},{3,1},{4,20},{5,7},{6,22},{7,5},{8,24},{9,11},... | collective-permute-start | bytes 380936 | tf_op jit(solution)/shard_map/send_1_2/ppermute | solution.py:280
  20.4 6.8 %collective-permute-start.14 = (f32[31,8,128]{2,1,0:T(8,128)S(1)}, f32[31,8,128]{2,1,0:T(8,128)S(1)}, u32[]{:S(2)}, u32[]{:S(2)}) collective-permute-start(f32[31,8,128]{2,1,0:T(8,128)S(1)} %merge_2_1.1.own_ref), channel_id=1, source_target_pairs={{0,16},{1,9},{2,18},{3,11},{4,20},{5,13},{6,22},{7,15},{8,24},{9,1... | collective-permute-start | bytes 380936 | tf_op jit(solution)/shard_map/send_2_2/ppermute | solution.py:280
  23.2 7.4 %collective-permute-start.3 = (f32[31,8,128]{2,1,0:T(8,128)S(1)}, f32[31,8,128]{2,1,0:T(8,128)S(1)}, u32[]{:S(2)}, u32[]{:S(2)}) collective-permute-start(f32[31,8,128]{2,1,0:T(8,128)S(1)} %merge_0_2.1.own), channel_id=1, source_target_pairs={{0,16},{1,3},{2,18},{3,1},{4,20},{5,7},{6,22},{7,5},{8,24},{9,11},... | collective-permute-start | bytes 380936 | tf_op jit(solution)/shard_map/send_0_3/ppermute | solution.py:280
  24.9 6.7 %collective-permute-start.9 = (f32[31,8,128]{2,1,0:T(8,128)S(1)}, f32[31,8,128]{2,1,0:T(8,128)S(1)}, u32[]{:S(2)}, u32[]{:S(2)}) collective-permute-start(f32[31,8,128]{2,1,0:T(8,128)S(1)} %merge_1_2.1.own), channel_id=1, source_target_pairs={{0,8},{1,9},{2,10},{3,11},{4,12},{5,13},{6,14},{7,15},{8,0},{9,1},... | collective-permute-start | bytes 380936 | tf_op jit(solution)/shard_map/send_1_3/ppermute | solution.py:280
  27.2 6.1 %collective-permute-start.15 = (f32[31,8,128]{2,1,0:T(8,128)S(1)}, f32[31,8,128]{2,1,0:T(8,128)S(1)}, u32[]{:S(2)}, u32[]{:S(2)}) collective-permute-start(f32[31,8,128]{2,1,0:T(8,128)S(1)} %merge_2_2.1.own), channel_id=1, source_target_pairs={{0,4},{1,3},{2,6},{3,1},{4,0},{5,7},{6,2},{7,5},{8,12},{9,11},{10,... | collective-permute-start | bytes 380936 | tf_op jit(solution)/shard_map/send_2_3/ppermute | solution.py:280
  30.7 5.1 %collective-permute-start.4 = (f32[20,8,128]{2,1,0:T(8,128)S(1)}, f32[20,8,128]{2,1,0:T(8,128)S(1)}, u32[]{:S(2)}, u32[]{:S(2)}) collective-permute-start(f32[20,8,128]{2,1,0:T(8,128)S(1)} %merge_0_3.1.own_ref), channel_id=1, source_target_pairs={{0,2},{1,17},{2,0},{3,19},{4,6},{5,21},{6,4},{7,23},{8,10},{9,25},... | collective-permute-start | bytes 245768 | tf_op jit(solution)/shard_map/send_0_4/ppermute | solution.py:280
  31.7 4.5 %collective-permute-start.10 = (f32[20,8,128]{2,1,0:T(8,128)S(1)}, f32[20,8,128]{2,1,0:T(8,128)S(1)}, u32[]{:S(2)}, u32[]{:S(2)}) collective-permute-start(f32[20,8,128]{2,1,0:T(8,128)S(1)} %merge_1_3.1.own_ref), channel_id=1, source_target_pairs={{0,4},{1,17},{2,6},{3,19},{4,0},{5,21},{6,2},{7,23},{8,12},{9,25},... | collective-permute-start | bytes 245768 | tf_op jit(solution)/shard_map/send_1_4/ppermute | solution.py:280
  33.4 4.9 %collective-permute-start.16 = (f32[20,8,128]{2,1,0:T(8,128)S(1)}, f32[20,8,128]{2,1,0:T(8,128)S(1)}, u32[]{:S(2)}, u32[]{:S(2)}) collective-permute-start(f32[20,8,128]{2,1,0:T(8,128)S(1)} %merge_2_3.1.own_ref), channel_id=1, source_target_pairs={{0,2},{1,17},{2,0},{3,19},{4,6},{5,21},{6,4},{7,23},{8,10},{9,25},... | collective-permute-start | bytes 245768 | tf_op jit(solution)/shard_map/send_2_4/ppermute | solution.py:280
  35.8 5.4 %collective-permute-start.5 = (f32[2,20,8,128]{3,2,1,0:T(8,128)S(1)}, f32[2,20,8,128]{3,2,1,0:T(8,128)S(1)}, u32[]{:S(2)}, u32[]{:S(2)}) collective-permute-start(f32[2,20,8,128]{3,2,1,0:T(8,128)S(1)} %merge_0_4.1.refs_1_), channel_id=1, source_target_pairs={{0,8},{1,5},{2,10},{3,7},{4,12},{5,1},{6,14},{7,3},{8,0},{9,13},{1... | collective-permute-start | bytes 491528 | tf_op jit(solution)/shard_map/send_0_5/ppermute | solution.py:280
  36.3 5.4 %collective-permute-start.11 = (f32[2,20,8,128]{3,2,1,0:T(8,128)S(1)}, f32[2,20,8,128]{3,2,1,0:T(8,128)S(1)}, u32[]{:S(2)}, u32[]{:S(2)}) collective-permute-start(f32[2,20,8,128]{3,2,1,0:T(8,128)S(1)} %merge_1_4.1.refs_3_), channel_id=1, source_target_pairs={{0,2},{1,5},{2,0},{3,7},{4,6},{5,1},{6,4},{7,3},{8,10},{9,13},{10,... | collective-permute-start | bytes 491528 | tf_op jit(solution)/shard_map/send_1_5/ppermute | solution.py:280
  38.3 5.4 %collective-permute-start.17 = (f32[2,20,8,128]{3,2,1,0:T(8,128)S(1)}, f32[2,20,8,128]{3,2,1,0:T(8,128)S(1)}, u32[]{:S(2)}, u32[]{:S(2)}) collective-permute-start(f32[2,20,8,128]{3,2,1,0:T(8,128)S(1)} %merge_2_4.1.refs_5_), channel_id=1, source_target_pairs={{0,8},{1,5},{2,10},{3,7},{4,12},{5,1},{6,14},{7,3},{8,0},{9,13},{1... | collective-permute-start | bytes 491528 | tf_op jit(solution)/shard_map/send_2_5/ppermute | solution.py:280
  45.5 1.2 %collective-permute-start.18 = (f32[8,128]{1,0:T(8,128)S(1)}, f32[8,128]{1,0:T(8,128)S(1)}, u32[]{:S(2)}, u32[]{:S(2)}) collective-permute-start(f32[8,128]{1,0:T(8,128)S(1)} %get-tuple-element.33), channel_id=1, source_target_pairs={{0,1},{1,0},{2,3},{3,2},{4,5},{5,4},{6,7},{7,6},{8,9},{9,8},{10,11... | collective-permute-start | bytes 12296 | tf_op jit(solution)/shard_map/ppermute | solution.py:319

commit v8 on v7

--- a/solution.py
+++ b/solution.py
@@ -16,11 +16,11 @@
 HALVINGS = 2
 HOURS, HIGH, LOW, TILES = SLOTS, SLOTS + 1, 2 * SLOTS + 1, 3 * SLOTS + 1
 KINDS = (0, HIGH, jnp.add), (HIGH, LOW, jnp.maximum), (LOW, TILES, jnp.minimum)
-ORDERS = (((2, 1), (0, 3), (1, 2), (3, 0)), ((0, 1), (1, 3), (3, 0), (2, 2)), ((2, 1), (0, 3), (3, 2), (1, 0)))
+ORDERS = (((2, 1), (0, 3), (1, 2), (3, 0)), ((0, 1), (2, 3), (3, 0), (1, 2)), ((2, 1), (0, 3), (3, 2), (1, 0)))
 AXES = ("year", "space")
 PIECES = 8
 LATE = 4
-TOGETHER = 4
+TOGETHER = 2
 
 VMEM = pl.BlockSpec(memory_space=pltpu.VMEM)
 SMEM = pl.BlockSpec(memory_space=pltpu.SMEM)

time: 47.5 us -> 47.4 us (level)
  no operation moved by 1% of the time
where the time goes in v8:
time: 47.4 us; the launch traced here: 47.2 us
  starting transfers between devices  26.3 us (55%)
  waiting for transfers between devices  14.2 us (30%)
  Pallas kernels  5.49 us (12%)
  between operations  0.73 us (2%)
  other arithmetic  0.53 us (1%)
    ppermute x18, starting transfers between devices, exchange(): lax.ppermute(pltpu.with_memory_space_constraint(x, pltpu.VMEM), AXES, par...  26.2 us
    ppermute x18, waiting for transfers between devices, exchange(): lax.ppermute(pltpu.with_memory_space_constraint(x, pltpu.VMEM), AXES, par...  14.1 us
    pallas_call x18, Pallas kernels, local_call(): pl.pallas_call(kernel, in_specs=specs, out_shape=out_shape, name=name, co...  5.49 us
  transfers between devices with their start and end apart: 19, of which 11 were waited for; matrix products, arithmetic and copies ran while one was open for 0% of the time, Pallas kernels for 3%

profile of v8, /device:TPU:0, one launch (start us, length us, event | category | flops | bytes accessed | tf_op | source)
XLA Modules:
  0.0 47.2 jit_solution(10951721078461367305)
XLA Ops:
  0.6 2.1 %stats.1 = (f32[2,31,8,128]{3,2,1,0:T(8,128)S(1)}, f32[2,31,8,128]{3,2,1,0:T(8,128)S(1)}, f32[2,31,8,128]{3,2,1,0:T(8,128)S(1)}, f32[2,31,8,128]{3,2,1,0:T(8,128...) custom-call(s32[128]{0:T(128)} %day_in.3, s32[128]{0:T(128)} %tally_in.1, ...), custom_call_target="tpu_custom_call" | custom-call | tf_op jit(solution)/shard_map/stats/pallas_call | solution.py:35
  2.8 3.1 %collective-permute-start = (f32[2,31,8,128]{3,2,1,0:T(8,128)S(1)}, f32[2,31,8,128]{3,2,1,0:T(8,128)S(1)}, u32[]{:S(2)}, u32[]{:S(2)}) collective-permute-start(f32[2,31,8,128]{3,2,1,0:T(8,128)S(1)} %get-tuple-element.19), channel_id=1, source_target_pairs={{0,8},{1,5},{2,10},{3,7},{4,12},{5,1},{6,14},{7,3},{8,0},{9,13},{1... | collective-permute-start | bytes 761864 | tf_op jit(solution)/shard_map/send_0_0/ppermute | solution.py:280
  5.9 1.5 %collective-permute-start.6 = (f32[2,31,8,128]{3,2,1,0:T(8,128)S(1)}, f32[2,31,8,128]{3,2,1,0:T(8,128)S(1)}, u32[]{:S(2)}, u32[]{:S(2)}) collective-permute-start(f32[2,31,8,128]{3,2,1,0:T(8,128)S(1)} %get-tuple-element.23), channel_id=1, source_target_pairs={{0,2},{1,5},{2,0},{3,7},{4,6},{5,1},{6,4},{7,3},{8,10},{9,13},{10,... | collective-permute-start | bytes 761864 | tf_op jit(solution)/shard_map/send_1_0/ppermute | solution.py:280
  7.8 2.3 %collective-permute-done.got_ref = f32[2,31,8,128]{3,2,1,0:T(8,128)S(1)} collective-permute-done((f32[2,31,8,128]{3,2,1,0:T(8,128)S(1)}, f32[2,31,8,128]{3,2,1,0:T(8,128)S(1)}, u32[]{:S(2)}, u32[]{:S(2)}) %collective-permute-start) | collective-permute-done | bytes 253984 | tf_op jit(solution)/shard_map/send_0_0/ppermute | solution.py:280
  10.2 2.0 %collective-permute-start.1 = (f32[31,8,128]{2,1,0:T(8,128)S(1)}, f32[31,8,128]{2,1,0:T(8,128)S(1)}, u32[]{:S(2)}, u32[]{:S(2)}) collective-permute-start(f32[31,8,128]{2,1,0:T(8,128)S(1)} %get-tuple-element.21), channel_id=1, source_target_pairs={{0,2},{1,17},{2,0},{3,19},{4,6},{5,21},{6,4},{7,23},{8,10},{9,25},... | collective-permute-start | bytes 380936 | tf_op jit(solution)/shard_map/send_0_1/ppermute | solution.py:280
  12.2 1.6 %collective-permute-start.7 = (f32[31,8,128]{2,1,0:T(8,128)S(1)}, f32[31,8,128]{2,1,0:T(8,128)S(1)}, u32[]{:S(2)}, u32[]{:S(2)}) collective-permute-start(f32[31,8,128]{2,1,0:T(8,128)S(1)} %get-tuple-element.25), channel_id=1, source_target_pairs={{0,8},{1,17},{2,10},{3,19},{4,12},{5,21},{6,14},{7,23},{8,0},{9,25... | collective-permute-start | bytes 380936 | tf_op jit(solution)/shard_map/send_1_1/ppermute | solution.py:280
  13.9 1.2 %collective-permute-done.12.got_ref = f32[2,31,8,128]{3,2,1,0:T(8,128)S(1)} collective-permute-done((f32[2,31,8,128]{3,2,1,0:T(8,128)S(1)}, f32[2,31,8,128]{3,2,1,0:T(8,128)S(1)}, u32[]{:S(2)}, u32[]{:S(2)}) %collective-permute-start.12) | collective-permute-done | bytes 253984 | tf_op jit(solution)/shard_map/send_2_0/ppermute | solution.py:280
  15.1 0.9 %collective-permute-start.13 = (f32[31,8,128]{2,1,0:T(8,128)S(1)}, f32[31,8,128]{2,1,0:T(8,128)S(1)}, u32[]{:S(2)}, u32[]{:S(2)}) collective-permute-start(f32[31,8,128]{2,1,0:T(8,128)S(1)} %get-tuple-element.29), channel_id=1, source_target_pairs={{0,2},{1,17},{2,0},{3,19},{4,6},{5,21},{6,4},{7,23},{8,10},{9,25},... | collective-permute-start | bytes 380936 | tf_op jit(solution)/shard_map/send_2_1/ppermute | solution.py:280
  16.0 1.6 %collective-permute-start.2 = (f32[31,8,128]{2,1,0:T(8,128)S(1)}, f32[31,8,128]{2,1,0:T(8,128)S(1)}, u32[]{:S(2)}, u32[]{:S(2)}) collective-permute-start(f32[31,8,128]{2,1,0:T(8,128)S(1)} %merge_0_1.1.own_ref), channel_id=1, source_target_pairs={{0,4},{1,9},{2,6},{3,11},{4,0},{5,13},{6,2},{7,15},{8,12},{9,1},{1... | collective-permute-start | bytes 380936 | tf_op jit(solution)/shard_map/send_0_2/ppermute | solution.py:280
  18.0 2.6 %collective-permute-start.8 = (f32[31,8,128]{2,1,0:T(8,128)S(1)}, f32[31,8,128]{2,1,0:T(8,128)S(1)}, u32[]{:S(2)}, u32[]{:S(2)}) collective-permute-start(f32[31,8,128]{2,1,0:T(8,128)S(1)} %merge_1_1.1.own_ref), channel_id=1, source_target_pairs={{0,16},{1,3},{2,18},{3,1},{4,20},{5,7},{6,22},{7,5},{8,24},{9,11},... | collective-permute-start | bytes 380936 | tf_op jit(solution)/shard_map/send_1_2/ppermute | solution.py:280
  20.6 2.3 %collective-permute-start.14 = (f32[31,8,128]{2,1,0:T(8,128)S(1)}, f32[31,8,128]{2,1,0:T(8,128)S(1)}, u32[]{:S(2)}, u32[]{:S(2)}) collective-permute-start(f32[31,8,128]{2,1,0:T(8,128)S(1)} %merge_2_1.1.own_ref), channel_id=1, source_target_pairs={{0,16},{1,9},{2,18},{3,11},{4,20},{5,13},{6,22},{7,15},{8,24},{9,1... | collective-permute-start | bytes 380936 | tf_op jit(solution)/shard_map/send_2_2/ppermute | solution.py:280
  22.9 0.9 %collective-permute-start.3 = (f32[31,8,128]{2,1,0:T(8,128)S(1)}, f32[31,8,128]{2,1,0:T(8,128)S(1)}, u32[]{:S(2)}, u32[]{:S(2)}) collective-permute-start(f32[31,8,128]{2,1,0:T(8,128)S(1)} %merge_0_2.1.own), channel_id=1, source_target_pairs={{0,16},{1,3},{2,18},{3,1},{4,20},{5,7},{6,22},{7,5},{8,24},{9,11},... | collective-permute-start | bytes 380936 | tf_op jit(solution)/shard_map/send_0_3/ppermute | solution.py:280
  23.9 1.6 %collective-permute-start.9 = (f32[31,8,128]{2,1,0:T(8,128)S(1)}, f32[31,8,128]{2,1,0:T(8,128)S(1)}, u32[]{:S(2)}, u32[]{:S(2)}) collective-permute-start(f32[31,8,128]{2,1,0:T(8,128)S(1)} %merge_1_2.1.own), channel_id=1, source_target_pairs={{0,4},{1,9},{2,6},{3,11},{4,0},{5,13},{6,2},{7,15},{8,12},{9,1},{1... | collective-permute-start | bytes 380936 | tf_op jit(solution)/shard_map/send_1_3/ppermute | solution.py:280
  25.5 1.3 %collective-permute-done.14.got_ref = f32[31,8,128]{2,1,0:T(8,128)S(1)} collective-permute-done((f32[31,8,128]{2,1,0:T(8,128)S(1)}, f32[31,8,128]{2,1,0:T(8,128)S(1)}, u32[]{:S(2)}, u32[]{:S(2)}) %collective-permute-start.14) | collective-permute-done | bytes 127008 | tf_op jit(solution)/shard_map/send_2_2/ppermute | solution.py:280
  26.8 1.6 %collective-permute-start.15 = (f32[31,8,128]{2,1,0:T(8,128)S(1)}, f32[31,8,128]{2,1,0:T(8,128)S(1)}, u32[]{:S(2)}, u32[]{:S(2)}) collective-permute-start(f32[31,8,128]{2,1,0:T(8,128)S(1)} %merge_2_2.1.own), channel_id=1, source_target_pairs={{0,4},{1,3},{2,6},{3,1},{4,0},{5,7},{6,2},{7,5},{8,12},{9,11},{10,... | collective-permute-start | bytes 380936 | tf_op jit(solution)/shard_map/send_2_3/ppermute | solution.py:280
  28.4 2.7 %collective-permute-done.3.got = f32[31,8,128]{2,1,0:T(8,128)S(1)} collective-permute-done((f32[31,8,128]{2,1,0:T(8,128)S(1)}, f32[31,8,128]{2,1,0:T(8,128)S(1)}, u32[]{:S(2)}, u32[]{:S(2)}) %collective-permute-start.3) | collective-permute-done | bytes 127008 | tf_op jit(solution)/shard_map/send_0_3/ppermute | solution.py:280
  31.4 2.0 %collective-permute-start.10 = (f32[20,8,128]{2,1,0:T(8,128)S(1)}, f32[20,8,128]{2,1,0:T(8,128)S(1)}, u32[]{:S(2)}, u32[]{:S(2)}) collective-permute-start(f32[20,8,128]{2,1,0:T(8,128)S(1)} %merge_1_3.1.own_ref), channel_id=1, source_target_pairs={{0,8},{1,17},{2,10},{3,19},{4,12},{5,21},{6,14},{7,23},{8,0},{9,25... | collective-permute-start | bytes 245768 | tf_op jit(solution)/shard_map/send_1_4/ppermute | solution.py:280
  34.1 1.6 %collective-permute-done.4.got_ref = f32[20,8,128]{2,1,0:T(8,128)S(1)} collective-permute-done((f32[20,8,128]{2,1,0:T(8,128)S(1)}, f32[20,8,128]{2,1,0:T(8,128)S(1)}, u32[]{:S(2)}, u32[]{:S(2)}) %collective-permute-start.4) | collective-permute-done | bytes 81952 | tf_op jit(solution)/shard_map/send_0_4/ppermute | solution.py:280
  36.3 2.0 %collective-permute-start.11 = (f32[2,20,8,128]{3,2,1,0:T(8,128)S(1)}, f32[2,20,8,128]{3,2,1,0:T(8,128)S(1)}, u32[]{:S(2)}, u32[]{:S(2)}) collective-permute-start(f32[2,20,8,128]{3,2,1,0:T(8,128)S(1)} %merge_1_4.1.refs_3_), channel_id=1, source_target_pairs={{0,2},{1,5},{2,0},{3,7},{4,6},{5,1},{6,4},{7,3},{8,10},{9,13},{10,... | collective-permute-start | bytes 491528 | tf_op jit(solution)/shard_map/send_1_5/ppermute | solution.py:280
  38.3 0.9 %collective-permute-start.17 = (f32[2,20,8,128]{3,2,1,0:T(8,128)S(1)}, f32[2,20,8,128]{3,2,1,0:T(8,128)S(1)}, u32[]{:S(2)}, u32[]{:S(2)}) collective-permute-start(f32[2,20,8,128]{3,2,1,0:T(8,128)S(1)} %merge_2_4.1.refs_5_), channel_id=1, source_target_pairs={{0,8},{1,5},{2,10},{3,7},{4,12},{5,1},{6,14},{7,3},{8,0},{9,13},{1... | collective-permute-start | bytes 491528 | tf_op jit(solution)/shard_map/send_2_5/ppermute | solution.py:280
  39.2 1.9 %collective-permute-done.5.refs_0_ = f32[2,20,8,128]{3,2,1,0:T(8,128)S(1)} collective-permute-done((f32[2,20,8,128]{3,2,1,0:T(8,128)S(1)}, f32[2,20,8,128]{3,2,1,0:T(8,128)S(1)}, u32[]{:S(2)}, u32[]{:S(2)}) %collective-permute-start.5) | collective-permute-done | bytes 163872 | tf_op jit(solution)/shard_map/send_0_5/ppermute | solution.py:280
  41.6 2.0 %collective-permute-done.17.refs_4_ = f32[2,20,8,128]{3,2,1,0:T(8,128)S(1)} collective-permute-done((f32[2,20,8,128]{3,2,1,0:T(8,128)S(1)}, f32[2,20,8,128]{3,2,1,0:T(8,128)S(1)}, u32[]{:S(2)}, u32[]{:S(2)}) %collective-permute-start.17) | collective-permute-done | bytes 163872 | tf_op jit(solution)/shard_map/send_2_5/ppermute | solution.py:280
  43.6 1.8 %depart.1 = (f32[8,256,128]{2,1,0:T(8,128)S(1)}, f32[8,128]{1,0:T(8,128)S(1)}, f32[16,256,128]{2,1,0:T(8,128)}) custom-call(s32[128]{0:T(128)S(1)} %copy-done.1, f32[16,256,128]{2,1,0:T(8,128)S(1)} %get-tuple-element.18.x_ref, f32[32,128]{1,0:T(8,128)S(1)} %bitcast.13, f32[2,20,8,128]{3,2,1,0:T(8,128)S(1)} %collective-permute-done.5.refs_0_, ...), custom_call_target="tpu_custom_call" | custom-call | tf_op jit(solution)/shard_map/depart/pallas_call | solution.py:35
  45.6 1.0 %emit.1 = f32[16,256,128]{2,1,0:T(8,128)} custom-call(f32[8,256,128]{2,1,0:T(8,128)S(1)} %get-tuple-element.31.part_ref, f32[16,256,128]{2,1,0:T(8,128)} %get-tuple-element.32.before_ref), custom_call_target="tpu_custom_call", output_to_operand_aliasing={{}: (1, {})} | custom-call | tf_op jit(solution)/shard_map/emit/pallas_call | solution.py:35
  (38 shorter events, 3.9 us)
Async XLA Ops:
  2.8 7.4 %collective-permute-start = (f32[2,31,8,128]{3,2,1,0:T(8,128)S(1)}, f32[2,31,8,128]{3,2,1,0:T(8,128)S(1)}, u32[]{:S(2)}, u32[]{:S(2)}) collective-permute-start(f32[2,31,8,128]{3,2,1,0:T(8,128)S(1)} %get-tuple-element.19), channel_id=1, source_target_pairs={{0,8},{1,5},{2,10},{3,7},{4,12},{5,1},{6,14},{7,3},{8,0},{9,13},{1... | collective-permute-start | bytes 761864 | tf_op jit(solution)/shard_map/send_0_0/ppermute | solution.py:280
  5.9 6.3 %collective-permute-start.6 = (f32[2,31,8,128]{3,2,1,0:T(8,128)S(1)}, f32[2,31,8,128]{3,2,1,0:T(8,128)S(1)}, u32[]{:S(2)}, u32[]{:S(2)}) collective-permute-start(f32[2,31,8,128]{3,2,1,0:T(8,128)S(1)} %get-tuple-element.23), channel_id=1, source_target_pairs={{0,2},{1,5},{2,0},{3,7},{4,6},{5,1},{6,4},{7,3},{8,10},{9,13},{10,... | collective-permute-start | bytes 761864 | tf_op jit(solution)/shard_map/send_1_0/ppermute | solution.py:280
  7.4 7.6 %collective-permute-start.12 = (f32[2,31,8,128]{3,2,1,0:T(8,128)S(1)}, f32[2,31,8,128]{3,2,1,0:T(8,128)S(1)}, u32[]{:S(2)}, u32[]{:S(2)}) collective-permute-start(f32[2,31,8,128]{3,2,1,0:T(8,128)S(1)} %get-tuple-element.27), channel_id=1, source_target_pairs={{0,8},{1,5},{2,10},{3,7},{4,12},{5,1},{6,14},{7,3},{8,0},{9,13},{1... | collective-permute-start | bytes 761864 | tf_op jit(solution)/shard_map/send_2_0/ppermute | solution.py:280
  10.2 5.8 %collective-permute-start.1 = (f32[31,8,128]{2,1,0:T(8,128)S(1)}, f32[31,8,128]{2,1,0:T(8,128)S(1)}, u32[]{:S(2)}, u32[]{:S(2)}) collective-permute-start(f32[31,8,128]{2,1,0:T(8,128)S(1)} %get-tuple-element.21), channel_id=1, source_target_pairs={{0,2},{1,17},{2,0},{3,19},{4,6},{5,21},{6,4},{7,23},{8,10},{9,25},... | collective-permute-start | bytes 380936 | tf_op jit(solution)/shard_map/send_0_1/ppermute | solution.py:280
  12.2 5.8 %collective-permute-start.7 = (f32[31,8,128]{2,1,0:T(8,128)S(1)}, f32[31,8,128]{2,1,0:T(8,128)S(1)}, u32[]{:S(2)}, u32[]{:S(2)}) collective-permute-start(f32[31,8,128]{2,1,0:T(8,128)S(1)} %get-tuple-element.25), channel_id=1, source_target_pairs={{0,8},{1,17},{2,10},{3,19},{4,12},{5,21},{6,14},{7,23},{8,0},{9,25... | collective-permute-start | bytes 380936 | tf_op jit(solution)/shard_map/send_1_1/ppermute | solution.py:280
  15.1 5.5 %collective-permute-start.13 = (f32[31,8,128]{2,1,0:T(8,128)S(1)}, f32[31,8,128]{2,1,0:T(8,128)S(1)}, u32[]{:S(2)}, u32[]{:S(2)}) collective-permute-start(f32[31,8,128]{2,1,0:T(8,128)S(1)} %get-tuple-element.29), channel_id=1, source_target_pairs={{0,2},{1,17},{2,0},{3,19},{4,6},{5,21},{6,4},{7,23},{8,10},{9,25},... | collective-permute-start | bytes 380936 | tf_op jit(solution)/shard_map/send_2_1/ppermute | solution.py:280
  16.0 27.7 %copy-start = (f32[4096]{0:T(1024)S(1)}, f32[4096]{0:T(1024)}, u32[]{:S(2)}) copy-start(f32[4096]{0:T(1024)} %param.7) | copy-start | bytes 49156
  16.0 27.7 %copy-start.1 = (s32[128]{0:T(128)S(1)}, s32[128]{0:T(128)}, u32[]{:S(2)}) copy-start(s32[128]{0:T(128)} %day_in.3) | copy-start | bytes 1540
  16.0 6.9 %collective-permute-start.2 = (f32[31,8,128]{2,1,0:T(8,128)S(1)}, f32[31,8,128]{2,1,0:T(8,128)S(1)}, u32[]{:S(2)}, u32[]{:S(2)}) collective-permute-start(f32[31,8,128]{2,1,0:T(8,128)S(1)} %merge_0_1.1.own_ref), channel_id=1, source_target_pairs={{0,4},{1,9},{2,6},{3,11},{4,0},{5,13},{6,2},{7,15},{8,12},{9,1},{1... | collective-permute-start | bytes 380936 | tf_op jit(solution)/shard_map/send_0_2/ppermute | solution.py:280
  18.0 5.9 %collective-permute-start.8 = (f32[31,8,128]{2,1,0:T(8,128)S(1)}, f32[31,8,128]{2,1,0:T(8,128)S(1)}, u32[]{:S(2)}, u32[]{:S(2)}) collective-permute-start(f32[31,8,128]{2,1,0:T(8,128)S(1)} %merge_1_1.1.own_ref), channel_id=1, source_target_pairs={{0,16},{1,3},{2,18},{3,1},{4,20},{5,7},{6,22},{7,5},{8,24},{9,11},... | collective-permute-start | bytes 380936 | tf_op jit(solution)/shard_map/send_1_2/ppermute | solution.py:280
  20.6 6.2 %collective-permute-start.14 = (f32[31,8,128]{2,1,0:T(8,128)S(1)}, f32[31,8,128]{2,1,0:T(8,128)S(1)}, u32[]{:S(2)}, u32[]{:S(2)}) collective-permute-start(f32[31,8,128]{2,1,0:T(8,128)S(1)} %merge_2_1.1.own_ref), channel_id=1, source_target_pairs={{0,16},{1,9},{2,18},{3,11},{4,20},{5,13},{6,22},{7,15},{8,24},{9,1... | collective-permute-start | bytes 380936 | tf_op jit(solution)/shard_map/send_2_2/ppermute | solution.py:280
  22.9 8.2 %collective-permute-start.3 = (f32[31,8,128]{2,1,0:T(8,128)S(1)}, f32[31,8,128]{2,1,0:T(8,128)S(1)}, u32[]{:S(2)}, u32[]{:S(2)}) collective-permute-start(f32[31,8,128]{2,1,0:T(8,128)S(1)} %merge_0_2.1.own), channel_id=1, source_target_pairs={{0,16},{1,3},{2,18},{3,1},{4,20},{5,7},{6,22},{7,5},{8,24},{9,11},... | collective-permute-start | bytes 380936 | tf_op jit(solution)/shard_map/send_0_3/ppermute | solution.py:280
  23.9 7.4 %collective-permute-start.9 = (f32[31,8,128]{2,1,0:T(8,128)S(1)}, f32[31,8,128]{2,1,0:T(8,128)S(1)}, u32[]{:S(2)}, u32[]{:S(2)}) collective-permute-start(f32[31,8,128]{2,1,0:T(8,128)S(1)} %merge_1_2.1.own), channel_id=1, source_target_pairs={{0,4},{1,9},{2,6},{3,11},{4,0},{5,13},{6,2},{7,15},{8,12},{9,1},{1... | collective-permute-start | bytes 380936 | tf_op jit(solution)/shard_map/send_1_3/ppermute | solution.py:280
  26.8 6.6 %collective-permute-start.15 = (f32[31,8,128]{2,1,0:T(8,128)S(1)}, f32[31,8,128]{2,1,0:T(8,128)S(1)}, u32[]{:S(2)}, u32[]{:S(2)}) collective-permute-start(f32[31,8,128]{2,1,0:T(8,128)S(1)} %merge_2_2.1.own), channel_id=1, source_target_pairs={{0,4},{1,3},{2,6},{3,1},{4,0},{5,7},{6,2},{7,5},{8,12},{9,11},{10,... | collective-permute-start | bytes 380936 | tf_op jit(solution)/shard_map/send_2_3/ppermute | solution.py:280
  31.2 4.5 %collective-permute-start.4 = (f32[20,8,128]{2,1,0:T(8,128)S(1)}, f32[20,8,128]{2,1,0:T(8,128)S(1)}, u32[]{:S(2)}, u32[]{:S(2)}) collective-permute-start(f32[20,8,128]{2,1,0:T(8,128)S(1)} %merge_0_3.1.own_ref), channel_id=1, source_target_pairs={{0,2},{1,17},{2,0},{3,19},{4,6},{5,21},{6,4},{7,23},{8,10},{9,25},... | collective-permute-start | bytes 245768 | tf_op jit(solution)/shard_map/send_0_4/ppermute | solution.py:280
  31.4 4.8 %collective-permute-start.10 = (f32[20,8,128]{2,1,0:T(8,128)S(1)}, f32[20,8,128]{2,1,0:T(8,128)S(1)}, u32[]{:S(2)}, u32[]{:S(2)}) collective-permute-start(f32[20,8,128]{2,1,0:T(8,128)S(1)} %merge_1_3.1.own_ref), channel_id=1, source_target_pairs={{0,8},{1,17},{2,10},{3,19},{4,12},{5,21},{6,14},{7,23},{8,0},{9,25... | collective-permute-start | bytes 245768 | tf_op jit(solution)/shard_map/send_1_4/ppermute | solution.py:280
  33.5 4.7 %collective-permute-start.16 = (f32[20,8,128]{2,1,0:T(8,128)S(1)}, f32[20,8,128]{2,1,0:T(8,128)S(1)}, u32[]{:S(2)}, u32[]{:S(2)}) collective-permute-start(f32[20,8,128]{2,1,0:T(8,128)S(1)} %merge_2_3.1.own_ref), channel_id=1, source_target_pairs={{0,2},{1,17},{2,0},{3,19},{4,6},{5,21},{6,4},{7,23},{8,10},{9,25},... | collective-permute-start | bytes 245768 | tf_op jit(solution)/shard_map/send_2_4/ppermute | solution.py:280
  35.7 5.4 %collective-permute-start.5 = (f32[2,20,8,128]{3,2,1,0:T(8,128)S(1)}, f32[2,20,8,128]{3,2,1,0:T(8,128)S(1)}, u32[]{:S(2)}, u32[]{:S(2)}) collective-permute-start(f32[2,20,8,128]{3,2,1,0:T(8,128)S(1)} %merge_0_4.1.refs_1_), channel_id=1, source_target_pairs={{0,8},{1,5},{2,10},{3,7},{4,12},{5,1},{6,14},{7,3},{8,0},{9,13},{1... | collective-permute-start | bytes 491528 | tf_op jit(solution)/shard_map/send_0_5/ppermute | solution.py:280
  36.3 5.4 %collective-permute-start.11 = (f32[2,20,8,128]{3,2,1,0:T(8,128)S(1)}, f32[2,20,8,128]{3,2,1,0:T(8,128)S(1)}, u32[]{:S(2)}, u32[]{:S(2)}) collective-permute-start(f32[2,20,8,128]{3,2,1,0:T(8,128)S(1)} %merge_1_4.1.refs_3_), channel_id=1, source_target_pairs={{0,2},{1,5},{2,0},{3,7},{4,6},{5,1},{6,4},{7,3},{8,10},{9,13},{10,... | collective-permute-start | bytes 491528 | tf_op jit(solution)/shard_map/send_1_5/ppermute | solution.py:280
  38.3 5.4 %collective-permute-start.17 = (f32[2,20,8,128]{3,2,1,0:T(8,128)S(1)}, f32[2,20,8,128]{3,2,1,0:T(8,128)S(1)}, u32[]{:S(2)}, u32[]{:S(2)}) collective-permute-start(f32[2,20,8,128]{3,2,1,0:T(8,128)S(1)} %merge_2_4.1.refs_5_), channel_id=1, source_target_pairs={{0,8},{1,5},{2,10},{3,7},{4,12},{5,1},{6,14},{7,3},{8,0},{9,13},{1... | collective-permute-start | bytes 491528 | tf_op jit(solution)/shard_map/send_2_5/ppermute | solution.py:280
  45.5 1.2 %collective-permute-start.18 = (f32[8,128]{1,0:T(8,128)S(1)}, f32[8,128]{1,0:T(8,128)S(1)}, u32[]{:S(2)}, u32[]{:S(2)}) collective-permute-start(f32[8,128]{1,0:T(8,128)S(1)} %get-tuple-element.33), channel_id=1, source_target_pairs={{0,1},{1,0},{2,3},{3,2},{4,5},{5,4},{6,7},{7,6},{8,9},{9,8},{10,11... | collective-permute-start | bytes 12296 | tf_op jit(solution)/shard_map/ppermute | solution.py:319
